TPU v7x, 32 devices: a whole 2x2x4 slice. The times are simulated.
32 devices in a mesh: clips: 2 (over x), context: 4 (over y, core), tensor: 4 (over z).
Axes of the slice: x: 2, y: 2, z: 4, core: 2. Of those that a mesh axis runs over, the one named last changes fastest.
Arguments:
- inputs: bfloat16 [2, 2048, 1024], P('clips', 'context'), may hold values from -6 to 6
- gain_first: float32 [1024], replicated, may hold values from 0.5 to 1.5
- first_in: float32 [1024, 4096], P(('clips', 'context'), 'tensor'), may hold values from -0.1875 to 0.1875
- first_out: float32 [4096, 1024], P('tensor', ('clips', 'context')), may hold values from -0.09375 to 0.09375
- gain_attend: float32 [1024], replicated, may hold values from 0.5 to 1.5
- attend_in: float32 [3, 1024, 1024], P(None, ('clips', 'context'), 'tensor'), may hold values from -0.1875 to 0.1875
- attend_out: float32 [1024, 1024], P('tensor', ('clips', 'context')), may hold values from -2 to 2
- relative: float32 [73, 64], replicated, may hold values from -6 to 6
- gain_convolve: float32 [1024], replicated, may hold values from 0.5 to 1.5
- convolve_in: float32 [2, 1024, 1024], P(None, ('clips', 'context'), 'tensor'), may hold values from -0.1875 to 0.1875
- depthwise: float32 [31, 1024], P(None, 'tensor'), may hold values from -1 to 1
- gain_middle: float32 [1024], P('tensor'), may hold values from 0.5 to 1.5
- convolve_out: float32 [1024, 1024], P('tensor', ('clips', 'context')), may hold values from -0.1875 to 0.1875
- gain_second: float32 [1024], replicated, may hold values from 0.5 to 1.5
- second_in: float32 [1024, 4096], P(('clips', 'context'), 'tensor'), may hold values from -0.1875 to 0.1875
- second_out: float32 [4096, 1024], P('tensor', ('clips', 'context')), may hold values from -0.09375 to 0.09375
- gain_final: float32 [1024], replicated, may hold values from 0.5 to 1.5
- cotangent: bfloat16 [2, 2048, 1024], P('clips', 'context'), may hold values from -6 to 6
Outputs:
- layer_out: bfloat16 [2, 2048, 1024], P('clips', 'context')
- grad_inputs: float32 [2, 2048, 1024], P('clips', 'context')
- grad_gain_first: float32 [1024], replicated
- grad_first_in: float32 [1024, 4096], P(('clips', 'context'), 'tensor')
- grad_first_out: float32 [4096, 1024], P('tensor', ('clips', 'context'))
- grad_gain_attend: float32 [1024], replicated
- grad_attend_in: float32 [3, 1024, 1024], P(None, ('clips', 'context'), 'tensor')
- grad_attend_out: float32 [1024, 1024], P('tensor', ('clips', 'context'))
- grad_relative: float32 [73, 64], replicated
- grad_gain_convolve: float32 [1024], replicated
- grad_convolve_in: float32 [2, 1024, 1024], P(None, ('clips', 'context'), 'tensor')
- grad_depthwise: float32 [31, 1024], P(None, 'tensor')
- grad_gain_middle: float32 [1024], P('tensor')
- grad_convolve_out: float32 [1024, 1024], P('tensor', ('clips', 'context'))
- grad_gain_second: float32 [1024], replicated
- grad_second_in: float32 [1024, 4096], P(('clips', 'context'), 'tensor')
- grad_second_out: float32 [4096, 1024], P('tensor', ('clips', 'context'))
- grad_gain_final: float32 [1024], replicated
All inputs are finite; a program needn't handle non-finite values.
Results may differ from a plain program's by a relative error of at most 0.035.
Values may be sent and summed in bfloat16 or wider, within the bound.
A program may use at most 128 MiB of HBM per device.

v0:
```python
from functools import partial
import math

import jax
import jax.numpy as jnp
from jax import lax
from jax.sharding import PartitionSpec as P

D = 1024
HEAD_DIM = 64
LEFT = 64
RIGHT = 8


epsilon = 1e-05
highest = lax.Precision.HIGHEST


def shifted_2(value, axis, steps):
    count = lax.axis_size(axis)
    initial, last = (max(0, -steps), min(count, count - steps))
    return lax.ppermute(value, axis, [(source, source + steps) for source in range(initial, last)])


def dot_rows(former, latter):
    return jnp.dot(former, latter, preferred_element_type=jnp.float32)


def dot_inner(former, latter):
    return lax.dot_general(
        former, latter, (((0,), (0,)), ((), ())), preferred_element_type=jnp.float32
    )


def dot_outer(former, latter):
    return lax.dot_general(
        former, latter, (((1,), (1,)), ((), ())), preferred_element_type=jnp.float32
    )


def layer_norm(rows_in, gain_vec):
    row_mean = jnp.mean(rows_in, axis=-1, keepdims=True)
    centred = rows_in - row_mean
    variance = jnp.mean(centred * centred, axis=-1, keepdims=True)
    return centred * lax.rsqrt(variance + epsilon) * gain_vec


def norm_back(rows_in, gain_vec, upstream):
    unused, pullback = jax.vjp(layer_norm, rows_in, gain_vec)
    return pullback(upstream)


def gate_unit(unit_half, gate_half):
    return unit_half * jax.nn.sigmoid(gate_half)


def fetch(weight_in, weight_out):
    return (
        lax.all_gather(weight_in.astype(jnp.bfloat16), ("clips", "context"), axis=1, tiled=True),
        lax.all_gather(weight_out.astype(jnp.bfloat16), ("clips", "context"), axis=1, tiled=True),
    )


def weights_back(weight_in, weight_out):
    result_pair = (
        lax.all_gather(weight_in.astype(jnp.bfloat16), ("clips", "context"), axis=1, tiled=True),
        lax.all_gather(weight_out.astype(jnp.bfloat16), ("clips", "context"), axis=1, tiled=True),
    )
    return result_pair


def send_grads(grad_in, grad_out):
    return (
        lax.psum_scatter(grad_in, ("clips", "context"), scatter_dimension=1, tiled=True),
        lax.psum_scatter(grad_out, ("clips", "context"), scatter_dimension=1, tiled=True),
    )


def branch_total(partial_sum):
    return lax.psum(partial_sum.astype(jnp.bfloat16), "tensor").astype(jnp.float32)


def input_total(partial_sum):
    return lax.psum(partial_sum.astype(jnp.bfloat16), "tensor").astype(jnp.float32)


def ffn_forward(rows_in, gain_vec, weight_in, weight_out):
    normed = layer_norm(rows_in, gain_vec).astype(jnp.bfloat16)
    hidden = dot_rows(normed, weight_in)
    active = jax.nn.silu(hidden).astype(jnp.bfloat16)
    return (branch_total(dot_rows(active, weight_out)), (normed, hidden, active))


def ffn_backward(rows_in, gain_vec, weight_in, weight_out, saved, upstream):
    normed, hidden, active = saved
    branch_grad = (0.5 * upstream).astype(jnp.bfloat16)
    grad_out = dot_inner(active, branch_grad)
    unused, pullback = jax.vjp(jax.nn.silu, hidden)
    hidden_grad = pullback(dot_outer(branch_grad, weight_out))[0].astype(jnp.bfloat16)
    grad_in = dot_inner(normed, hidden_grad)
    normed_grad = input_total(dot_outer(hidden_grad, weight_in))
    rows_grad, gain_grad = norm_back(rows_in, gain_vec, normed_grad)
    return (upstream + rows_grad, gain_grad, grad_in, grad_out)


def skew_band(band_rows, first_row, key_count):
    query_count, band_width = band_rows.shape
    width = key_count + LEFT + band_width
    widened = jnp.pad(band_rows, ((0, 0), (0, width + 1 - band_width)))
    shifted = widened.reshape(-1)[: query_count * width].reshape(query_count, width)
    extended = jnp.concatenate([jnp.zeros((query_count, key_count), jnp.float32), shifted], axis=1)
    return lax.dynamic_slice_in_dim(extended, key_count - first_row + LEFT, key_count, 1)


def unskew_band(grad_tile, first_row, band_width):
    query_count, key_count = grad_tile.shape
    width = key_count + LEFT + band_width
    extended = jnp.zeros((query_count, key_count + width), jnp.float32)
    extended = lax.dynamic_update_slice_in_dim(extended, grad_tile, key_count - first_row + LEFT, 1)
    flat = extended[:, key_count:].reshape(-1)
    flat = jnp.concatenate([flat, jnp.zeros((query_count,), jnp.float32)])
    return flat.reshape(query_count, width + 1)[:, :band_width]


def head_scores(query_h, key_h, rel_table, position):
    query_count = query_h.shape[0]
    key_count = key_h.shape[0]
    content = dot_outer(query_h, key_h)
    rel_scores = dot_outer(query_h, rel_table)
    first_row = position * query_count
    query_rows = first_row + jnp.arange(query_count, dtype=jnp.int32)
    key_cols = jnp.arange(key_count, dtype=jnp.int32)
    offsets = key_cols[None, :] - query_rows[:, None]
    banded = skew_band(rel_scores, first_row, key_count)
    rel_bias = jnp.where(
        offsets < -LEFT, rel_scores[:, :1], jnp.where(offsets > RIGHT, rel_scores[:, -1:], banded)
    )
    return ((content + rel_bias) * (1.0 / math.sqrt(HEAD_DIM)), offsets, first_row)


def head_forward(head, queries, key_rows, value_rows, rel_table, position):
    start_col = head * HEAD_DIM
    query_h = lax.dynamic_slice_in_dim(queries, start_col, HEAD_DIM, 1)
    key_h = lax.dynamic_slice_in_dim(key_rows, start_col, HEAD_DIM, 1)
    value_h = lax.dynamic_slice_in_dim(value_rows, start_col, HEAD_DIM, 1)
    logits, offsets, first_row = head_scores(query_h, key_h, rel_table, position)
    row_max = jnp.max(logits, axis=1, keepdims=True)
    log_total = row_max + jnp.log(jnp.sum(jnp.exp(logits - row_max), axis=1, keepdims=True))
    attend_prob = jnp.exp(logits - log_total).astype(jnp.bfloat16)
    return (dot_rows(attend_prob, value_h), log_total)


def head_backward(head, queries, key_rows, value_rows, mixed_grad, log_total, rel_table, position):
    score_scale = 1.0 / math.sqrt(HEAD_DIM)
    start_col = head * HEAD_DIM
    query_h = lax.dynamic_slice_in_dim(queries, start_col, HEAD_DIM, 1)
    key_h = lax.dynamic_slice_in_dim(key_rows, start_col, HEAD_DIM, 1)
    value_h = lax.dynamic_slice_in_dim(value_rows, start_col, HEAD_DIM, 1)
    grad_h = lax.dynamic_slice_in_dim(mixed_grad, start_col, HEAD_DIM, 1)
    logits, offsets, first_row = head_scores(query_h, key_h, rel_table, position)
    attend_prob = jnp.exp(logits - log_total[head])
    value_grad = dot_inner(attend_prob.astype(jnp.bfloat16), grad_h)
    prob_grad = dot_outer(grad_h, value_h)
    logit_grad = attend_prob * (prob_grad - jnp.sum(attend_prob * prob_grad, axis=1, keepdims=True))
    logit_grad = logit_grad.astype(jnp.bfloat16)
    query_grad = score_scale * dot_rows(logit_grad, key_h)
    key_grad = score_scale * dot_inner(logit_grad, query_h)
    wide_grad = logit_grad.astype(jnp.float32)
    inside = (offsets >= -LEFT) & (offsets <= RIGHT)
    bin_grad = unskew_band(jnp.where(inside, wide_grad, 0.0), first_row, rel_table.shape[0])
    below = jnp.sum(jnp.where(offsets < -LEFT, wide_grad, 0.0), axis=1)
    above = jnp.sum(jnp.where(offsets > RIGHT, wide_grad, 0.0), axis=1)
    bin_grad = bin_grad.at[:, 0].add(below)
    bin_grad = bin_grad.at[:, -1].add(above)
    bin_grad = score_scale * bin_grad
    query_grad = query_grad + jnp.dot(bin_grad, rel_table.astype(jnp.float32), precision=highest)
    table_grad = lax.dot_general(
        bin_grad, query_h.astype(jnp.float32), (((0,), (0,)), ((), ())), precision=highest
    )
    return (query_grad, key_grad, value_grad, table_grad)


def attend_forward(rows_in, gain_vec, weight_in, weight_out, relative, position):
    rows_here = rows_in.shape[0]
    local_width = weight_in.shape[2]
    local_heads = local_width // HEAD_DIM
    normed = layer_norm(rows_in, gain_vec).astype(jnp.bfloat16)
    projected = jnp.einsum(
        "td,kde->kte", normed, weight_in, preferred_element_type=jnp.float32
    ).astype(jnp.bfloat16)
    key_rows, value_rows = (
        lax.all_gather(projected[1], "context", axis=0, tiled=True),
        lax.all_gather(projected[2], "context", axis=0, tiled=True),
    )
    per_head = partial(
        head_forward,
        queries=projected[0],
        key_rows=key_rows,
        value_rows=value_rows,
        rel_table=relative.astype(jnp.bfloat16),
        position=position,
    )
    head_outs, log_total = lax.map(per_head, jnp.arange(local_heads, dtype=jnp.int32))
    mixed = jnp.transpose(head_outs, (1, 0, 2)).reshape(rows_here, local_width).astype(jnp.bfloat16)
    return (
        branch_total(dot_rows(mixed, weight_out)),
        (normed, projected, key_rows, value_rows, log_total, mixed),
    )


def attend_backward(weight_in, weight_out, relative, position, saved, upstream):
    normed, projected, key_rows, value_rows, log_total, mixed = saved
    rows_here, local_width = mixed.shape
    local_heads = local_width // HEAD_DIM
    branch_grad = upstream.astype(jnp.bfloat16)
    grad_out = dot_inner(mixed, branch_grad)
    mixed_grad = dot_outer(branch_grad, weight_out).astype(jnp.bfloat16)
    per_head = partial(
        head_backward,
        queries=projected[0],
        key_rows=key_rows,
        value_rows=value_rows,
        mixed_grad=mixed_grad,
        log_total=log_total,
        rel_table=relative.astype(jnp.bfloat16),
        position=position,
    )
    query_grad, key_grad, value_grad, table_grad = lax.map(
        per_head, jnp.arange(local_heads, dtype=jnp.int32)
    )
    key_grad, value_grad = (
        lax.psum_scatter(
            key_grad.astype(jnp.bfloat16), "context", scatter_dimension=1, tiled=True
        ).astype(jnp.float32),
        lax.psum_scatter(
            value_grad.astype(jnp.bfloat16), "context", scatter_dimension=1, tiled=True
        ).astype(jnp.float32),
    )
    stacked = jnp.stack([query_grad, key_grad, value_grad])
    stacked = (
        jnp.transpose(stacked, (0, 2, 1, 3)).reshape(3, rows_here, local_width).astype(jnp.bfloat16)
    )
    grad_in = jnp.einsum("td,kte->kde", normed, stacked, preferred_element_type=jnp.float32)
    partial_sum = jnp.einsum("kte,kde->td", stacked, weight_in, preferred_element_type=jnp.float32)
    return (partial_sum, jnp.sum(table_grad, axis=0), grad_in, grad_out)


def conv_forward(rows_in, gain_vec, weight_in, weight_out, depthwise, gain_middle):
    normed = layer_norm(rows_in, gain_vec).astype(jnp.bfloat16)
    projected = jnp.einsum("td,kde->kte", normed, weight_in, preferred_element_type=jnp.float32)
    gated = gate_unit(projected[0], projected[1])
    rows_here = gated.shape[0]
    reach_rows = depthwise.shape[0] - 1
    edge_rows = shifted_2(gated[rows_here - reach_rows :], "context", 1)
    padded = jnp.concatenate([edge_rows, gated], axis=0)
    mixed = depthwise[0] * padded[0:rows_here]
    for offset in range(1, reach_rows + 1):
        mixed = mixed + depthwise[offset] * padded[offset : offset + rows_here]
    row_sums, row_squares = lax.psum(
        (jnp.sum(mixed, axis=1), jnp.sum(mixed * mixed, axis=1)), "tensor"
    )
    row_mean = row_sums / D
    inverse = lax.rsqrt(row_squares / D - row_mean * row_mean + epsilon)
    scaled = (mixed - row_mean[:, None]) * inverse[:, None]
    shaped = scaled * gain_middle
    active = jax.nn.silu(shaped).astype(jnp.bfloat16)
    return (
        branch_total(dot_rows(active, weight_out)),
        (normed, projected, padded, scaled, inverse, shaped, active),
    )


def conv_backward(weight_in, weight_out, depthwise, gain_middle, saved, upstream):
    normed, projected, padded, scaled, inverse, shaped, active = saved
    rows_here, channels = scaled.shape
    reach_rows = depthwise.shape[0] - 1
    branch_grad = upstream.astype(jnp.bfloat16)
    grad_out = dot_inner(active, branch_grad)
    unused, pullback = jax.vjp(jax.nn.silu, shaped)
    shaped_grad = pullback(dot_outer(branch_grad, weight_out))[0]
    middle_grad = jnp.sum(shaped_grad * scaled, axis=0)
    scaled_grad = shaped_grad * gain_middle
    first_sum, second_sum = lax.psum(
        (jnp.sum(scaled_grad, axis=1), jnp.sum(scaled_grad * scaled, axis=1)), "tensor"
    )
    mixed_grad = inverse[:, None] * (
        scaled_grad - first_sum[:, None] / D - scaled * (second_sum[:, None] / D)
    )
    padded_grad = jnp.zeros((rows_here + reach_rows, channels), jnp.float32)
    for offset in range(reach_rows + 1):
        padded_grad = padded_grad.at[offset : offset + rows_here].add(
            depthwise[offset] * mixed_grad
        )
    depth_grad = jnp.stack(
        [
            jnp.sum(padded[offset : offset + rows_here] * mixed_grad, axis=0)
            for offset in range(reach_rows + 1)
        ]
    )
    back_rows = shifted_2(padded_grad[:reach_rows], "context", -1)
    gated_grad = padded_grad[reach_rows:] + jnp.pad(
        back_rows, ((rows_here - reach_rows, 0), (0, 0))
    )
    unused, pullback = jax.vjp(gate_unit, projected[0], projected[1])
    unit_grad, gate_grad = pullback(gated_grad)
    stacked = jnp.stack([unit_grad, gate_grad]).astype(jnp.bfloat16)
    grad_in = jnp.einsum("td,kte->kde", normed, stacked, preferred_element_type=jnp.float32)
    partial_sum = jnp.einsum("kte,kde->td", stacked, weight_in, preferred_element_type=jnp.float32)
    return (partial_sum, grad_in, grad_out, middle_grad, depth_grad)


def local(
    inputs,
    gain_first,
    first_in,
    first_out,
    gain_attend,
    attend_in,
    attend_out,
    relative,
    gain_convolve,
    convolve_in,
    depthwise,
    gain_middle,
    convolve_out,
    gain_second,
    second_in,
    second_out,
    gain_final,
    cotangent,
):
    position = lax.axis_index("context")
    start_rows = inputs[0].astype(jnp.float32)
    first_pair = fetch(first_in[None], first_out)
    branch_out, first_saved = ffn_forward(start_rows, gain_first, first_pair[0][0], first_pair[1])
    after_first = start_rows + 0.5 * branch_out
    attend_pair = fetch(attend_in, attend_out)
    branch_out, attend_saved = attend_forward(
        after_first, gain_attend, attend_pair[0], attend_pair[1], relative, position
    )
    after_attend = after_first + branch_out
    convolve_pair = fetch(convolve_in, convolve_out)
    branch_out, convolve_saved = conv_forward(
        after_attend, gain_convolve, convolve_pair[0], convolve_pair[1], depthwise, gain_middle
    )
    after_convolve = after_attend + branch_out
    second_pair = fetch(second_in[None], second_out)
    branch_out, second_saved = ffn_forward(
        after_convolve, gain_second, second_pair[0][0], second_pair[1]
    )
    after_second = after_convolve + 0.5 * branch_out
    final_out, pullback = jax.vjp(layer_norm, after_second, gain_final)
    upstream, grad_final = pullback(cotangent[0].astype(jnp.float32))
    second_pair = weights_back(second_in[None], second_out)
    upstream, grad_gain_second, grad_in, grad_out = ffn_backward(
        after_convolve, gain_second, second_pair[0][0], second_pair[1], second_saved, upstream
    )
    second_grads = send_grads(grad_in[None], grad_out)
    convolve_pair = weights_back(convolve_in, convolve_out)
    partial_sum, grad_in, grad_out, grad_middle, grad_depth = conv_backward(
        convolve_pair[0], convolve_pair[1], depthwise, gain_middle, convolve_saved, upstream
    )
    rows_grad, grad_gain_convolve = norm_back(after_attend, gain_convolve, input_total(partial_sum))
    upstream = upstream + rows_grad
    convolve_grads = send_grads(grad_in, grad_out)
    attend_pair = weights_back(attend_in, attend_out)
    partial_sum, table_grad, grad_in, grad_out = attend_backward(
        attend_pair[0], attend_pair[1], relative, position, attend_saved, upstream
    )
    normed_grad, table_grad = (
        lax.psum(partial_sum.astype(jnp.bfloat16), "tensor").astype(jnp.float32),
        lax.psum(table_grad.astype(jnp.bfloat16), "tensor").astype(jnp.float32),
    )
    rows_grad, grad_gain_attend = norm_back(after_first, gain_attend, normed_grad)
    upstream = upstream + rows_grad
    attend_grads = send_grads(grad_in, grad_out)
    first_pair = weights_back(first_in[None], first_out)
    upstream, grad_gain_first, grad_in, grad_out = ffn_backward(
        start_rows, gain_first, first_pair[0][0], first_pair[1], first_saved, upstream
    )
    first_grads = send_grads(grad_in[None], grad_out)
    smalls = lax.psum(
        (
            grad_gain_first,
            grad_gain_attend,
            table_grad,
            grad_gain_convolve,
            grad_depth,
            grad_middle,
            grad_gain_second,
            grad_final,
        ),
        ("clips", "context"),
    )
    return (
        final_out.astype(jnp.bfloat16)[None],
        upstream[None],
        smalls[0],
        first_grads[0][0],
        first_grads[1],
        smalls[1],
        attend_grads[0],
        attend_grads[1],
        smalls[2],
        smalls[3],
        convolve_grads[0],
        smalls[4],
        smalls[5],
        convolve_grads[1],
        smalls[6],
        second_grads[0][0],
        second_grads[1],
        smalls[7],
    )


def solution(mesh):
    placed = (
        P("clips", "context", None),
        P(),
        P(("clips", "context"), "tensor"),
        P("tensor", ("clips", "context")),
        P(),
        P(None, ("clips", "context"), "tensor"),
        P("tensor", ("clips", "context")),
        P(),
        P(),
        P(None, ("clips", "context"), "tensor"),
        P(None, "tensor"),
        P("tensor"),
        P("tensor", ("clips", "context")),
        P(),
        P(("clips", "context"), "tensor"),
        P("tensor", ("clips", "context")),
        P(),
        P("clips", "context", None),
    )
    return jax.shard_map(
        local,
        mesh=mesh,
        in_specs=placed,
        out_specs=(
            P("clips", "context", None),
            P("clips", "context", None),
            P(),
            P(("clips", "context"), "tensor"),
            P("tensor", ("clips", "context")),
            P(),
            P(None, ("clips", "context"), "tensor"),
            P("tensor", ("clips", "context")),
            P(),
            P(),
            P(None, ("clips", "context"), "tensor"),
            P(None, "tensor"),
            P("tensor"),
            P("tensor", ("clips", "context")),
            P(),
            P(("clips", "context"), "tensor"),
            P("tensor", ("clips", "context")),
            P(),
        ),
        check_vma=False,
    )
```

profile of v0, /device:TPU:0, one launch (start us, length us, event | category | flops | bytes accessed | tf_op | source)
XLA Modules:
  0.0 1796.6 jit_solution(3377429776977933191)
XLA Ops:
  12.2 28.8 %all-gather.21.cloned.1.call-done = bf16[1024,1024]{1,0:T(8,128)(2,1)} async-done(((bf16[128,1024]{1,0:T(8,128)(2,1)}), bf16[1024,1024]{1,0:T(8,128)(2,1)}) %all-gather.21.cloned.1.call-update) | async-done | bytes 2097168 | tf_op jit(solution)/shard_map/all_gather | solution.py:59
  43.9 27.7 %all-gather.13.cloned.1.call-done = bf16[1024,1024]{1,0:T(8,128)(2,1)} async-done(((bf16[1024,128]{1,0:T(8,128)(2,1)}), bf16[1024,1024]{1,0:T(8,128)(2,1)}) %all-gather.13.cloned.1.call-update) | async-done | bytes 2097168 | tf_op jit(solution)/shard_map/all_gather | solution.py:60
  76.3 51.2 %all-reduce.20.cloned.1.call-done = bf16[512,1024]{1,0:T(8,128)(2,1)} async-done(((bf16[512,1024]{1,0:T(8,128)(2,1)}), bf16[512,1024]{1,0:T(8,128)(2,1)}) %all-reduce.20.cloned.1.call-update) | async-done | bytes 1048592 | tf_op jit(solution)/shard_map/psum | solution.py:80
  130.4 24.4 %all-gather.15.cloned.1.call-done = bf16[3,1024,256]{2,1,0:T(8,128)(2,1)} async-done(((bf16[3,128,256]{2,1,0:T(8,128)(2,1)}), bf16[3,1024,256]{2,1,0:T(8,128)(2,1)}) %all-gather.15.cloned.1.call-update) | async-done | bytes 1572880 | tf_op jit(solution)/shard_map/all_gather | solution.py:59
  159.1 10.2 all_gather.43
  169.3 6.0 all-gather.25.cloned.1.call-done
  175.3 18.7 %all-gather.23.cloned.1.call-done = bf16[1,2048,256]{2,1,0:T(8,128)(2,1)} async-done(((bf16[1,512,256]{2,1,0:T(8,128)(2,1)}), bf16[1,2048,256]{2,1,0:T(8,128)(2,1)}) %all-gather.23.cloned.1.call-update) | async-done | bytes 1048592 | tf_op jit(solution)/shard_map/all_gather | solution.py:192
  194.0 109.4 %while.67 = (s32[]{:T(128)}, bf16[4,512,64]{1,2,0:T(8,128)(2,1)S(1)}, f32[4,512,1]{1,2,0:T(1,128)S(1)}, s32[4]{0:T(128)S(1)}, bf16[512,256]{1,0:T(8,128)(2,1)S(1...) while((s32[]{:T(128)}, ...), condition=%wide.region_8.9_spmd, body=%wide.region_5.8_spmd.sunk | while | flops 285802496 | bytes 41778916 | solution.py:203
  198.1 7.9 reshape.1104
  206.0 8.1 reshape.1105
  225.5 7.9 reshape.1104
  233.3 8.1 reshape.1105
  252.8 7.9 reshape.1104
  260.7 8.1 reshape.1105
  280.1 7.9 reshape.1104
  288.0 8.1 reshape.1105
  307.8 49.1 %all-reduce.22.cloned.1.call-done = bf16[512,1024]{1,0:T(8,128)(2,1)} async-done(((bf16[512,1024]{1,0:T(8,128)(2,1)}), bf16[512,1024]{1,0:T(8,128)(2,1)}) %all-reduce.22.cloned.1.call-update) | async-done | bytes 1048592 | tf_op jit(solution)/shard_map/psum | solution.py:80
  359.5 22.6 %all-gather.17.cloned.1.call-done = bf16[2,1024,256]{2,1,0:T(8,128)(2,1)} async-done(((bf16[2,128,256]{2,1,0:T(8,128)(2,1)}), bf16[2,1024,256]{2,1,0:T(8,128)(2,1)}) %all-gather.17.cloned.1.call-update) | async-done | bytes 1048592 | tf_op jit(solution)/shard_map/all_gather | solution.py:59
  386.7 11.1 all_gather.45
  400.4 11.7 all-reduce.9
  418.5 45.5 %all-reduce.24.cloned.1.call-done = bf16[512,1024]{1,0:T(8,128)(2,1)} async-done(((bf16[512,1024]{1,0:T(8,128)(2,1)}), bf16[512,1024]{1,0:T(8,128)(2,1)}) %all-reduce.24.cloned.1.call-update) | async-done | bytes 1048592 | tf_op jit(solution)/shard_map/psum | solution.py:80
  467.2 26.2 %all-gather.27.cloned.1.call-done = bf16[1024,1024]{1,0:T(8,128)(2,1)} async-done(((bf16[128,1024]{1,0:T(8,128)(2,1)}), bf16[1024,1024]{1,0:T(8,128)(2,1)}) %all-gather.27.cloned.1.call-update) | async-done | bytes 2097168 | tf_op jit(solution)/shard_map/all_gather | solution.py:59
  498.3 25.7 %all-gather.19.cloned.1.call-done = bf16[1024,1024]{1,0:T(8,128)(2,1)} async-done(((bf16[1024,128]{1,0:T(8,128)(2,1)}), bf16[1024,1024]{1,0:T(8,128)(2,1)}) %all-gather.19.cloned.1.call-update) | async-done | bytes 2097168 | tf_op jit(solution)/shard_map/all_gather | solution.py:60
  528.9 51.6 %all-reduce.26.cloned.1.call-done = bf16[512,1024]{1,0:T(8,128)(2,1)} async-done(((bf16[512,1024]{1,0:T(8,128)(2,1)}), bf16[512,1024]{1,0:T(8,128)(2,1)}) %all-reduce.26.cloned.1.call-update) | async-done | bytes 1048592 | tf_op jit(solution)/shard_map/psum | solution.py:80
  593.0 51.2 %all-reduce.28.cloned.1.call-done = bf16[512,1024]{1,0:T(8,128)(2,1)} async-done(((bf16[512,1024]{1,0:T(8,128)(2,1)}), bf16[512,1024]{1,0:T(8,128)(2,1)}) %all-reduce.28.cloned.1.call-update) | async-done | bytes 1048592 | tf_op jit(solution)/shard_map/psum | solution.py:84
  651.8 10.3 all-reduce.8
  774.5 50.1 %all-reduce.30.cloned.1.call-done = bf16[512,1024]{1,0:T(8,128)(2,1)} async-done(((bf16[512,1024]{1,0:T(8,128)(2,1)}), bf16[512,1024]{1,0:T(8,128)(2,1)}) %all-reduce.30.cloned.1.call-update) | async-done | bytes 1048592 | tf_op jit(solution)/shard_map/psum | solution.py:84
  831.4 403.6 %while.68 = (s32[]{:T(128)}, bf16[4,512,64]{1,2,0:T(8,128)(2,1)}, bf16[4,2048,64]{1,2,0:T(8,128)(2,1)}, bf16[4,2048,64]{1,2,0:T(8,128)(2,1)}, f32[4,73,64]{1,2,0...) while((s32[]{:T(128)}, bf16[4,512,64]{1,2,0:T(8,128)(2,1)}, ...), condition=%wide.region_40.41_spmd, body=%wide.region_35.40_spmd.sunk | while | flops 762914816 | bytes 148115488 | solution.py:228
  842.4 7.9 reshape.1106
  850.3 8.1 reshape.1107
  858.5 5.7 multiply_reduce_fusion.41
  876.4 22.0 %dynamic_update_slice.75 = f32[512,4233]{1,0:T(8,128)} dynamic-update-slice(f32[512,4233]{1,0:T(8,128)} %broadcast.927, f32[512,2048]{1,0:T(8,128)} %convert_select_fusion.4, s32[]{:T(128)} %constant.1133.clone.1..sunk.1, s32[]{:T(128)} %get-tuple-element.1302) | dynamic-update-slice | bytes 8388612 | tf_op jit(solution)/shard_map/while/body/eval_jaxpr/dynamic_update_slice | solution.py:119
  903.3 7.4 reshape.1108
  914.7 8.5 reshape.1109
  943.2 7.9 reshape.1106
  951.1 8.1 reshape.1107
  959.2 5.7 multiply_reduce_fusion.41
  977.2 22.0 %dynamic_update_slice.75 = f32[512,4233]{1,0:T(8,128)} dynamic-update-slice(f32[512,4233]{1,0:T(8,128)} %broadcast.927, f32[512,2048]{1,0:T(8,128)} %convert_select_fusion.4, s32[]{:T(128)} %constant.1133.clone.1..sunk.1, s32[]{:T(128)} %get-tuple-element.1302) | dynamic-update-slice | bytes 8388612 | tf_op jit(solution)/shard_map/while/body/eval_jaxpr/dynamic_update_slice | solution.py:119
  1004.1 7.4 reshape.1108
  1015.5 8.5 reshape.1109
  1044.0 7.9 reshape.1106
  1051.9 8.1 reshape.1107
  1060.0 5.7 multiply_reduce_fusion.41
  1078.0 22.0 %dynamic_update_slice.75 = f32[512,4233]{1,0:T(8,128)} dynamic-update-slice(f32[512,4233]{1,0:T(8,128)} %broadcast.927, f32[512,2048]{1,0:T(8,128)} %convert_select_fusion.4, s32[]{:T(128)} %constant.1133.clone.1..sunk.1, s32[]{:T(128)} %get-tuple-element.1302) | dynamic-update-slice | bytes 8388612 | tf_op jit(solution)/shard_map/while/body/eval_jaxpr/dynamic_update_slice | solution.py:119
  1104.8 7.4 reshape.1108
  1116.3 8.5 reshape.1109
  1144.7 7.9 reshape.1106
  1152.6 8.1 reshape.1107
  1178.7 22.0 %dynamic_update_slice.75 = f32[512,4233]{1,0:T(8,128)} dynamic-update-slice(f32[512,4233]{1,0:T(8,128)} %broadcast.927, f32[512,2048]{1,0:T(8,128)} %convert_select_fusion.4, s32[]{:T(128)} %constant.1133.clone.1..sunk.1, s32[]{:T(128)} %get-tuple-element.1302) | dynamic-update-slice | bytes 8388612 | tf_op jit(solution)/shard_map/while/body/eval_jaxpr/dynamic_update_slice | solution.py:119
  1205.6 7.4 reshape.1108
  1217.0 8.5 reshape.1109
  1235.7 23.8 %reduce-scatter.11.cloned.1.call-done = bf16[4,512,64]{1,2,0:T(8,128)(2,1)} async-done(((bf16[4,2048,64]{1,2,0:T(8,128)(2,1)}), bf16[4,512,64]{1,2,0:T(8,128)(2,1)}) %reduce-scatter.11.cloned.1.call-update) | async-done | bytes 262160 | tf_op jit(solution)/shard_map/reduce_scatter | solution.py:232
  1259.5 27.2 %reduce-scatter.13.cloned.1.call-done = bf16[4,512,64]{1,2,0:T(8,128)(2,1)} async-done(((bf16[4,2048,64]{1,2,0:T(8,128)(2,1)}), bf16[4,512,64]{1,2,0:T(8,128)(2,1)}) %reduce-scatter.13.cloned.1.call-update) | async-done | bytes 262160 | tf_op jit(solution)/shard_map/reduce_scatter | solution.py:235
  1294.0 49.6 %all-reduce.32.cloned.1.call-done = bf16[512,1024]{1,0:T(8,128)(2,1)} async-done(((bf16[512,1024]{1,0:T(8,128)(2,1)}), bf16[512,1024]{1,0:T(8,128)(2,1)}) %all-reduce.32.cloned.1.call-update) | async-done | bytes 1048592 | tf_op jit(solution)/shard_map/psum | solution.py:371
  1389.9 17.5 psum.161
  1409.2 32.5 %all-reduce.34.cloned.1.call-done = bf16[512,1024]{1,0:T(8,128)(2,1)} async-done(((bf16[512,1024]{1,0:T(8,128)(2,1)}), bf16[512,1024]{1,0:T(8,128)(2,1)}) %all-reduce.34.cloned.1.call-update) | async-done | bytes 1048592 | tf_op jit(solution)/shard_map/psum | solution.py:84
  1444.8 25.8 %all-reduce.35 = (f32[1024]{0:T(1024)}, f32[1024]{0:T(1024)}, f32[73,64]{0,1:T(8,128)}, f32[1024]{0:T(1024)}, f32[31,256]{1,0:T(8,128)}, /*index=5*/f32[256]{0:T(256)}, f32[1024]{0:T(1024)}, f32[1024]{0:T(1024)}) all-reduce(f32[1024]{0:T(1024)S(1)} %get-tuple-element.866, ...), channel_id=1, replica_groups=mesh['clips'=2,'context'=4,'tensor'=4] {'clips','context'}, use_global_device_ids=true, to_apply=%region_50.51 | all-reduce | flops 17984 | bytes 134528 | tf_op jit(solution)/shard_map/psum | solution.py:382
  1474.3 16.0 reduce-scatter.19.cloned.1.call-done
  1492.2 37.9 %reduce-scatter.25.cloned.1.call-done = f32[256,128]{1,0:T(8,128)} async-done(((f32[256,1024]{1,0:T(8,128)}), f32[256,128]{1,0:T(8,128)}) %reduce-scatter.25.cloned.1.call-update) | async-done | bytes 131088 | tf_op jit(solution)/shard_map/reduce_scatter | solution.py:75
  1530.1 39.7 %reduce-scatter.21.cloned.1.call-done = f32[256,128]{1,0:T(8,128)} async-done(((f32[256,1024]{1,0:T(8,128)}), f32[256,128]{1,0:T(8,128)}) %reduce-scatter.21.cloned.1.call-update) | async-done | bytes 131088 | tf_op jit(solution)/shard_map/reduce_scatter | solution.py:75
  1569.8 55.0 %reduce-scatter.29.cloned.1.call-done = f32[1024,128]{1,0:T(8,128)} async-done(((f32[1024,1024]{1,0:T(8,128)}), f32[1024,128]{1,0:T(8,128)}) %reduce-scatter.29.cloned.1.call-update) | async-done | bytes 524304 | tf_op jit(solution)/shard_map/reduce_scatter | solution.py:75
  1624.8 55.0 %reduce-scatter.27.cloned.1.call-done = f32[1,128,1024]{2,1,0:T(8,128)} async-done(((f32[1,1024,1024]{2,1,0:T(8,128)}), f32[1,128,1024]{2,1,0:T(8,128)}) %reduce-scatter.27.cloned.1.call-update) | async-done | bytes 524304 | tf_op jit(solution)/shard_map/reduce_scatter | solution.py:74
  1679.8 55.0 %reduce-scatter.17.cloned.1.call-done = f32[1024,128]{1,0:T(8,128)} async-done(((f32[1024,1024]{1,0:T(8,128)}), f32[1024,128]{1,0:T(8,128)}) %reduce-scatter.17.cloned.1.call-update) | async-done | bytes 524304 | tf_op jit(solution)/shard_map/reduce_scatter | solution.py:75
  1734.8 55.0 %reduce-scatter.15.cloned.1.call-done = f32[1,128,1024]{2,1,0:T(8,128)} async-done(((f32[1,1024,1024]{2,1,0:T(8,128)}), f32[1,128,1024]{2,1,0:T(8,128)}) %reduce-scatter.15.cloned.1.call-update) | async-done | bytes 524304 | tf_op jit(solution)/shard_map/reduce_scatter | solution.py:74
  (685 shorter events, 456.8 us)
Async XLA Ops:
  7.2 33.8 %copy-start.62 = (f32[1024]{0:T(1024)S(1)}, f32[1024]{0:T(1024)}, u32[]{:S(2)}) copy-start(f32[1024]{0:T(1024)} %param.89) | copy-start | bytes 12292
  7.2 33.8 %all-gather.21.cloned.1.call-start = ((), (), s32[]{:S(2)}) async-start(), calls=%async_computation.32 | async-start | bytes 2359296 | tf_op jit(solution)/shard_map/all_gather | solution.py:59
  9.1 62.5 %all-gather.13.cloned.1.call-start = ((), (), s32[]{:S(2)}) async-start(), calls=%async_computation.10 | async-start | bytes 2359296 | tf_op jit(solution)/shard_map/all_gather | solution.py:60
  11.0 116.5 %all-reduce.20.cloned.1.call-start = ((), (), s32[]{:S(2)}) async-start(), calls=%async_computation.11 | async-start | bytes 2097152 | tf_op jit(solution)/shard_map/psum | solution.py:80
  11.3 29.8 %copy-start.54 = (f32[512]{0:T(512)}, f32[512]{0:T(512)S(1)}, u32[]{:S(2)}) copy-start(f32[512]{0:T(512)S(1)} %broadcast_multiply_fusion.8) | copy-start | bytes 6148
  12.2 28.8 %copy-start.76 = (f32[512]{0:T(512)}, f32[512]{0:T(512)S(1)}, u32[]{:S(2)}) copy-start(f32[512]{0:T(512)S(1)} %fusion.175) | copy-start | bytes 6148
  43.9 31.5 %copy-start.143 = (f32[512,1024]{1,0:T(8,128)}, f32[512,1024]{1,0:T(8,128)S(1)}, u32[]{:S(2)}) copy-start(f32[512,1024]{1,0:T(8,128)S(1)} %fusion.109) | copy-start | bytes 6291460
  43.9 31.6 %copy-start.42 = (f32[3,128,256]{2,1,0:T(8,128)S(1)}, f32[3,128,256]{2,1,0:T(8,128)}, u32[]{:S(2)}) copy-start(f32[3,128,256]{2,1,0:T(8,128)} %param.93) | copy-start | bytes 1179652
  75.5 79.2 %all-gather.15.cloned.1.call-start = ((), (), s32[]{:S(2)}) async-start(), calls=%async_computation.12 | async-start | bytes 1769472 | tf_op jit(solution)/shard_map/all_gather | solution.py:59
  76.3 78.5 %copy-start.58 = (f32[1024]{0:T(1024)S(1)}, f32[1024]{0:T(1024)}, u32[]{:S(2)}) copy-start(f32[1024]{0:T(1024)} %param.92) | copy-start | bytes 12292
  76.3 99.0 %all-gather.25.cloned.1.call-start = ((), (), s32[]{:S(2)}) async-start(), calls=%async_computation.34 | async-start | bytes 1310720 | tf_op jit(solution)/shard_map/all_gather | solution.py:193
  129.3 25.5 %copy-start.56 = (f32[512]{0:T(512)}, f32[512]{0:T(512)S(1)}, u32[]{:S(2)}) copy-start(f32[512]{0:T(512)S(1)} %broadcast_multiply_fusion.7) | copy-start | bytes 6148
  130.4 24.4 %copy-start.80 = (f32[512]{0:T(512)}, f32[512]{0:T(512)S(1)}, u32[]{:S(2)}) copy-start(f32[512]{0:T(512)S(1)} %fusion.176) | copy-start | bytes 6148
  158.3 35.7 %all-gather.23.cloned.1.call-start = ((), (), s32[]{:S(2)}) async-start(), calls=%async_computation.33 | async-start | bytes 1310720 | tf_op jit(solution)/shard_map/all_gather | solution.py:192
  158.8 198.1 %all-reduce.22.cloned.1.call-start = ((), (), s32[]{:S(2)}) async-start(), calls=%async_computation.13 | async-start | bytes 2097152 | tf_op jit(solution)/shard_map/psum | solution.py:80
  169.3 134.1 %copy-start.26 = (bf16[256,1024]{1,0:T(8,128)(2,1)}, bf16[256,1024]{1,0:T(8,128)(2,1)S(1)}, u32[]{:S(2)}) copy-start(bf16[256,1024]{1,0:T(8,128)(2,1)S(1)} %all_gather.43) | copy-start | bytes 1572868
  304.9 77.2 %all-gather.17.cloned.1.call-start = ((), (), s32[]{:S(2)}) async-start(), calls=%async_computation.14 | async-start | bytes 1179648 | tf_op jit(solution)/shard_map/all_gather | solution.py:59
  305.6 158.3 %all-reduce.24.cloned.1.call-start = ((), (), s32[]{:S(2)}) async-start(), calls=%async_computation.15 | async-start | bytes 2097152 | tf_op jit(solution)/shard_map/psum | solution.py:80
  359.0 469.0 %copy-start.5 = (f32[512,1024]{1,0:T(8,128)}, f32[512,1024]{1,0:T(8,128)S(1)}, u32[]{:S(2)}) copy-start(f32[512,1024]{1,0:T(8,128)S(1)} %get-tuple-element.976) | copy-start | bytes 6291460
  359.0 23.1 %copy-start.50 = (f32[1024]{0:T(1024)S(1)}, f32[1024]{0:T(1024)}, u32[]{:S(2)}) copy-start(f32[1024]{0:T(1024)} %param.96) | copy-start | bytes 12292
  359.1 469.0 %copy-start.48 = (f32[512]{0:T(512)}, f32[512]{0:T(512)S(1)}, u32[]{:S(2)}) copy-start(f32[512]{0:T(512)S(1)} %broadcast_multiply_fusion.6) | copy-start | bytes 6148
  359.4 468.6 %copy-start.65 = (f32[512]{0:T(512)}, f32[512]{0:T(512)S(1)}, u32[]{:S(2)}) copy-start(f32[512]{0:T(512)S(1)} %fusion.177) | copy-start | bytes 6148
  359.4 27.2 %copy-start.43 = (bf16[256,128]{1,0:T(8,128)(2,1)S(1)}, bf16[256,128]{1,0:T(8,128)(2,1)}, u32[]{:S(2)}) copy-start(bf16[256,128]{1,0:T(8,128)(2,1)} %convert_element_type.255) | copy-start | bytes 196612
  384.1 13.7 copy-start.28
  384.5 277.7 %copy-start.13 = (f32[512,256]{1,0:T(8,128)}, f32[512,256]{1,0:T(8,128)S(1)}, u32[]{:S(2)}) copy-start(f32[512,256]{1,0:T(8,128)S(1)} %fusion.168) | copy-start | bytes 1572868
  384.5 13.2 collective-permute-start
  397.7 370.2 %copy-start.39 = (f32[30,256]{1,0:T(8,128)}, f32[30,256]{1,0:T(8,128)S(1)}, u32[]{:S(2)}) copy-start(f32[30,256]{1,0:T(8,128)S(1)} %collective-permute-done) | copy-start | bytes 92164
  400.4 249.1 %copy-start.24 = (f32[512,256]{1,0:T(8,128)}, f32[512,256]{1,0:T(8,128)S(1)}, u32[]{:S(2)}) copy-start(f32[512,256]{1,0:T(8,128)S(1)} %get-tuple-element.974) | copy-start | bytes 1572868
  412.1 250.1 %copy-start.68 = (f32[512]{0:T(512)}, f32[512]{0:T(512)S(1)}, u32[]{:S(2)}) copy-start(f32[512]{0:T(512)S(1)} %get-tuple-element.1024) | copy-start | bytes 6148
  412.1 250.1 %copy-start.70 = (f32[512]{0:T(512)}, f32[512]{0:T(512)S(1)}, u32[]{:S(2)}) copy-start(f32[512]{0:T(512)S(1)} %get-tuple-element.1025) | copy-start | bytes 6148
  414.7 78.7 %all-gather.27.cloned.1.call-start = ((), (), s32[]{:S(2)}) async-start(), calls=%async_computation.35 | async-start | bytes 2359296 | tf_op jit(solution)/shard_map/all_gather | solution.py:59
  416.5 107.4 %all-gather.19.cloned.1.call-start = ((), (), s32[]{:S(2)}) async-start(), calls=%async_computation.16 | async-start | bytes 2359296 | tf_op jit(solution)/shard_map/all_gather | solution.py:60
  418.5 162.0 %all-reduce.26.cloned.1.call-start = ((), (), s32[]{:S(2)}) async-start(), calls=%async_computation.17 | async-start | bytes 2097152 | tf_op jit(solution)/shard_map/psum | solution.py:80
  465.5 27.9 %copy-start.60 = (f32[1024]{0:T(1024)S(1)}, f32[1024]{0:T(1024)}, u32[]{:S(2)}) copy-start(f32[1024]{0:T(1024)} %param.101) | copy-start | bytes 12292
  465.5 183.2 %copy-start.52 = (f32[512]{0:T(512)}, f32[512]{0:T(512)S(1)}, u32[]{:S(2)}) copy-start(f32[512]{0:T(512)S(1)} %broadcast_multiply_fusion.4) | copy-start | bytes 6148
  467.2 181.5 %copy-start.72 = (f32[512]{0:T(512)}, f32[512]{0:T(512)S(1)}, u32[]{:S(2)}) copy-start(f32[512]{0:T(512)S(1)} %fusion.178) | copy-start | bytes 6148
  528.4 115.8 %all-reduce.28.cloned.1.call-start = ((), (), s32[]{:S(2)}) async-start(), calls=%async_computation.18 | async-start | bytes 2097152 | tf_op jit(solution)/shard_map/psum | solution.py:84
  593.0 231.6 %all-reduce.30.cloned.1.call-start = ((), (), s32[]{:S(2)}) async-start(), calls=%async_computation.19 | async-start | bytes 2097152 | tf_op jit(solution)/shard_map/psum | solution.py:84
  664.8 103.1 %copy-start = (f32[512,256]{1,0:T(8,128)}, f32[512,256]{1,0:T(8,128)S(1)}, u32[]{:S(2)}) copy-start(f32[512,256]{1,0:T(8,128)S(1)} %get-tuple-element.967) | copy-start | bytes 1572868
  764.7 3.2 collective-permute-start.1
  773.7 485.8 %reduce-scatter.11.cloned.1.call-start = ((), (), s32[]{:S(2)}) async-start(), calls=%async_computation.20 | async-start | bytes 1310720 | tf_op jit(solution)/shard_map/reduce_scatter | solution.py:232
  1235.0 51.7 %copy-start.38 = (bf16[4,512,64]{1,2,0:T(8,128)(2,1)S(1)}, bf16[4,512,64]{1,2,0:T(8,128)(2,1)}, u32[]{:S(2)}) copy-start(bf16[4,512,64]{1,2,0:T(8,128)(2,1)} %get-tuple-element.816) | copy-start | bytes 786436
  1235.1 51.6 %reduce-scatter.13.cloned.1.call-start = ((), (), s32[]{:S(2)}) async-start(), calls=%async_computation.21 | async-start | bytes 1310720 | tf_op jit(solution)/shard_map/reduce_scatter | solution.py:235
  1235.7 107.9 %all-reduce.32.cloned.1.call-start = ((), (), s32[]{:S(2)}) async-start(), calls=%async_computation.22 | async-start | bytes 2097152 | tf_op jit(solution)/shard_map/psum | solution.py:371
  1291.5 115.9 %reduce-scatter.23.cloned.1.call-start = ((), (), s32[]{:S(2)}) async-start(), calls=%async_computation.28 | async-start | bytes 2359296 | tf_op jit(solution)/shard_map/reduce_scatter | solution.py:74
  1291.6 51.9 %copy-start.59 = (f32[1024]{0:T(1024)S(1)}, f32[1024]{0:T(1024)}, u32[]{:S(2)}) copy-start(f32[1024]{0:T(1024)} %param.92) | copy-start | bytes 12292
  1293.9 49.7 %copy-start.4 = (bf16[1,512,1024]{2,1,0:T(8,128)(2,1)S(1)}, bf16[1,512,1024]{2,1,0:T(8,128)(2,1)}, u32[]{:S(2)}) copy-start(bf16[1,512,1024]{2,1,0:T(8,128)(2,1)} %param.88) | copy-start | bytes 3145732
  1293.9 49.7 %copy-start.10 = (bf16[512,1024]{1,0:T(8,128)(2,1)S(1)}, bf16[512,1024]{1,0:T(8,128)(2,1)}, u32[]{:S(2)}) copy-start(bf16[512,1024]{1,0:T(8,128)(2,1)} %all-reduce.20.cloned.1.call-done) | copy-start | bytes 3145732
  1293.9 49.7 %copy-start.57 = (f32[512]{0:T(512)S(1)}, f32[512]{0:T(512)}, u32[]{:S(2)}) copy-start(f32[512]{0:T(512)} %copy-done.56) | copy-start | bytes 6148
  1293.9 51.7 %copy-start.79 = (f32[512]{0:T(512)S(1)}, f32[512]{0:T(512)}, u32[]{:S(2)}) copy-start(f32[512]{0:T(512)} %copy-done.78) | copy-start | bytes 6148
  1293.9 51.7 %copy-start.81 = (f32[512]{0:T(512)S(1)}, f32[512]{0:T(512)}, u32[]{:S(2)}) copy-start(f32[512]{0:T(512)} %copy-done.80) | copy-start | bytes 6148
  1294.0 147.8 %all-reduce.34.cloned.1.call-start = ((), (), s32[]{:S(2)}) async-start(), calls=%async_computation.23 | async-start | bytes 2097152 | tf_op jit(solution)/shard_map/psum | solution.py:84
  1354.5 135.8 %reduce-scatter.19.cloned.1.call-start = ((), (), s32[]{:S(2)}) async-start(), calls=%async_computation.26 | async-start | bytes 3538944 | tf_op jit(solution)/shard_map/reduce_scatter | solution.py:74
  1357.4 172.6 %reduce-scatter.25.cloned.1.call-start = ((), (), s32[]{:S(2)}) async-start(), calls=%async_computation.29 | async-start | bytes 1179648 | tf_op jit(solution)/shard_map/reduce_scatter | solution.py:75
  1361.8 208.0 %reduce-scatter.21.cloned.1.call-start = ((), (), s32[]{:S(2)}) async-start(), calls=%async_computation.27 | async-start | bytes 1179648 | tf_op jit(solution)/shard_map/reduce_scatter | solution.py:75
  1364.9 260.0 %reduce-scatter.29.cloned.1.call-start = ((), (), s32[]{:S(2)}) async-start(), calls=%async_computation.31 | async-start | bytes 4718592 | tf_op jit(solution)/shard_map/reduce_scatter | solution.py:75
  1370.7 309.2 %reduce-scatter.27.cloned.1.call-start = ((), (), s32[]{:S(2)}) async-start(), calls=%async_computation.30 | async-start | bytes 4718592 | tf_op jit(solution)/shard_map/reduce_scatter | solution.py:74
  1376.9 357.9 %reduce-scatter.17.cloned.1.call-start = ((), (), s32[]{:S(2)}) async-start(), calls=%async_computation.25 | async-start | bytes 4718592 | tf_op jit(solution)/shard_map/reduce_scatter | solution.py:75
  1382.5 407.3 %reduce-scatter.15.cloned.1.call-start = ((), (), s32[]{:S(2)}) async-start(), calls=%async_computation.24 | async-start | bytes 4718592 | tf_op jit(solution)/shard_map/reduce_scatter | solution.py:74
  1389.0 54.5 %copy-start.75 = (f32[512]{0:T(512)S(1)}, f32[512]{0:T(512)}, u32[]{:S(2)}) copy-start(f32[512]{0:T(512)} %copy-done.74) | copy-start | bytes 6148
  1409.2 35.6 %copy-start.82 = (f32[1024]{0:T(1024)S(1)}, f32[1024]{0:T(1024)}, u32[]{:S(2)}) copy-start(f32[1024]{0:T(1024)} %get-tuple-element.864) | copy-start | bytes 12292
  1409.2 35.6 %copy-start.83 = (f32[1024]{0:T(1024)S(1)}, f32[1024]{0:T(1024)}, u32[]{:S(2)}) copy-start(f32[1024]{0:T(1024)} %get-tuple-element.858) | copy-start | bytes 12292
  1409.2 35.6 %copy-start.84 = (f32[1024]{0:T(1024)S(1)}, f32[1024]{0:T(1024)}, u32[]{:S(2)}) copy-start(f32[1024]{0:T(1024)} %get-tuple-element.860) | copy-start | bytes 12292
  1409.2 35.6 %copy-start.137 = (f32[256]{0:T(256)S(1)}, f32[256]{0:T(256)}, u32[]{:S(2)}) copy-start(f32[256]{0:T(256)} %get-tuple-element.898) | copy-start | bytes 3076
  (123 other events, 555.1 us)
Sparse Core Ops, SparseCore 0:
  10.5 30.4 all-gather.20
  43.5 28.0 all-gather.12
  75.6 51.8 all-reduce.19
  129.8 24.8 all-gather.14
  158.4 16.8 all-gather.24
  177.3 16.6 all-gather.22
  305.0 51.8 all-reduce.21
  359.4 22.6 all-gather.16
  414.8 49.1 all-reduce.23
  466.3 27.0 all-gather.26
  495.8 28.0 all-gather.18
  528.6 51.8 all-reduce.25
  593.1 51.1 all-reduce.27
  773.8 50.7 all-reduce.29
  1235.2 24.2 reduce-scatter.10
  1261.9 24.7 reduce-scatter.12
  1291.6 51.8 all-reduce.31
  1346.7 40.3 reduce-scatter.22
  1389.5 52.2 all-reduce.33
  1444.9 45.3 reduce-scatter.18
  1494.1 35.9 reduce-scatter.24
  1533.8 35.9 reduce-scatter.20
  1573.7 51.0 reduce-scatter.28
  1628.6 51.1 reduce-scatter.26
  1683.8 51.0 reduce-scatter.16
  1738.6 51.1 reduce-scatter.14
where the time goes:
time: 1810 us; the launch traced here: 1800 us
  waiting for transfers between devices  929 us (51%)
  local copies, waits for them, and re-layouts  465 us (26%)
  matrix products  161 us (9%)
  other arithmetic  119 us (7%)
  blocking collectives  86.6 us (5%)
    psum x4, waiting for transfers between devices, branch_total(): lax.psum(partial_sum.astype(jnp.bfloat16), 'tensor').astype(jnp.float32)  197 us
    reduce_scatter x4, waiting for transfers between devices, send_grads(): lax.psum_scatter(grad_out, ('clips', 'context'), scatter_dimension=1, til...  188 us
    psum x3, waiting for transfers between devices, input_total(): lax.psum(partial_sum.astype(jnp.bfloat16), 'tensor').astype(jnp.float32)  134 us
    reshape x16, local copies, waits for them, and re-layouts, skew_band(): widened.reshape(-1)[:query_count * width].reshape(query_count, width)  128 us
    reduce_scatter x4, waiting for transfers between devices, send_grads(): lax.psum_scatter(grad_in, ('clips', 'context'), scatter_dimension=1, tile...  126 us
    all_gather x4, waiting for transfers between devices, fetch(): lax.all_gather(weight_in.astype(jnp.bfloat16), ('clips', 'context'), axis...  102 us
    dynamic_update_slice x4, local copies, waits for them, and re-layouts, unskew_band(): lax.dynamic_update_slice_in_dim(extended, grad_tile, key_count - first_ro...  88.1 us
    scatter-add x27, local copies, waits for them, and re-layouts, conv_backward(): padded_grad.at[offset:offset + rows_here]  69.4 us
  transfers between devices with their start and end apart: 28, of which 26 were waited for; matrix products, arithmetic and copies ran while one was open for 4% of the time, Pallas kernels for 0%

commit v1 on v0

--- a/solution.py
+++ b/solution.py
@@ -4,6 +4,8 @@
 import jax
 import jax.numpy as jnp
 from jax import lax
+from jax.experimental import pallas as pl
+from jax.experimental.pallas import tpu as pltpu
 from jax.sharding import PartitionSpec as P
 
 D = 1024
@@ -69,11 +71,15 @@
     return result_pair
 
 
+def scatter_sum(grad, axis):
+    summed = lax.psum_scatter(
+        grad.astype(jnp.bfloat16), ("clips", "context"), scatter_dimension=axis, tiled=True
+    )
+    return summed.astype(jnp.float32)
+
+
 def send_grads(grad_in, grad_out):
-    return (
-        lax.psum_scatter(grad_in, ("clips", "context"), scatter_dimension=1, tiled=True),
-        lax.psum_scatter(grad_out, ("clips", "context"), scatter_dimension=1, tiled=True),
-    )
+    return (scatter_sum(grad_in, 1), scatter_sum(grad_out, 1))
 
 
 def branch_total(partial_sum):
@@ -103,87 +109,226 @@
     return (upstream + rows_grad, gain_grad, grad_in, grad_out)
 
 
-def skew_band(band_rows, first_row, key_count):
-    query_count, band_width = band_rows.shape
-    width = key_count + LEFT + band_width
-    widened = jnp.pad(band_rows, ((0, 0), (0, width + 1 - band_width)))
-    shifted = widened.reshape(-1)[: query_count * width].reshape(query_count, width)
-    extended = jnp.concatenate([jnp.zeros((query_count, key_count), jnp.float32), shifted], axis=1)
-    return lax.dynamic_slice_in_dim(extended, key_count - first_row + LEFT, key_count, 1)
-
-
-def unskew_band(grad_tile, first_row, band_width):
-    query_count, key_count = grad_tile.shape
-    width = key_count + LEFT + band_width
-    extended = jnp.zeros((query_count, key_count + width), jnp.float32)
-    extended = lax.dynamic_update_slice_in_dim(extended, grad_tile, key_count - first_row + LEFT, 1)
-    flat = extended[:, key_count:].reshape(-1)
-    flat = jnp.concatenate([flat, jnp.zeros((query_count,), jnp.float32)])
-    return flat.reshape(query_count, width + 1)[:, :band_width]
-
-
-def head_scores(query_h, key_h, rel_table, position):
-    query_count = query_h.shape[0]
-    key_count = key_h.shape[0]
-    content = dot_outer(query_h, key_h)
-    rel_scores = dot_outer(query_h, rel_table)
-    first_row = position * query_count
-    query_rows = first_row + jnp.arange(query_count, dtype=jnp.int32)
-    key_cols = jnp.arange(key_count, dtype=jnp.int32)
-    offsets = key_cols[None, :] - query_rows[:, None]
-    banded = skew_band(rel_scores, first_row, key_count)
-    rel_bias = jnp.where(
-        offsets < -LEFT, rel_scores[:, :1], jnp.where(offsets > RIGHT, rel_scores[:, -1:], banded)
-    )
-    return ((content + rel_bias) * (1.0 / math.sqrt(HEAD_DIM)), offsets, first_row)
-
-
-def head_forward(head, queries, key_rows, value_rows, rel_table, position):
-    start_col = head * HEAD_DIM
-    query_h = lax.dynamic_slice_in_dim(queries, start_col, HEAD_DIM, 1)
-    key_h = lax.dynamic_slice_in_dim(key_rows, start_col, HEAD_DIM, 1)
-    value_h = lax.dynamic_slice_in_dim(value_rows, start_col, HEAD_DIM, 1)
-    logits, offsets, first_row = head_scores(query_h, key_h, rel_table, position)
-    row_max = jnp.max(logits, axis=1, keepdims=True)
-    log_total = row_max + jnp.log(jnp.sum(jnp.exp(logits - row_max), axis=1, keepdims=True))
-    attend_prob = jnp.exp(logits - log_total).astype(jnp.bfloat16)
-    return (dot_rows(attend_prob, value_h), log_total)
-
-
-def head_backward(head, queries, key_rows, value_rows, mixed_grad, log_total, rel_table, position):
-    score_scale = 1.0 / math.sqrt(HEAD_DIM)
-    start_col = head * HEAD_DIM
-    query_h = lax.dynamic_slice_in_dim(queries, start_col, HEAD_DIM, 1)
-    key_h = lax.dynamic_slice_in_dim(key_rows, start_col, HEAD_DIM, 1)
-    value_h = lax.dynamic_slice_in_dim(value_rows, start_col, HEAD_DIM, 1)
-    grad_h = lax.dynamic_slice_in_dim(mixed_grad, start_col, HEAD_DIM, 1)
-    logits, offsets, first_row = head_scores(query_h, key_h, rel_table, position)
-    attend_prob = jnp.exp(logits - log_total[head])
-    value_grad = dot_inner(attend_prob.astype(jnp.bfloat16), grad_h)
-    prob_grad = dot_outer(grad_h, value_h)
-    logit_grad = attend_prob * (prob_grad - jnp.sum(attend_prob * prob_grad, axis=1, keepdims=True))
-    logit_grad = logit_grad.astype(jnp.bfloat16)
-    query_grad = score_scale * dot_rows(logit_grad, key_h)
-    key_grad = score_scale * dot_inner(logit_grad, query_h)
-    wide_grad = logit_grad.astype(jnp.float32)
-    inside = (offsets >= -LEFT) & (offsets <= RIGHT)
-    bin_grad = unskew_band(jnp.where(inside, wide_grad, 0.0), first_row, rel_table.shape[0])
-    below = jnp.sum(jnp.where(offsets < -LEFT, wide_grad, 0.0), axis=1)
-    above = jnp.sum(jnp.where(offsets > RIGHT, wide_grad, 0.0), axis=1)
-    bin_grad = bin_grad.at[:, 0].add(below)
-    bin_grad = bin_grad.at[:, -1].add(above)
-    bin_grad = score_scale * bin_grad
-    query_grad = query_grad + jnp.dot(bin_grad, rel_table.astype(jnp.float32), precision=highest)
-    table_grad = lax.dot_general(
-        bin_grad, query_h.astype(jnp.float32), (((0,), (0,)), ((), ())), precision=highest
-    )
-    return (query_grad, key_grad, value_grad, table_grad)
+QB = 128
+BAND = 3 * QB
+SPAN = 4 * QB
+NT = (((1,), (1,)), ((), ()))
+
+
+def span_table(relative):
+    table = relative.astype(jnp.bfloat16)
+    low = jnp.broadcast_to(table[:1], (2 * QB - 1 - LEFT, table.shape[1]))
+    high = jnp.broadcast_to(table[-1:], (SPAN - (2 * QB - 1 - LEFT) - table.shape[0], table.shape[1]))
+    spread = jnp.concatenate([low, table, high], axis=0)
+    return jnp.concatenate([spread, spread], axis=1)
+
+
+def fill_scores(first_block, q_mask, k_ref, span_ref, s_ref, edge_ref):
+    keys = k_ref.shape[0]
+    s_ref[:, QB : QB + keys] = lax.dot_general(q_mask, k_ref[...], NT, preferred_element_type=jnp.float32)
+    spread = lax.dot_general(q_mask, span_ref[...], NT, preferred_element_type=jnp.float32)
+    edge_ref[0] = jnp.broadcast_to(spread[:, :1], (QB, QB))
+    edge_ref[1] = jnp.zeros((QB, QB), jnp.float32)
+    edge_ref[2] = jnp.broadcast_to(spread[:, SPAN - 1 :], (QB, QB))
+    skewed = pltpu.roll(spread, SPAN - (QB - 1), 1, stride=1, stride_axis=0)
+    at = pl.ds(pl.multiple_of(first_block * QB, QB), BAND)
+    s_ref[:, at] = s_ref[:, at] + skewed[:, :BAND]
+
+
+def edge_of(block, first_block):
+    return jnp.where(block < first_block - 1, 0, jnp.where(block > first_block + 1, 2, 1))
+
+
+def forward_kernel(pos_ref, q_ref, k_ref, v_ref, span_ref, o_ref, lse_ref, s_ref, edge_ref, p_ref):
+    keys = k_ref.shape[0]
+    blocks = keys // QB
+    first_block = pos_ref[0] * pl.num_programs(1) + pl.program_id(1)
+    lane = lax.broadcasted_iota(jnp.int32, (QB, 2 * HEAD_DIM), 1)
+    outs, lses = [], []
+    for half in range(2):
+        mine = (lane < HEAD_DIM) if half == 0 else (lane >= HEAD_DIM)
+        q_mask = jnp.where(mine, q_ref[...], jnp.zeros_like(q_ref))
+        fill_scores(first_block, q_mask, k_ref, span_ref, s_ref, edge_ref)
+        top = None
+        for block in range(blocks):
+            z = s_ref[:, (block + 1) * QB : (block + 2) * QB] + edge_ref[edge_of(block, first_block)]
+            top = z if top is None else jnp.maximum(top, z)
+        top = jnp.max(top, axis=1, keepdims=True)
+        edge_ref[...] = edge_ref[...] - top[None]
+        total = None
+        for block in range(blocks):
+            z = s_ref[:, (block + 1) * QB : (block + 2) * QB] + edge_ref[edge_of(block, first_block)]
+            p = jnp.exp(z)
+            total = p if total is None else total + p
+            p_ref[:, block * QB : (block + 1) * QB] = p.astype(jnp.bfloat16)
+        total = jnp.sum(total, axis=1, keepdims=True)
+        out = jnp.dot(p_ref[...], v_ref[...], preferred_element_type=jnp.float32) / total
+        outs.append(out)
+        lses.append(jnp.broadcast_to(top + jnp.log(total), (QB, 2 * HEAD_DIM)))
+    low = lane < HEAD_DIM
+    o_ref[...] = jnp.where(low, outs[0], outs[1]).astype(o_ref.dtype)
+    lse_ref[...] = jnp.where(low, lses[0], lses[1])
+
+
+def attention_forward(position, q, k, v, span):
+    rows, width = q.shape
+    keys = k.shape[0]
+    pairs = width // (2 * HEAD_DIM)
+    two = 2 * HEAD_DIM
+    row_spec = pl.BlockSpec((QB, two), lambda p, b, pos: (b, p))
+    key_spec = pl.BlockSpec((keys, two), lambda p, b, pos: (0, p))
+    return pl.pallas_call(
+        forward_kernel,
+        out_shape=(
+            jax.ShapeDtypeStruct((rows, width), jnp.bfloat16),
+            jax.ShapeDtypeStruct((rows, width), jnp.float32),
+        ),
+        grid_spec=pltpu.PrefetchScalarGridSpec(
+            num_scalar_prefetch=1,
+            grid=(pairs, rows // QB),
+            in_specs=[row_spec, key_spec, key_spec, pl.BlockSpec((SPAN, two), lambda p, b, pos: (0, 0))],
+            out_specs=(row_spec, row_spec),
+            scratch_shapes=[
+                pltpu.VMEM((QB, keys + 2 * QB), jnp.float32),
+                pltpu.VMEM((3, QB, QB), jnp.float32),
+                pltpu.VMEM((QB, keys), jnp.bfloat16),
+            ],
+        ),
+        compiler_params=pltpu.CompilerParams(vmem_limit_bytes=40 << 20),
+        cost_estimate=pl.CostEstimate(flops=8 * rows * keys * width, bytes_accessed=4 * (keys + rows) * width, transcendentals=0),
+        name="attention_forward",
+    )(position.reshape(1), q, k, v, span)
+
+
+def backward_kernel(pos_ref, q_ref, qt_ref, g_ref, gt_ref, o_ref, lse_ref, k_ref, v_ref, span_ref,
+                    dq_ref, dkt_ref, dvt_ref, bins_ref, ends_ref,
+                    s_ref, edge_ref, d_ref, p_ref, z_ref, wide_ref, dk_acc, dv_acc):
+    keys = k_ref.shape[0]
+    blocks = keys // QB
+    step = pl.program_id(1)
+    first_block = pos_ref[0] * pl.num_programs(1) + step
+    lane = lax.broadcasted_iota(jnp.int32, (QB, 2 * HEAD_DIM), 1)
+
+    @pl.when((pl.program_id(0) == 0) & (step == 0))
+    def _():
+        bins_ref[...] = jnp.zeros_like(bins_ref)
+        ends_ref[...] = jnp.zeros_like(ends_ref)
+
+    @pl.when(step == 0)
+    def _():
+        dk_acc[...] = jnp.zeros_like(dk_acc)
+        dv_acc[...] = jnp.zeros_like(dv_acc)
+        wide_ref[:, : 2 * HEAD_DIM] = k_ref[...]
+
+    @pl.when((pl.program_id(0) == 0) & (step == 0))
+    def _():
+        z_ref[:, :QB] = jnp.zeros((QB, QB), jnp.bfloat16)
+        z_ref[:, QB + keys :] = jnp.zeros((QB, QB), jnp.bfloat16)
+
+    row_at = lax.broadcasted_iota(jnp.int32, (keys, QB), 0)
+    col_at = lax.broadcasted_iota(jnp.int32, (keys, QB), 1)
+    below = (row_at < (first_block - 1) * QB) & (col_at == 0)
+    above = (row_at >= (first_block + 2) * QB) & (col_at == 1)
+    wide_ref[:, 2 * HEAD_DIM :] = jnp.where(below | above, 1.0, 0.0).astype(jnp.bfloat16)
+
+    flip_at = lax.broadcasted_iota(jnp.int32, (QB, QB), 0) + lax.broadcasted_iota(jnp.int32, (QB, QB), 1)
+    flip = jnp.where(flip_at == QB - 1, 1.0, 0.0).astype(jnp.bfloat16)
+    dqs = []
+    for half in range(2):
+        rows = slice(half * HEAD_DIM, (half + 1) * HEAD_DIM)
+        mine = (lane < HEAD_DIM) if half == 0 else (lane >= HEAD_DIM)
+        q_mask = jnp.where(mine, q_ref[...], jnp.zeros_like(q_ref))
+        g_mask = jnp.where(mine, g_ref[...], jnp.zeros_like(g_ref))
+        fill_scores(first_block, q_mask, k_ref, span_ref, s_ref, edge_ref)
+        d_ref[...] = lax.dot_general(g_mask, v_ref[...], NT, preferred_element_type=jnp.float32)
+        delta = jnp.sum(g_mask.astype(jnp.float32) * o_ref[...].astype(jnp.float32), axis=1, keepdims=True)
+        lse = lse_ref[:, half * HEAD_DIM : half * HEAD_DIM + 1]
+        edge_ref[...] = edge_ref[...] - lse[None]
+        delta = jnp.broadcast_to(delta, (QB, QB))
+        for block in range(blocks):
+            here = slice(block * QB, (block + 1) * QB)
+            there = slice((block + 1) * QB, (block + 2) * QB)
+            p = jnp.exp(s_ref[:, there] + edge_ref[edge_of(block, first_block)])
+            p_ref[:, here] = p.astype(jnp.bfloat16)
+            z_ref[:, there] = (p * (d_ref[:, here] - delta)).astype(jnp.bfloat16)
+        z_all = z_ref[:, QB : QB + keys]
+        dv_acc[rows] += jnp.dot(gt_ref[rows], p_ref[...], preferred_element_type=jnp.float32)
+        dk_acc[rows] += jnp.dot(qt_ref[rows], z_all, preferred_element_type=jnp.float32)
+        dq = jnp.dot(z_all, wide_ref[...], preferred_element_type=jnp.float32)
+        at = pl.ds(pl.multiple_of(first_block * QB, QB), BAND)
+        band = jnp.dot(flip, z_ref[:, at], preferred_element_type=jnp.float32)
+        band = jnp.concatenate([band, jnp.zeros((QB, SPAN - BAND), jnp.float32)], axis=1)
+        spread = pltpu.roll(band, 0, 1, stride=1, stride_axis=0).astype(jnp.bfloat16)
+        spread = jnp.dot(flip, spread, preferred_element_type=jnp.float32).astype(jnp.bfloat16)
+        dq_rel = jnp.dot(spread, span_ref[...], preferred_element_type=jnp.float32)
+        below_sum = dq[:, 2 * HEAD_DIM : 2 * HEAD_DIM + 1]
+        above_sum = dq[:, 2 * HEAD_DIM + 1 : 2 * HEAD_DIM + 2]
+        span_low = span_ref[:1, :].astype(jnp.float32)
+        span_high = span_ref[SPAN - 1 :, :].astype(jnp.float32)
+        dqs.append(dq[:, : 2 * HEAD_DIM] + dq_rel + below_sum * span_low + above_sum * span_high)
+        bins_ref[...] += jnp.dot(qt_ref[rows], spread, preferred_element_type=jnp.float32)
+        q_wide = q_mask.astype(jnp.float32)
+        ends_ref[0:1, :] += jnp.sum(q_wide * below_sum, axis=0, keepdims=True)
+        ends_ref[1:2, :] += jnp.sum(q_wide * above_sum, axis=0, keepdims=True)
+    scale = 1.0 / 8.0
+    dq_ref[...] = (jnp.where(lane < HEAD_DIM, dqs[0], dqs[1]) * scale).astype(dq_ref.dtype)
+
+    @pl.when(step == pl.num_programs(1) - 1)
+    def _():
+        dkt_ref[...] = dk_acc[...].astype(dkt_ref.dtype)
+        dvt_ref[...] = dv_acc[...].astype(dvt_ref.dtype)
+
+
+def attention_backward(position, q, q_t, g, g_t, o, lse, k, v, span):
+    rows, width = q.shape
+    keys = k.shape[0]
+    pairs = width // (2 * HEAD_DIM)
+    two = 2 * HEAD_DIM
+    row_spec = pl.BlockSpec((QB, two), lambda p, b, pos: (b, p))
+    col_spec = pl.BlockSpec((two, QB), lambda p, b, pos: (p, b))
+    key_spec = pl.BlockSpec((keys, two), lambda p, b, pos: (0, p))
+    keyt_spec = pl.BlockSpec((two, keys), lambda p, b, pos: (p, 0))
+    fixed = lambda shape: pl.BlockSpec(shape, lambda p, b, pos: (0, 0))
+    dq, dkt, dvt, bins, ends = pl.pallas_call(
+        backward_kernel,
+        out_shape=(
+            jax.ShapeDtypeStruct((rows, width), jnp.bfloat16),
+            jax.ShapeDtypeStruct((width, keys), jnp.bfloat16),
+            jax.ShapeDtypeStruct((width, keys), jnp.bfloat16),
+            jax.ShapeDtypeStruct((HEAD_DIM, SPAN), jnp.float32),
+            jax.ShapeDtypeStruct((8, two), jnp.float32),
+        ),
+        grid_spec=pltpu.PrefetchScalarGridSpec(
+            num_scalar_prefetch=1,
+            grid=(pairs, rows // QB),
+            in_specs=[row_spec, col_spec, row_spec, col_spec, row_spec, row_spec, key_spec, key_spec, fixed((SPAN, two))],
+            out_specs=(row_spec, keyt_spec, keyt_spec, fixed((HEAD_DIM, SPAN)), fixed((8, two))),
+            scratch_shapes=[
+                pltpu.VMEM((QB, keys + 2 * QB), jnp.float32),
+                pltpu.VMEM((3, QB, QB), jnp.float32),
+                pltpu.VMEM((QB, keys), jnp.float32),
+                pltpu.VMEM((QB, keys), jnp.bfloat16),
+                pltpu.VMEM((QB, keys + 2 * QB), jnp.bfloat16),
+                pltpu.VMEM((keys, 2 * two), jnp.bfloat16),
+                pltpu.VMEM((two, keys), jnp.float32),
+                pltpu.VMEM((two, keys), jnp.float32),
+            ],
+        ),
+        compiler_params=pltpu.CompilerParams(vmem_limit_bytes=40 << 20),
+        cost_estimate=pl.CostEstimate(flops=20 * rows * keys * width, bytes_accessed=8 * (keys + rows) * width, transcendentals=0),
+        name="attention_backward",
+    )(position.reshape(1), q, q_t, g, g_t, o, lse, k, v, span)
+    at = 2 * QB - 1 - LEFT
+    ends = ends[:2, :HEAD_DIM] + ends[:2, HEAD_DIM:]
+    spread = bins.T
+    inner = spread[at + 1 : at + LEFT + RIGHT]
+    low = jnp.sum(spread[: at + 1], axis=0) + ends[0]
+    high = jnp.sum(spread[at + LEFT + RIGHT :], axis=0) + ends[1]
+    table = jnp.concatenate([low[None], inner, high[None]], axis=0)
+    return dq, dkt, dvt, table
 
 
 def attend_forward(rows_in, gain_vec, weight_in, weight_out, relative, position):
-    rows_here = rows_in.shape[0]
-    local_width = weight_in.shape[2]
-    local_heads = local_width // HEAD_DIM
     normed = layer_norm(rows_in, gain_vec).astype(jnp.bfloat16)
     projected = jnp.einsum(
         "td,kde->kte", normed, weight_in, preferred_element_type=jnp.float32
@@ -192,57 +337,29 @@
         lax.all_gather(projected[1], "context", axis=0, tiled=True),
         lax.all_gather(projected[2], "context", axis=0, tiled=True),
     )
-    per_head = partial(
-        head_forward,
-        queries=projected[0],
-        key_rows=key_rows,
-        value_rows=value_rows,
-        rel_table=relative.astype(jnp.bfloat16),
-        position=position,
-    )
-    head_outs, log_total = lax.map(per_head, jnp.arange(local_heads, dtype=jnp.int32))
-    mixed = jnp.transpose(head_outs, (1, 0, 2)).reshape(rows_here, local_width).astype(jnp.bfloat16)
+    queries = projected[0] * jnp.bfloat16(1.0 / math.sqrt(HEAD_DIM))
+    span = span_table(relative)
+    mixed, log_total = attention_forward(position, queries, key_rows, value_rows, span)
     return (
         branch_total(dot_rows(mixed, weight_out)),
-        (normed, projected, key_rows, value_rows, log_total, mixed),
+        (normed, queries, key_rows, value_rows, log_total, mixed, span),
     )
 
 
 def attend_backward(weight_in, weight_out, relative, position, saved, upstream):
-    normed, projected, key_rows, value_rows, log_total, mixed = saved
-    rows_here, local_width = mixed.shape
-    local_heads = local_width // HEAD_DIM
+    normed, queries, key_rows, value_rows, log_total, mixed, span = saved
     branch_grad = upstream.astype(jnp.bfloat16)
     grad_out = dot_inner(mixed, branch_grad)
     mixed_grad = dot_outer(branch_grad, weight_out).astype(jnp.bfloat16)
-    per_head = partial(
-        head_backward,
-        queries=projected[0],
-        key_rows=key_rows,
-        value_rows=value_rows,
-        mixed_grad=mixed_grad,
-        log_total=log_total,
-        rel_table=relative.astype(jnp.bfloat16),
-        position=position,
-    )
-    query_grad, key_grad, value_grad, table_grad = lax.map(
-        per_head, jnp.arange(local_heads, dtype=jnp.int32)
-    )
-    key_grad, value_grad = (
-        lax.psum_scatter(
-            key_grad.astype(jnp.bfloat16), "context", scatter_dimension=1, tiled=True
-        ).astype(jnp.float32),
-        lax.psum_scatter(
-            value_grad.astype(jnp.bfloat16), "context", scatter_dimension=1, tiled=True
-        ).astype(jnp.float32),
-    )
-    stacked = jnp.stack([query_grad, key_grad, value_grad])
-    stacked = (
-        jnp.transpose(stacked, (0, 2, 1, 3)).reshape(3, rows_here, local_width).astype(jnp.bfloat16)
-    )
+    query_grad, key_grad, value_grad, table_grad = attention_backward(
+        position, queries, queries.T, mixed_grad, mixed_grad.T, mixed, log_total, key_rows, value_rows, span
+    )
+    key_grad = lax.psum_scatter(key_grad, "context", scatter_dimension=1, tiled=True)
+    value_grad = lax.psum_scatter(value_grad, "context", scatter_dimension=1, tiled=True)
+    stacked = jnp.stack([query_grad, key_grad.T, value_grad.T])
     grad_in = jnp.einsum("td,kte->kde", normed, stacked, preferred_element_type=jnp.float32)
     partial_sum = jnp.einsum("kte,kde->td", stacked, weight_in, preferred_element_type=jnp.float32)
-    return (partial_sum, jnp.sum(table_grad, axis=0), grad_in, grad_out)
+    return (partial_sum, table_grad, grad_in, grad_out)
 
 
 def conv_forward(rows_in, gain_vec, weight_in, weight_out, depthwise, gain_middle):

time: 1810 us -> 1240 us (0.69)
  local copies, waits for them, and re-layouts: 465 us -> 107 us
  matrix products: 161 us -> 65.5 us
  waiting for transfers between devices: 929 us -> 840 us
  other arithmetic: 119 us -> 59 us
  Pallas kernels: 0 us -> 47.1 us
    reduce_scatter x10 -> x4, waiting for transfers between devices: 365 us -> 135 us  [the longest x2 84.8 us: scatter_sum(): lax.psum_scatter(grad.astype(jnp.bfloat16), ('clips', 'context'), scatter...]
    reshape x24 -> x0, local copies, waits for them, and re-layouts: 192 us -> none  [the longest x16 128 us: skew_band(): widened.reshape(-1)[:query_count * width].reshape(query_count, width)]
    unnamed x26 -> x32, waiting for transfers between devices: 1.44 us -> 148 us
    dynamic_update_slice x8 -> x0, local copies, waits for them, and re-layouts: 88.1 us -> none  [the longest x4 88.1 us: unskew_band(): lax.dynamic_update_slice_in_dim(extended, grad_tile, key_count - first_ro...]
    dot_general x26 -> x6, matrix products: 68.5 us -> 9.68 us  [dot_outer(): lax.dot_general(former, latter, (((1,), (1,)), ((), ())), preferred_eleme...]
    pallas_call x0 -> x2, Pallas kernels: none -> 47.1 us  [the longest x1 31.1 us: attention_backward(): pl.pallas_call(backward_kernel, out_shape=(jax.ShapeDtypeStruct((rows, wi...]
    unnamed x297 -> x263, local copies, waits for them, and re-layouts: 18.7 us -> 49.1 us
    add x26, other arithmetic: 28.3 us -> 1.91 us  [conv_backward(): padded_grad.at[offset:offset + rows_here]]
  transfers between devices with their start and end apart: 28 -> 28, of which waited for: 26 -> 27; matrix products, arithmetic and copies ran while one was open for 4% -> 8% of each run, Pallas kernels for 0% -> 0%
where the time goes in v1:
time: 1240 us; the launch traced here: 1230 us
  waiting for transfers between devices  840 us (68%)
  local copies, waits for them, and re-layouts  107 us (9%)
  blocking collectives  88.7 us (7%)
  matrix products  65.5 us (5%)
  other arithmetic  59 us (5%)
  Pallas kernels  47.1 us (4%)
  between operations  16.5 us (1%)
    psum x4, waiting for transfers between devices, branch_total(): lax.psum(partial_sum.astype(jnp.bfloat16), 'tensor').astype(jnp.float32)  198 us
    psum x3, waiting for transfers between devices, input_total(): lax.psum(partial_sum.astype(jnp.bfloat16), 'tensor').astype(jnp.float32)  154 us
    unnamed x32, waiting for transfers between devices  148 us
    all_gather x4, waiting for transfers between devices, fetch(): lax.all_gather(weight_in.astype(jnp.bfloat16), ('clips', 'context'), axis...  103 us
    reduce_scatter x2, waiting for transfers between devices, scatter_sum(): lax.psum_scatter(grad.astype(jnp.bfloat16), ('clips', 'context'), scatter...  84.8 us
    scatter-add x27, local copies, waits for them, and re-layouts, conv_backward(): padded_grad.at[offset:offset + rows_here]  54.1 us
    all_gather x2, waiting for transfers between devices, fetch(): lax.all_gather(weight_out.astype(jnp.bfloat16), ('clips', 'context'), axi...  52.7 us
    unnamed x263, local copies, waits for them, and re-layouts  49.1 us
  transfers between devices with their start and end apart: 28, of which 27 were waited for; matrix products, arithmetic and copies ran while one was open for 8% of the time, Pallas kernels for 0%

profile of v1, /device:TPU:0, one launch (start us, length us, event | category | flops | bytes accessed | tf_op | source)
XLA Modules:
  0.0 1229.3 jit_solution(10990924159268640388)
XLA Ops:
  11.7 29.3 %all-gather.21.cloned.1.call-done = bf16[1024,1024]{1,0:T(8,128)(2,1)} async-done(((bf16[128,1024]{1,0:T(8,128)(2,1)}), bf16[1024,1024]{1,0:T(8,128)(2,1)}) %all-gather.21.cloned.1.call-update) | async-done | bytes 2097168 | tf_op jit(solution)/shard_map/all_gather | solution.py:61
  41.0 4.2 fusion.47
  45.2 26.4 %all-gather.13.cloned.1.call-done = bf16[1024,1024]{1,0:T(8,128)(2,1)} async-done(((bf16[1024,128]{1,0:T(8,128)(2,1)}), bf16[1024,1024]{1,0:T(8,128)(2,1)}) %all-gather.13.cloned.1.call-update) | async-done | bytes 2097168 | tf_op jit(solution)/shard_map/all_gather | solution.py:62
  71.6 4.5 convolution_convert_fusion.8
  76.9 51.2 %all-reduce.15.cloned.1.call-done = bf16[512,1024]{1,0:T(8,128)(2,1)} async-done(((bf16[512,1024]{1,0:T(8,128)(2,1)}), bf16[512,1024]{1,0:T(8,128)(2,1)}) %all-reduce.15.cloned.1.call-update) | async-done | bytes 1048592 | tf_op jit(solution)/shard_map/psum | solution.py:86
  130.5 24.9 %all-gather.15.cloned.1.call-done = bf16[3,1024,256]{2,1,0:T(8,128)(2,1)} async-done(((bf16[3,128,256]{2,1,0:T(8,128)(2,1)}), bf16[3,1024,256]{2,1,0:T(8,128)(2,1)}) %all-gather.15.cloned.1.call-update) | async-done | bytes 1572880 | tf_op jit(solution)/shard_map/all_gather | solution.py:61
  155.3 2.6 fusion.42
  159.7 11.8 all_gather.43
  171.7 4.6 all-gather.25.cloned.1.call-done
  176.3 18.7 %all-gather.23.cloned.1.call-done = bf16[1,2048,256]{2,1,0:T(8,128)(2,1)} async-done(((bf16[1,512,256]{2,1,0:T(8,128)(2,1)}), bf16[1,2048,256]{2,1,0:T(8,128)(2,1)}) %all-gather.23.cloned.1.call-update) | async-done | bytes 1048592 | tf_op jit(solution)/shard_map/all_gather | solution.py:337
  197.5 16.0 %attention_forward.1 = (bf16[512,256]{1,0:T(8,128)(2,1)S(1)}, f32[512,256]{1,0:T(8,128)S(1)}) custom-call(s32[1]{0:T(128)} %bitcast.2.pos_ref, bf16[512,256]{1,0:T(8,128)(2,1)S(1)} %get-tuple-element.514.q_ref, bf16[2048,256]{1,0:T(8,128)(2,1)S(1)} %bitcast.256, bf16[2048,256]{1,0:T(8,128)(2,1)S(1)} %bitcast.254, ...), custom_call_target="tpu_custom_call" | custom-call | flops 2147483648 | bytes 2621440 | tf_op jit(solution)/shard_map/attention_forward/pallas_call | solution.py:180
  219.4 47.6 %all-reduce.17.cloned.1.call-done = bf16[512,1024]{1,0:T(8,128)(2,1)} async-done(((bf16[512,1024]{1,0:T(8,128)(2,1)}), bf16[512,1024]{1,0:T(8,128)(2,1)}) %all-reduce.17.cloned.1.call-update) | async-done | bytes 1048592 | tf_op jit(solution)/shard_map/psum | solution.py:86
  270.4 21.7 %all-gather.17.cloned.1.call-done = bf16[2,1024,256]{2,1,0:T(8,128)(2,1)} async-done(((bf16[2,128,256]{2,1,0:T(8,128)(2,1)}), bf16[2,1024,256]{2,1,0:T(8,128)(2,1)}) %all-gather.17.cloned.1.call-update) | async-done | bytes 1048592 | tf_op jit(solution)/shard_map/all_gather | solution.py:61
  292.1 2.6 convolution_bitcast_fusion
  295.9 2.1 collective-permute-start
  298.0 10.1 all_gather.45
  308.3 2.4 fusion.134
  310.7 11.7 all-reduce.4
  322.5 2.3 convolution_convert_fusion.6
  326.5 47.6 %all-reduce.19.cloned.1.call-done = bf16[512,1024]{1,0:T(8,128)(2,1)} async-done(((bf16[512,1024]{1,0:T(8,128)(2,1)}), bf16[512,1024]{1,0:T(8,128)(2,1)}) %all-reduce.19.cloned.1.call-update) | async-done | bytes 1048592 | tf_op jit(solution)/shard_map/psum | solution.py:86
  374.0 2.1 fusion.137
  376.6 26.9 %all-gather.27.cloned.1.call-done = bf16[1024,1024]{1,0:T(8,128)(2,1)} async-done(((bf16[128,1024]{1,0:T(8,128)(2,1)}), bf16[1024,1024]{1,0:T(8,128)(2,1)}) %all-gather.27.cloned.1.call-update) | async-done | bytes 2097168 | tf_op jit(solution)/shard_map/all_gather | solution.py:61
  403.4 4.2 fusion.131
  407.7 26.3 %all-gather.19.cloned.1.call-done = bf16[1024,1024]{1,0:T(8,128)(2,1)} async-done(((bf16[1024,128]{1,0:T(8,128)(2,1)}), bf16[1024,1024]{1,0:T(8,128)(2,1)}) %all-gather.19.cloned.1.call-update) | async-done | bytes 2097168 | tf_op jit(solution)/shard_map/all_gather | solution.py:62
  434.0 4.5 convolution_convert_fusion.5
  438.6 52.0 %all-reduce.21.cloned.1.call-done = bf16[512,1024]{1,0:T(8,128)(2,1)} async-done(((bf16[512,1024]{1,0:T(8,128)(2,1)}), bf16[512,1024]{1,0:T(8,128)(2,1)}) %all-reduce.21.cloned.1.call-update) | async-done | bytes 1048592 | tf_op jit(solution)/shard_map/psum | solution.py:86
  500.2 2.3 convolution_convert_fusion.4
  502.9 50.9 %all-reduce.23.cloned.1.call-done = bf16[512,1024]{1,0:T(8,128)(2,1)} async-done(((bf16[512,1024]{1,0:T(8,128)(2,1)}), bf16[512,1024]{1,0:T(8,128)(2,1)}) %all-reduce.23.cloned.1.call-update) | async-done | bytes 1048592 | tf_op jit(solution)/shard_map/psum | solution.py:90
  559.8 10.2 all-reduce.3
  571.8 2.1 scatter-add.101
  576.2 2.1 scatter-add.105
  635.8 50.5 %all-reduce.25.cloned.1.call-done = bf16[512,1024]{1,0:T(8,128)(2,1)} async-done(((bf16[512,1024]{1,0:T(8,128)(2,1)}), bf16[512,1024]{1,0:T(8,128)(2,1)}) %all-reduce.25.cloned.1.call-update) | async-done | bytes 1048592 | tf_op jit(solution)/shard_map/psum | solution.py:90
  686.4 2.5 fusion.19
  688.9 2.9 fusion.22
  696.3 31.1 %attention_backward.1 = (bf16[512,256]{1,0:T(8,128)(2,1)S(1)}, bf16[256,2048]{1,0:T(8,128)(2,1)}, bf16[256,2048]{1,0:T(8,128)(2,1)}, f32[64,512]{1,0:T(8,128)S(1)}, f32[8,128]{1,0:T(8,128)S(1)}) custom-call(s32[1]{0:T(128)} %bitcast.2.pos_ref, bf16[512,256]{1,0:T(8,128)(2,1)S(1)} %get-tuple-element.514.q_ref, bf16[256,512]{1,0:T(8,128)(2,1)S(1)} %copy.49.qt_ref, ...), custom_call_target="tpu_custom_call" | custom-call | flops 5368709120 | bytes 5242880 | tf_op jit(solution)/shard_map/attention_backward/pallas_call | solution.py:292
  728.3 23.4 %reduce-scatter.23.cloned.1.call-done = bf16[256,512]{1,0:T(8,128)(2,1)} async-done(((bf16[256,2048]{1,0:T(8,128)(2,1)}), bf16[256,512]{1,0:T(8,128)(2,1)}) %reduce-scatter.23.cloned.1.call-update) | async-done | bytes 262160 | tf_op jit(solution)/shard_map/reduce_scatter | solution.py:357
  751.7 27.2 %reduce-scatter.25.cloned.1.call-done = bf16[256,512]{1,0:T(8,128)(2,1)} async-done(((bf16[256,2048]{1,0:T(8,128)(2,1)}), bf16[256,512]{1,0:T(8,128)(2,1)}) %reduce-scatter.25.cloned.1.call-update) | async-done | bytes 262160 | tf_op jit(solution)/shard_map/reduce_scatter | solution.py:358
  778.9 3.1 bitcast_convert_fusion
  782.1 3.2 convolution_convert_fusion.11
  787.5 2.8 fusion.40
  790.3 3.7 copy.67
  794.0 2.6 copy.74
  798.4 3.7 convolution_convert_fusion
  802.2 2.6 copy.71
  806.4 4.1 convert_bitcast_fusion.1
  810.5 23.5 %all-reduce.27.cloned.1.call-done = bf16[512,1024]{1,0:T(8,128)(2,1)} async-done(((bf16[512,1024]{1,0:T(8,128)(2,1)}), bf16[512,1024]{1,0:T(8,128)(2,1)}) %all-reduce.27.cloned.1.call-update) | async-done | bytes 1048592 | tf_op jit(solution)/shard_map/psum | solution.py:488
  842.7 2.3 convolution_convert_fusion.3
  845.1 2.5 fusion.39
  847.5 4.1 copy.63
  851.7 3.1 copy.73
  855.1 5.0 convolution_convert_fusion.1
  860.1 4.0 copy.61
  865.3 2.9 convert_bitcast_fusion.2
  873.4 18.8 %psum.161 = bf16[73,64]{0,1:T(8,128)(2,1)S(1)} all-reduce(bf16[73,64]{0,1:T(8,128)(2,1)S(1)} %pad_maximum_fusion.7), channel_id=1, replica_groups=mesh['clips'=2,'context'=4,'tensor'=4] {'tensor'}, use_global_device_ids=true, to_apply=%region_48.49 | all-reduce | flops 4672 | bytes 18688 | tf_op jit(solution)/shard_map/psum | solution.py:489
  892.1 18.0 %reduce-scatter.37.cloned.1.call-done = bf16[128,512]{1,0:T(8,128)(2,1)} async-done(((bf16[1024,512]{1,0:T(8,128)(2,1)}), bf16[128,512]{1,0:T(8,128)(2,1)}) %reduce-scatter.37.cloned.1.call-update) | async-done | bytes 131088
  912.0 35.8 %reduce-scatter.35.cloned.1.call-done = bf16[128,256]{1,0:T(8,128)(2,1)} async-done(((bf16[1024,256]{1,0:T(8,128)(2,1)}), bf16[128,256]{1,0:T(8,128)(2,1)}) %reduce-scatter.35.cloned.1.call-update) | async-done | bytes 65552
  949.4 42.8 %reduce-scatter.41.cloned.1.call-done = bf16[128,1024]{1,0:T(8,128)(2,1)} async-done(((bf16[1024,1024]{1,0:T(8,128)(2,1)}), bf16[128,1024]{1,0:T(8,128)(2,1)}) %reduce-scatter.41.cloned.1.call-update) | async-done | bytes 262160
  994.2 42.4 %reduce-scatter.29.cloned.1.call-done = bf16[1,128,1024]{2,1,0:T(8,128)(2,1)} async-done(((bf16[1,1024,1024]{2,1,0:T(8,128)(2,1)}), bf16[1,128,1024]{2,1,0:T(8,128)(2,1)}) %reduce-scatter.29.cloned.1.call-update) | async-done | bytes 262160 | tf_op jit(solution)/shard_map/reduce_scatter | solution.py:75
  1038.4 52.5 %all-reduce.29.cloned.1.call-done = bf16[512,1024]{1,0:T(8,128)(2,1)} async-done(((bf16[512,1024]{1,0:T(8,128)(2,1)}), bf16[512,1024]{1,0:T(8,128)(2,1)}) %all-reduce.29.cloned.1.call-update) | async-done | bytes 1048592 | tf_op jit(solution)/shard_map/psum | solution.py:90
  1094.1 26.2 %all-reduce.30 = (f32[1024]{0:T(1024)}, f32[1024]{0:T(1024)}, f32[73,64]{0,1:T(8,128)}, f32[1024]{0:T(1024)}, f32[31,256]{1,0:T(8,128)}, /*index=5*/f32[256]{0:T(256)}, f32[1024]{0:T(1024)}, f32[1024]{0:T(1024)}) all-reduce(f32[1024]{0:T(1024)S(1)} %get-tuple-element.448, ...), channel_id=1, replica_groups=mesh['clips'=2,'context'=4,'tensor'=4] {'clips','context'}, use_global_device_ids=true, to_apply=%region_39.40 | all-reduce | flops 17984 | bytes 134528 | tf_op jit(solution)/shard_map/psum | solution.py:499
  1120.3 3.7 add_bitcast_fusion
  1124.0 7.9 reduce-scatter.33.cloned.1.call-done
  1134.0 42.3 %reduce-scatter.31.cloned.1.call-done = bf16[128,1024]{1,0:T(8,128)(2,1)} async-done(((bf16[1024,1024]{1,0:T(8,128)(2,1)}), bf16[128,1024]{1,0:T(8,128)(2,1)}) %reduce-scatter.31.cloned.1.call-update) | async-done | bytes 262160
  1178.2 42.3 %reduce-scatter.27.cloned.1.call-done = bf16[1,128,1024]{2,1,0:T(8,128)(2,1)} async-done(((bf16[1,1024,1024]{2,1,0:T(8,128)(2,1)}), bf16[1,128,1024]{2,1,0:T(8,128)(2,1)}) %reduce-scatter.27.cloned.1.call-update) | async-done | bytes 262160 | tf_op jit(solution)/shard_map/reduce_scatter | solution.py:75
  (457 shorter events, 143.5 us)
Async XLA Ops:
  7.2 33.8 %copy-start.54 = (f32[1024]{0:T(1024)S(1)}, f32[1024]{0:T(1024)}, u32[]{:S(2)}) copy-start(f32[1024]{0:T(1024)} %param.81) | copy-start | bytes 12292
  7.2 33.8 %all-gather.21.cloned.1.call-start = ((), (), s32[]{:S(2)}) async-start(), calls=%async_computation.26 | async-start | bytes 2359296 | tf_op jit(solution)/shard_map/all_gather | solution.py:61
  9.1 62.5 %all-gather.13.cloned.1.call-start = ((), (), s32[]{:S(2)}) async-start(), calls=%async_computation.10 | async-start | bytes 2359296 | tf_op jit(solution)/shard_map/all_gather | solution.py:62
  11.0 117.2 %all-reduce.15.cloned.1.call-start = ((), (), s32[]{:S(2)}) async-start(), calls=%async_computation.11 | async-start | bytes 2097152 | tf_op jit(solution)/shard_map/psum | solution.py:86
  11.7 33.6 %copy-start.56 = (f32[512]{0:T(512)}, f32[512]{0:T(512)S(1)}, u32[]{:S(2)}) copy-start(f32[512]{0:T(512)S(1)} %fusion.26) | copy-start | bytes 6148
  11.7 33.5 %copy-start.58 = (f32[512]{0:T(512)}, f32[512]{0:T(512)S(1)}, u32[]{:S(2)}) copy-start(f32[512]{0:T(512)S(1)} %fusion.112) | copy-start | bytes 6148
  45.2 30.9 %copy-start.43 = (f32[3,128,256]{2,1,0:T(8,128)S(1)}, f32[3,128,256]{2,1,0:T(8,128)}, u32[]{:S(2)}) copy-start(f32[3,128,256]{2,1,0:T(8,128)} %param.85) | copy-start | bytes 1179652
  76.1 79.2 %all-gather.15.cloned.1.call-start = ((), (), s32[]{:S(2)}) async-start(), calls=%async_computation.12 | async-start | bytes 1769472 | tf_op jit(solution)/shard_map/all_gather | solution.py:61
  76.9 78.5 %copy-start.53 = (f32[1024]{0:T(1024)S(1)}, f32[1024]{0:T(1024)}, u32[]{:S(2)}) copy-start(f32[1024]{0:T(1024)} %param.84) | copy-start | bytes 12292
  76.9 99.4 %all-gather.25.cloned.1.call-start = ((), (), s32[]{:S(2)}) async-start(), calls=%async_computation.28 | async-start | bytes 1310720 | tf_op jit(solution)/shard_map/all_gather | solution.py:338
  130.4 27.6 %copy-start.60 = (f32[512]{0:T(512)}, f32[512]{0:T(512)S(1)}, u32[]{:S(2)}) copy-start(f32[512]{0:T(512)S(1)} %multiply_reduce_fusion.3) | copy-start | bytes 6148
  130.5 27.6 %copy-start.62 = (f32[512]{0:T(512)}, f32[512]{0:T(512)S(1)}, u32[]{:S(2)}) copy-start(f32[512]{0:T(512)S(1)} %fusion.113) | copy-start | bytes 6148
  159.0 36.1 %all-gather.23.cloned.1.call-start = ((), (), s32[]{:S(2)}) async-start(), calls=%async_computation.27 | async-start | bytes 1310720 | tf_op jit(solution)/shard_map/all_gather | solution.py:337
  159.5 107.4 %all-reduce.17.cloned.1.call-start = ((), (), s32[]{:S(2)}) async-start(), calls=%async_computation.13 | async-start | bytes 2097152 | tf_op jit(solution)/shard_map/psum | solution.py:86
  197.5 16.0 %copy-start.30 = (bf16[256,1024]{1,0:T(8,128)(2,1)S(1)}, bf16[256,1024]{1,0:T(8,128)(2,1)}, u32[]{:S(2)}) copy-start(bf16[256,1024]{1,0:T(8,128)(2,1)} %all_gather.43) | copy-start | bytes 1572868
  214.9 77.2 %all-gather.17.cloned.1.call-start = ((), (), s32[]{:S(2)}) async-start(), calls=%async_computation.14 | async-start | bytes 1179648 | tf_op jit(solution)/shard_map/all_gather | solution.py:61
  215.7 158.4 %all-reduce.19.cloned.1.call-start = ((), (), s32[]{:S(2)}) async-start(), calls=%async_computation.15 | async-start | bytes 2097152 | tf_op jit(solution)/shard_map/psum | solution.py:86
  218.3 89.9 %copy-start.71 = (f32[1,256]{1,0:T(1,128)}, f32[1,256]{1,0:T(1,128)S(1)}, u32[]{:S(2)}) copy-start(f32[1,256]{1,0:T(1,128)S(1)} %get-tuple-element.537) | copy-start | bytes 3076
  218.3 89.9 %copy-start.73 = (f32[1,256]{1,0:T(1,128)}, f32[1,256]{1,0:T(1,128)S(1)}, u32[]{:S(2)}) copy-start(f32[1,256]{1,0:T(1,128)S(1)} %get-tuple-element.538) | copy-start | bytes 3076
  218.3 89.9 %copy-start.75 = (f32[1,256]{1,0:T(1,128)}, f32[1,256]{1,0:T(1,128)S(1)}, u32[]{:S(2)}) copy-start(f32[1,256]{1,0:T(1,128)S(1)} %get-tuple-element.539) | copy-start | bytes 3076
  218.3 89.9 %copy-start.77 = (f32[1,256]{1,0:T(1,128)}, f32[1,256]{1,0:T(1,128)S(1)}, u32[]{:S(2)}) copy-start(f32[1,256]{1,0:T(1,128)S(1)} %get-tuple-element.540) | copy-start | bytes 3076
  218.3 89.9 %copy-start.79 = (f32[1,256]{1,0:T(1,128)}, f32[1,256]{1,0:T(1,128)S(1)}, u32[]{:S(2)}) copy-start(f32[1,256]{1,0:T(1,128)S(1)} %get-tuple-element.541) | copy-start | bytes 3076
  218.3 89.9 %copy-start.81 = (f32[1,256]{1,0:T(1,128)}, f32[1,256]{1,0:T(1,128)S(1)}, u32[]{:S(2)}) copy-start(f32[1,256]{1,0:T(1,128)S(1)} %get-tuple-element.542) | copy-start | bytes 3076
  218.3 89.9 %copy-start.83 = (f32[1,256]{1,0:T(1,128)}, f32[1,256]{1,0:T(1,128)S(1)}, u32[]{:S(2)}) copy-start(f32[1,256]{1,0:T(1,128)S(1)} %get-tuple-element.543) | copy-start | bytes 3076
  219.4 88.9 %copy-start.69 = (f32[1,256]{1,0:T(1,128)}, f32[1,256]{1,0:T(1,128)S(1)}, u32[]{:S(2)}) copy-start(f32[1,256]{1,0:T(1,128)S(1)} %get-tuple-element.535) | copy-start | bytes 3076
  268.8 23.4 %copy-start.51 = (f32[1024]{0:T(1024)S(1)}, f32[1024]{0:T(1024)}, u32[]{:S(2)}) copy-start(f32[1024]{0:T(1024)} %param.88) | copy-start | bytes 12292
  270.4 421.4 %copy-start.64 = (f32[512]{0:T(512)}, f32[512]{0:T(512)S(1)}, u32[]{:S(2)}) copy-start(f32[512]{0:T(512)S(1)} %fusion.114) | copy-start | bytes 6148
  295.9 12.3 %collective-permute-start = (f32[30,256]{1,0:T(8,128)S(1)}, f32[30,256]{1,0:T(8,128)S(1)}, u32[]{:S(2)}, u32[]{:S(2)}) collective-permute-start(f32[30,256]{1,0:T(8,128)S(1)} %slice.996), channel_id=1, source_target_pairs={{0,4},{4,8},{8,12},{1,5},{5,9},{9,13},{2,6},{6,10},{10,14},{3,7},{... | collective-permute-start | bytes 92168 | tf_op jit(solution)/shard_map/ppermute | solution.py:24
  308.2 16.6 %copy-start.41 = (bf16[256,1024]{1,0:T(8,128)(2,1)}, bf16[256,1024]{1,0:T(8,128)(2,1)S(1)}, u32[]{:S(2)}) copy-start(bf16[256,1024]{1,0:T(8,128)(2,1)S(1)} %all_gather.45) | copy-start | bytes 1572868
  310.7 14.0 %copy-start.34 = (f32[512,256]{1,0:T(8,128)}, f32[512,256]{1,0:T(8,128)S(1)}, u32[]{:S(2)}) copy-start(f32[512,256]{1,0:T(8,128)S(1)} %get-tuple-element.505) | copy-start | bytes 1572868
  322.5 247.5 %copy-start.93 = (f32[512]{0:T(512)}, f32[512]{0:T(512)S(1)}, u32[]{:S(2)}) copy-start(f32[512]{0:T(512)S(1)} %get-tuple-element.550) | copy-start | bytes 6148
  322.5 247.5 %copy-start.95 = (f32[512]{0:T(512)}, f32[512]{0:T(512)S(1)}, u32[]{:S(2)}) copy-start(f32[512]{0:T(512)S(1)} %get-tuple-element.551) | copy-start | bytes 6148
  324.8 78.6 %all-gather.27.cloned.1.call-start = ((), (), s32[]{:S(2)}) async-start(), calls=%async_computation.29 | async-start | bytes 2359296 | tf_op jit(solution)/shard_map/all_gather | solution.py:61
  325.6 108.4 %all-gather.19.cloned.1.call-start = ((), (), s32[]{:S(2)}) async-start(), calls=%async_computation.16 | async-start | bytes 2359296 | tf_op jit(solution)/shard_map/all_gather | solution.py:62
  326.4 164.1 %all-reduce.21.cloned.1.call-start = ((), (), s32[]{:S(2)}) async-start(), calls=%async_computation.17 | async-start | bytes 2097152 | tf_op jit(solution)/shard_map/psum | solution.py:86
  376.2 181.0 %copy-start.8 = (f32[512,1024]{1,0:T(8,128)}, f32[512,1024]{1,0:T(8,128)S(1)}, u32[]{:S(2)}) copy-start(f32[512,1024]{1,0:T(8,128)S(1)} %get-tuple-element.504) | copy-start | bytes 6291460
  376.2 27.2 %copy-start.52 = (f32[1024]{0:T(1024)S(1)}, f32[1024]{0:T(1024)}, u32[]{:S(2)}) copy-start(f32[1024]{0:T(1024)} %param.93) | copy-start | bytes 12292
  438.5 115.2 %all-reduce.23.cloned.1.call-start = ((), (), s32[]{:S(2)}) async-start(), calls=%async_computation.18 | async-start | bytes 2097152 | tf_op jit(solution)/shard_map/psum | solution.py:90
  496.6 60.6 %copy-start.91 = (f32[512]{0:T(512)}, f32[512]{0:T(512)S(1)}, u32[]{:S(2)}) copy-start(f32[512]{0:T(512)S(1)} %negate_multiply_fusion.4) | copy-start | bytes 6148
  502.5 183.9 %all-reduce.25.cloned.1.call-start = ((), (), s32[]{:S(2)}) async-start(), calls=%async_computation.19 | async-start | bytes 2097152 | tf_op jit(solution)/shard_map/psum | solution.py:90
  571.6 60.4 %copy-start.4 = (f32[512,256]{1,0:T(8,128)}, f32[512,256]{1,0:T(8,128)S(1)}, u32[]{:S(2)}) copy-start(f32[512,256]{1,0:T(8,128)S(1)} %get-tuple-element.498) | copy-start | bytes 1572868
  628.7 3.2 collective-permute-start.1
  635.4 116.3 %reduce-scatter.23.cloned.1.call-start = ((), (), s32[]{:S(2)}) async-start(), calls=%async_computation.20 | async-start | bytes 1310720 | tf_op jit(solution)/shard_map/reduce_scatter | solution.py:357
  727.5 51.4 %copy-start.113 = (bf16[3,1024,256]{2,1,0:T(8,128)(2,1)S(1)}, bf16[3,1024,256]{2,1,0:T(8,128)(2,1)}, u32[]{:S(2)}) copy-start(bf16[3,1024,256]{2,1,0:T(8,128)(2,1)} %all-gather.15.cloned.1.call-done) | copy-start | bytes 4718596
  727.5 51.4 %reduce-scatter.25.cloned.1.call-start = ((), (), s32[]{:S(2)}) async-start(), calls=%async_computation.21 | async-start | bytes 1310720 | tf_op jit(solution)/shard_map/reduce_scatter | solution.py:358
  728.1 106.0 %all-reduce.27.cloned.1.call-start = ((), (), s32[]{:S(2)}) async-start(), calls=%async_computation.22 | async-start | bytes 2097152 | tf_op jit(solution)/shard_map/psum | solution.py:488
  728.2 53.7 %copy-start.48 = (bf16[512,256]{0,1:T(8,128)(2,1)}, bf16[512,256]{0,1:T(8,128)(2,1)S(1)}, u32[]{:S(2)}) copy-start(bf16[512,256]{0,1:T(8,128)(2,1)S(1)} %copy.51) | copy-start | bytes 786436
  782.0 88.9 %reduce-scatter.39.cloned.1.call-start = ((), (), s32[]{:S(2)}) async-start(), calls=%async_computation.34 | async-start | bytes 589824
  787.4 122.7 %reduce-scatter.37.cloned.1.call-start = ((), (), s32[]{:S(2)}) async-start(), calls=%async_computation.33 | async-start | bytes 1179648
  796.6 151.2 %reduce-scatter.35.cloned.1.call-start = ((), (), s32[]{:S(2)}) async-start(), calls=%async_computation.32 | async-start | bytes 589824
  798.2 194.1 %reduce-scatter.41.cloned.1.call-start = ((), (), s32[]{:S(2)}) async-start(), calls=%async_computation.35 | async-start | bytes 2359296
  804.8 231.9 %reduce-scatter.29.cloned.1.call-start = ((), (), s32[]{:S(2)}) async-start(), calls=%async_computation.25 | async-start | bytes 2359296 | tf_op jit(solution)/shard_map/reduce_scatter | solution.py:75
  810.4 23.6 %copy-start.7 = (bf16[1,512,1024]{2,1,0:T(8,128)(2,1)S(1)}, bf16[1,512,1024]{2,1,0:T(8,128)(2,1)}, u32[]{:S(2)}) copy-start(bf16[1,512,1024]{2,1,0:T(8,128)(2,1)} %param.80) | copy-start | bytes 3145732
  810.4 23.6 %copy-start.14 = (bf16[512,1024]{1,0:T(8,128)(2,1)S(1)}, bf16[512,1024]{1,0:T(8,128)(2,1)}, u32[]{:S(2)}) copy-start(bf16[512,1024]{1,0:T(8,128)(2,1)} %all-reduce.15.cloned.1.call-done) | copy-start | bytes 3145732
  810.5 25.6 %copy-start.61 = (f32[512]{0:T(512)S(1)}, f32[512]{0:T(512)}, u32[]{:S(2)}) copy-start(f32[512]{0:T(512)} %copy-done.60) | copy-start | bytes 6148
  810.5 25.6 %copy-start.63 = (f32[512]{0:T(512)S(1)}, f32[512]{0:T(512)}, u32[]{:S(2)}) copy-start(f32[512]{0:T(512)} %copy-done.62) | copy-start | bytes 6148
  810.5 280.5 %all-reduce.29.cloned.1.call-start = ((), (), s32[]{:S(2)}) async-start(), calls=%async_computation.23 | async-start | bytes 2097152 | tf_op jit(solution)/shard_map/psum | solution.py:90
  845.0 286.9 %reduce-scatter.33.cloned.1.call-start = ((), (), s32[]{:S(2)}) async-start(), calls=%async_computation.31 | async-start | bytes 1769472
  854.8 321.5 %reduce-scatter.31.cloned.1.call-start = ((), (), s32[]{:S(2)}) async-start(), calls=%async_computation.30 | async-start | bytes 2359296
  864.1 356.4 %reduce-scatter.27.cloned.1.call-start = ((), (), s32[]{:S(2)}) async-start(), calls=%async_computation.24 | async-start | bytes 2359296 | tf_op jit(solution)/shard_map/reduce_scatter | solution.py:75
  992.2 100.6 %copy-start.57 = (f32[512]{0:T(512)S(1)}, f32[512]{0:T(512)}, u32[]{:S(2)}) copy-start(f32[512]{0:T(512)} %copy-done.56) | copy-start | bytes 6148
  1038.4 55.6 %copy-start.66 = (f32[1024]{0:T(1024)S(1)}, f32[1024]{0:T(1024)}, u32[]{:S(2)}) copy-start(f32[1024]{0:T(1024)} %get-tuple-element.446) | copy-start | bytes 12292
  1038.4 55.7 %copy-start.67 = (f32[1024]{0:T(1024)S(1)}, f32[1024]{0:T(1024)}, u32[]{:S(2)}) copy-start(f32[1024]{0:T(1024)} %get-tuple-element.440) | copy-start | bytes 12292
  1038.4 55.7 %copy-start.108 = (f32[256]{0:T(256)S(1)}, f32[256]{0:T(256)}, u32[]{:S(2)}) copy-start(f32[256]{0:T(256)} %get-tuple-element.480) | copy-start | bytes 3076
  (86 other events, 275.6 us)
Sparse Core Ops, SparseCore 0:
  10.5 30.4 all-gather.20
  43.5 28.0 all-gather.12
  76.2 51.8 all-reduce.14
  130.5 24.8 all-gather.14
  159.1 17.1 all-gather.24
  178.3 16.6 all-gather.22
  215.0 51.8 all-reduce.16
  269.5 22.6 all-gather.16
  324.9 49.1 all-reduce.18
  376.4 27.0 all-gather.26
  405.9 28.0 all-gather.18
  438.6 51.8 all-reduce.20
  502.6 51.1 all-reduce.22
  635.6 50.7 all-reduce.24
  727.6 24.0 reduce-scatter.22
  754.1 24.7 reduce-scatter.24
  782.1 51.8 all-reduce.26
  837.5 33.3 reduce-scatter.38
  874.1 35.9 reduce-scatter.36
  913.6 34.1 reduce-scatter.34
  951.1 41.1 reduce-scatter.40
  995.5 41.0 reduce-scatter.28
  1039.0 51.8 all-reduce.28
  1094.1 37.7 reduce-scatter.32
  1135.1 41.0 reduce-scatter.30
  1179.4 41.1 reduce-scatter.26

commit v2 on v1

--- a/solution.py
+++ b/solution.py
@@ -1,4 +1,3 @@
-from functools import partial
 import math
 
 import jax
@@ -13,9 +12,7 @@
 LEFT = 64
 RIGHT = 8
 
-
 epsilon = 1e-05
-highest = lax.Precision.HIGHEST
 
 
 def shifted_2(value, axis, steps):
@@ -47,11 +44,6 @@
     return centred * lax.rsqrt(variance + epsilon) * gain_vec
 
 
-def norm_back(rows_in, gain_vec, upstream):
-    unused, pullback = jax.vjp(layer_norm, rows_in, gain_vec)
-    return pullback(upstream)
-
-
 def gate_unit(unit_half, gate_half):
     return unit_half * jax.nn.sigmoid(gate_half)
 
@@ -63,14 +55,6 @@
     )
 
 
-def weights_back(weight_in, weight_out):
-    result_pair = (
-        lax.all_gather(weight_in.astype(jnp.bfloat16), ("clips", "context"), axis=1, tiled=True),
-        lax.all_gather(weight_out.astype(jnp.bfloat16), ("clips", "context"), axis=1, tiled=True),
-    )
-    return result_pair
-
-
 def scatter_sum(grad, axis):
     summed = lax.psum_scatter(
         grad.astype(jnp.bfloat16), ("clips", "context"), scatter_dimension=axis, tiled=True
@@ -82,31 +66,222 @@
     return (scatter_sum(grad_in, 1), scatter_sum(grad_out, 1))
 
 
-def branch_total(partial_sum):
-    return lax.psum(partial_sum.astype(jnp.bfloat16), "tensor").astype(jnp.float32)
-
-
-def input_total(partial_sum):
-    return lax.psum(partial_sum.astype(jnp.bfloat16), "tensor").astype(jnp.float32)
-
-
-def ffn_forward(rows_in, gain_vec, weight_in, weight_out):
-    normed = layer_norm(rows_in, gain_vec).astype(jnp.bfloat16)
+MESH_ID = pl.DeviceIdType.MESH
+CHUNKS = 32
+LAG = 5
+
+
+def line_sum(axis, partial_ref, acc_ref, from_end, from_mid, total_ref, send_sem, recv_sem, finish):
+    at = lax.axis_index(axis)
+    low = at < 2
+    end = jnp.where(low, 0, 3)
+    mid = jnp.where(low, 1, 2)
+    other = jnp.where(low, 2, 1)
+    is_mid = at == mid
+    size = partial_ref.shape[0] // CHUNKS
+
+    def rows(chunk):
+        return pl.ds(pl.multiple_of(chunk * size, size), size)
+
+    def hop(stage, chunk, source, target, device):
+        return pltpu.make_async_remote_copy(
+            src_ref=source.at[rows(chunk)],
+            dst_ref=target.at[rows(chunk)],
+            send_sem=send_sem.at[stage, chunk],
+            recv_sem=recv_sem.at[stage, chunk],
+            device_id={axis: device},
+            device_id_type=MESH_ID,
+        )
+
+    inward = lambda chunk: hop(0, chunk, partial_ref, from_end, mid)
+    across = lambda chunk: hop(1, chunk, acc_ref, from_mid, other)
+    outward = lambda chunk: hop(2, chunk, total_ref, total_ref, end)
+    barrier = pltpu.get_barrier_semaphore()
+
+    def loop(low, high, body):
+        def step(chunk, carry):
+            body(chunk)
+            return carry
+        lax.fori_loop(low, high, step, 0)
+
+    @pl.when(is_mid)
+    def _():
+        pl.semaphore_signal(barrier, inc=1, device_id={axis: end}, device_id_type=MESH_ID)
+        pl.semaphore_signal(barrier, inc=1, device_id={axis: other}, device_id_type=MESH_ID)
+        pl.semaphore_wait(barrier, 2)
+
+        def first(chunk):
+            inward(chunk).wait_recv()
+            here = rows(chunk)
+            acc_ref[here] = (partial_ref[here].astype(jnp.float32) + from_end[here].astype(jnp.float32)).astype(acc_ref.dtype)
+            across(chunk).start()
+
+        def second(chunk):
+            across(chunk).wait_recv()
+            here = rows(chunk)
+            total_ref[here] = (acc_ref[here].astype(jnp.float32) + from_mid[here].astype(jnp.float32)).astype(total_ref.dtype)
+            outward(chunk).start()
+            finish(here)
+
+        def both(chunk):
+            first(chunk)
+            second(chunk - LAG)
+
+        loop(0, LAG, first)
+        loop(LAG, CHUNKS, both)
+        loop(CHUNKS - LAG, CHUNKS, second)
+
+        def drain(chunk):
+            across(chunk).wait_send()
+            outward(chunk).wait_send()
+
+        loop(0, CHUNKS, drain)
+
+    @pl.when(jnp.logical_not(is_mid))
+    def _():
+        pl.semaphore_signal(barrier, inc=1, device_id={axis: mid}, device_id_type=MESH_ID)
+        pl.semaphore_wait(barrier, 1)
+        loop(0, CHUNKS, lambda chunk: inward(chunk).start())
+
+        def receive(chunk):
+            outward(chunk).wait_recv()
+            finish(rows(chunk))
+
+        loop(0, CHUNKS, receive)
+        loop(0, CHUNKS, lambda chunk: inward(chunk).wait_send())
+
+
+def unit_rows(rows_in):
+    mean = jnp.mean(rows_in, axis=-1, keepdims=True)
+    centred = rows_in - mean
+    variance = jnp.mean(centred * centred, axis=-1, keepdims=True)
+    inverse = lax.rsqrt(variance + epsilon)
+    return centred * inverse, inverse
+
+
+def rows_back(unit, inverse, scaled):
+    return inverse * (
+        scaled
+        - jnp.mean(scaled, axis=-1, keepdims=True)
+        - unit * jnp.mean(scaled * unit, axis=-1, keepdims=True)
+    )
+
+
+def gather_eight(value):
+    total = value[:8]
+    for at in range(8, value.shape[0], 8):
+        total = total + value[at : at + 8]
+    return total
+
+
+def sum_call(body, name, cid, partial, operands, outs):
+    rows, width = partial.shape
+    chunk_shape = pltpu.VMEM((rows, width), jnp.bfloat16)
+    vmem = pl.BlockSpec(memory_space=pltpu.VMEM)
+
+    def kernel(partial_ref, *refs):
+        ins, results = refs[: len(operands)], refs[len(operands) : len(operands) + len(outs)]
+        acc, from_end, from_mid, total, send_sem, recv_sem = refs[len(operands) + len(outs) :]
+        start, finish = body(total, ins, results)
+        start()
+        line_sum("tensor", partial_ref, acc, from_end, from_mid, total, send_sem, recv_sem, finish)
+
+    return pl.pallas_call(
+        kernel,
+        out_shape=tuple(jax.ShapeDtypeStruct(shape, kind) for shape, kind in outs),
+        in_specs=[vmem] * (1 + len(operands)),
+        out_specs=(vmem,) * len(outs),
+        scratch_shapes=[chunk_shape] * 4
+        + [pltpu.SemaphoreType.DMA((3, CHUNKS)), pltpu.SemaphoreType.DMA((3, CHUNKS))],
+        compiler_params=pltpu.CompilerParams(collective_id=cid, has_side_effects=True, vmem_limit_bytes=40 << 20),
+        cost_estimate=pl.CostEstimate(flops=60_000_000_000, bytes_accessed=100_000_000, transcendentals=0),
+        name=name,
+    )(partial, *operands)
+
+
+def forward_sum(cid, partial, rows_in, gain, scale):
+    def body(total, ins, results):
+        x_ref, gain_ref = ins
+        x_out, a_out = results
+
+        def finish(here):
+            x = x_ref[here].astype(jnp.float32) + scale * total[here].astype(jnp.float32)
+            x_out[here] = x
+            a_out[here] = (unit_rows(x)[0] * gain_ref[...]).astype(a_out.dtype)
+
+        return lambda: None, finish
+
+    shape = partial.shape
+    return sum_call(body, f"forward_sum_{cid}", cid, partial, (rows_in, gain.reshape(1, -1)), ((shape, jnp.float32), (shape, jnp.bfloat16)))
+
+
+def turn_sum(cid, partial, rows_in, gain, cotangent):
+    def body(total, ins, results):
+        x_ref, gain_ref, cot_ref = ins
+        out_ref, d_ref, half_ref, gain_grad_ref = results
+
+        def start():
+            gain_grad_ref[...] = jnp.zeros_like(gain_grad_ref)
+
+        def finish(here):
+            x = x_ref[here] + 0.5 * total[here].astype(jnp.float32)
+            unit, inverse = unit_rows(x)
+            out_ref[here] = (unit * gain_ref[...]).astype(out_ref.dtype)
+            upstream = cot_ref[here].astype(jnp.float32)
+            d = rows_back(unit, inverse, upstream * gain_ref[...])
+            d_ref[here] = d
+            half_ref[here] = (0.5 * d).astype(half_ref.dtype)
+            gain_grad_ref[...] += gather_eight(upstream * unit)
+
+        return start, finish
+
+    shape = partial.shape
+    out, d, half, gain_grad = sum_call(
+        body, f"turn_sum_{cid}", cid, partial, (rows_in, gain.reshape(1, -1), cotangent),
+        ((shape, jnp.bfloat16), (shape, jnp.float32), (shape, jnp.bfloat16), ((8, shape[1]), jnp.float32)),
+    )
+    return out, d, half, jnp.sum(gain_grad, axis=0)
+
+
+def backward_sum(cid, partial, rows_in, gain, upstream, scale):
+    def body(total, ins, results):
+        x_ref, gain_ref, up_ref = ins
+        d_ref, half_ref, gain_grad_ref = results
+
+        def start():
+            gain_grad_ref[...] = jnp.zeros_like(gain_grad_ref)
+
+        def finish(here):
+            unit, inverse = unit_rows(x_ref[here].astype(jnp.float32))
+            normed_grad = total[here].astype(jnp.float32)
+            d = up_ref[here] + rows_back(unit, inverse, normed_grad * gain_ref[...])
+            d_ref[here] = d
+            half_ref[here] = (scale * d).astype(half_ref.dtype)
+            gain_grad_ref[...] += gather_eight(normed_grad * unit)
+
+        return start, finish
+
+    shape = partial.shape
+    d, half, gain_grad = sum_call(
+        body, f"backward_sum_{cid}", cid, partial, (rows_in, gain.reshape(1, -1), upstream),
+        ((shape, jnp.float32), (shape, jnp.bfloat16), ((8, shape[1]), jnp.float32)),
+    )
+    return d, half, jnp.sum(gain_grad, axis=0)
+
+
+def feed(normed, weight_in, weight_out):
     hidden = dot_rows(normed, weight_in)
     active = jax.nn.silu(hidden).astype(jnp.bfloat16)
-    return (branch_total(dot_rows(active, weight_out)), (normed, hidden, active))
-
-
-def ffn_backward(rows_in, gain_vec, weight_in, weight_out, saved, upstream):
+    return dot_rows(active, weight_out).astype(jnp.bfloat16), (normed, hidden, active)
+
+
+def feed_back(weight_in, weight_out, saved, branch_grad):
     normed, hidden, active = saved
-    branch_grad = (0.5 * upstream).astype(jnp.bfloat16)
     grad_out = dot_inner(active, branch_grad)
     unused, pullback = jax.vjp(jax.nn.silu, hidden)
     hidden_grad = pullback(dot_outer(branch_grad, weight_out))[0].astype(jnp.bfloat16)
     grad_in = dot_inner(normed, hidden_grad)
-    normed_grad = input_total(dot_outer(hidden_grad, weight_in))
-    rows_grad, gain_grad = norm_back(rows_in, gain_vec, normed_grad)
-    return (upstream + rows_grad, gain_grad, grad_in, grad_out)
+    return dot_outer(hidden_grad, weight_in).astype(jnp.bfloat16), grad_in, grad_out
 
 
 QB = 128
@@ -328,8 +503,7 @@
     return dq, dkt, dvt, table
 
 
-def attend_forward(rows_in, gain_vec, weight_in, weight_out, relative, position):
-    normed = layer_norm(rows_in, gain_vec).astype(jnp.bfloat16)
+def attend_forward(normed, weight_in, weight_out, relative, position):
     projected = jnp.einsum(
         "td,kde->kte", normed, weight_in, preferred_element_type=jnp.float32
     ).astype(jnp.bfloat16)
@@ -341,14 +515,13 @@
     span = span_table(relative)
     mixed, log_total = attention_forward(position, queries, key_rows, value_rows, span)
     return (
-        branch_total(dot_rows(mixed, weight_out)),
+        dot_rows(mixed, weight_out).astype(jnp.bfloat16),
         (normed, queries, key_rows, value_rows, log_total, mixed, span),
     )
 
 
-def attend_backward(weight_in, weight_out, relative, position, saved, upstream):
+def attend_backward(weight_in, weight_out, position, saved, branch_grad):
     normed, queries, key_rows, value_rows, log_total, mixed, span = saved
-    branch_grad = upstream.astype(jnp.bfloat16)
     grad_out = dot_inner(mixed, branch_grad)
     mixed_grad = dot_outer(branch_grad, weight_out).astype(jnp.bfloat16)
     query_grad, key_grad, value_grad, table_grad = attention_backward(
@@ -359,11 +532,10 @@
     stacked = jnp.stack([query_grad, key_grad.T, value_grad.T])
     grad_in = jnp.einsum("td,kte->kde", normed, stacked, preferred_element_type=jnp.float32)
     partial_sum = jnp.einsum("kte,kde->td", stacked, weight_in, preferred_element_type=jnp.float32)
-    return (partial_sum, table_grad, grad_in, grad_out)
-
-
-def conv_forward(rows_in, gain_vec, weight_in, weight_out, depthwise, gain_middle):
-    normed = layer_norm(rows_in, gain_vec).astype(jnp.bfloat16)
+    return (partial_sum.astype(jnp.bfloat16), table_grad, grad_in, grad_out)
+
+
+def conv_forward(normed, weight_in, weight_out, depthwise, gain_middle):
     projected = jnp.einsum("td,kde->kte", normed, weight_in, preferred_element_type=jnp.float32)
     gated = gate_unit(projected[0], projected[1])
     rows_here = gated.shape[0]
@@ -382,16 +554,15 @@
     shaped = scaled * gain_middle
     active = jax.nn.silu(shaped).astype(jnp.bfloat16)
     return (
-        branch_total(dot_rows(active, weight_out)),
+        dot_rows(active, weight_out).astype(jnp.bfloat16),
         (normed, projected, padded, scaled, inverse, shaped, active),
     )
 
 
-def conv_backward(weight_in, weight_out, depthwise, gain_middle, saved, upstream):
+def conv_backward(weight_in, weight_out, depthwise, gain_middle, saved, branch_grad):
     normed, projected, padded, scaled, inverse, shaped, active = saved
-    rows_here, channels = scaled.shape
+    rows_here = scaled.shape[0]
     reach_rows = depthwise.shape[0] - 1
-    branch_grad = upstream.astype(jnp.bfloat16)
     grad_out = dot_inner(active, branch_grad)
     unused, pullback = jax.vjp(jax.nn.silu, shaped)
     shaped_grad = pullback(dot_outer(branch_grad, weight_out))[0]
@@ -403,27 +574,23 @@
     mixed_grad = inverse[:, None] * (
         scaled_grad - first_sum[:, None] / D - scaled * (second_sum[:, None] / D)
     )
-    padded_grad = jnp.zeros((rows_here + reach_rows, channels), jnp.float32)
-    for offset in range(reach_rows + 1):
-        padded_grad = padded_grad.at[offset : offset + rows_here].add(
-            depthwise[offset] * mixed_grad
-        )
+    next_rows = shifted_2(mixed_grad[:reach_rows], "context", -1)
+    padded_grad = jnp.concatenate([mixed_grad, next_rows], axis=0)
+    gated_grad = depthwise[reach_rows] * padded_grad[0:rows_here]
+    for offset in range(1, reach_rows + 1):
+        gated_grad = gated_grad + depthwise[reach_rows - offset] * padded_grad[offset : offset + rows_here]
     depth_grad = jnp.stack(
         [
             jnp.sum(padded[offset : offset + rows_here] * mixed_grad, axis=0)
             for offset in range(reach_rows + 1)
         ]
     )
-    back_rows = shifted_2(padded_grad[:reach_rows], "context", -1)
-    gated_grad = padded_grad[reach_rows:] + jnp.pad(
-        back_rows, ((rows_here - reach_rows, 0), (0, 0))
-    )
     unused, pullback = jax.vjp(gate_unit, projected[0], projected[1])
     unit_grad, gate_grad = pullback(gated_grad)
     stacked = jnp.stack([unit_grad, gate_grad]).astype(jnp.bfloat16)
     grad_in = jnp.einsum("td,kte->kde", normed, stacked, preferred_element_type=jnp.float32)
     partial_sum = jnp.einsum("kte,kde->td", stacked, weight_in, preferred_element_type=jnp.float32)
-    return (partial_sum, grad_in, grad_out, middle_grad, depth_grad)
+    return (partial_sum.astype(jnp.bfloat16), grad_in, grad_out, middle_grad, depth_grad)
 
 
 def local(
@@ -447,55 +614,36 @@
     cotangent,
 ):
     position = lax.axis_index("context")
-    start_rows = inputs[0].astype(jnp.float32)
-    first_pair = fetch(first_in[None], first_out)
-    branch_out, first_saved = ffn_forward(start_rows, gain_first, first_pair[0][0], first_pair[1])
-    after_first = start_rows + 0.5 * branch_out
-    attend_pair = fetch(attend_in, attend_out)
-    branch_out, attend_saved = attend_forward(
-        after_first, gain_attend, attend_pair[0], attend_pair[1], relative, position
-    )
-    after_attend = after_first + branch_out
-    convolve_pair = fetch(convolve_in, convolve_out)
-    branch_out, convolve_saved = conv_forward(
-        after_attend, gain_convolve, convolve_pair[0], convolve_pair[1], depthwise, gain_middle
-    )
-    after_convolve = after_attend + branch_out
-    second_pair = fetch(second_in[None], second_out)
-    branch_out, second_saved = ffn_forward(
-        after_convolve, gain_second, second_pair[0][0], second_pair[1]
-    )
-    after_second = after_convolve + 0.5 * branch_out
-    final_out, pullback = jax.vjp(layer_norm, after_second, gain_final)
-    upstream, grad_final = pullback(cotangent[0].astype(jnp.float32))
-    second_pair = weights_back(second_in[None], second_out)
-    upstream, grad_gain_second, grad_in, grad_out = ffn_backward(
-        after_convolve, gain_second, second_pair[0][0], second_pair[1], second_saved, upstream
-    )
+    start_rows = inputs[0]
+    first_in, first_out = fetch(first_in[None], first_out)
+    attend_in, attend_out = fetch(attend_in, attend_out)
+    convolve_in, convolve_out = fetch(convolve_in, convolve_out)
+    second_in, second_out = fetch(second_in[None], second_out)
+    first_in, second_in = first_in[0], second_in[0]
+    normed = layer_norm(start_rows.astype(jnp.float32), gain_first).astype(jnp.bfloat16)
+    branch, first_saved = feed(normed, first_in, first_out)
+    after_first, normed = forward_sum(1, branch, start_rows, gain_attend, 0.5)
+    branch, attend_saved = attend_forward(normed, attend_in, attend_out, relative, position)
+    after_attend, normed = forward_sum(2, branch, after_first, gain_convolve, 1.0)
+    branch, convolve_saved = conv_forward(normed, convolve_in, convolve_out, depthwise, gain_middle)
+    after_convolve, normed = forward_sum(3, branch, after_attend, gain_second, 1.0)
+    branch, second_saved = feed(normed, second_in, second_out)
+    final_out, upstream, branch_grad, grad_final = turn_sum(4, branch, after_convolve, gain_final, cotangent[0])
+    branch, grad_in, grad_out = feed_back(second_in, second_out, second_saved, branch_grad)
     second_grads = send_grads(grad_in[None], grad_out)
-    convolve_pair = weights_back(convolve_in, convolve_out)
-    partial_sum, grad_in, grad_out, grad_middle, grad_depth = conv_backward(
-        convolve_pair[0], convolve_pair[1], depthwise, gain_middle, convolve_saved, upstream
-    )
-    rows_grad, grad_gain_convolve = norm_back(after_attend, gain_convolve, input_total(partial_sum))
-    upstream = upstream + rows_grad
+    upstream, branch_grad, grad_gain_second = backward_sum(5, branch, after_convolve, gain_second, upstream, 1.0)
+    branch, grad_in, grad_out, grad_middle, grad_depth = conv_backward(
+        convolve_in, convolve_out, depthwise, gain_middle, convolve_saved, branch_grad
+    )
     convolve_grads = send_grads(grad_in, grad_out)
-    attend_pair = weights_back(attend_in, attend_out)
-    partial_sum, table_grad, grad_in, grad_out = attend_backward(
-        attend_pair[0], attend_pair[1], relative, position, attend_saved, upstream
-    )
-    normed_grad, table_grad = (
-        lax.psum(partial_sum.astype(jnp.bfloat16), "tensor").astype(jnp.float32),
-        lax.psum(table_grad.astype(jnp.bfloat16), "tensor").astype(jnp.float32),
-    )
-    rows_grad, grad_gain_attend = norm_back(after_first, gain_attend, normed_grad)
-    upstream = upstream + rows_grad
+    upstream, branch_grad, grad_gain_convolve = backward_sum(6, branch, after_attend, gain_convolve, upstream, 1.0)
+    branch, table_grad, grad_in, grad_out = attend_backward(attend_in, attend_out, position, attend_saved, branch_grad)
     attend_grads = send_grads(grad_in, grad_out)
-    first_pair = weights_back(first_in[None], first_out)
-    upstream, grad_gain_first, grad_in, grad_out = ffn_backward(
-        start_rows, gain_first, first_pair[0][0], first_pair[1], first_saved, upstream
-    )
+    upstream, branch_grad, grad_gain_attend = backward_sum(7, branch, after_first, gain_attend, upstream, 0.5)
+    branch, grad_in, grad_out = feed_back(first_in, first_out, first_saved, branch_grad)
     first_grads = send_grads(grad_in[None], grad_out)
+    upstream, branch_grad, grad_gain_first = backward_sum(8, branch, start_rows, gain_first, upstream, 1.0)
+    table_grad = lax.psum(table_grad, "tensor")
     smalls = lax.psum(
         (
             grad_gain_first,
@@ -510,7 +658,7 @@
         ("clips", "context"),
     )
     return (
-        final_out.astype(jnp.bfloat16)[None],
+        final_out[None],
         upstream[None],
         smalls[0],
         first_grads[0][0],

time: 1240 us -> 911 us (0.73)
  waiting for transfers between devices: 840 us -> 356 us
  Pallas kernels: 47.1 us -> 311 us
  local copies, waits for them, and re-layouts: 107 us -> 64.3 us
  other arithmetic: 59 us -> 30.7 us
  blocking collectives: 88.7 us -> 62.9 us
    psum x8 -> x1, waiting for transfers between devices: 376 us -> 56.4 us  [local(): lax.psum((grad_gain_first, grad_gain_attend, table_grad, grad_gain_convol...]
    pallas_call x0 -> x8, Pallas kernels: none -> 264 us  [sum_call(): pl.pallas_call(kernel, out_shape=tuple((jax.ShapeDtypeStruct(shape, kind)...]
    all_gather x4, waiting for transfers between devices: 103 us -> 28.5 us  [fetch(): lax.all_gather(weight_in.astype(jnp.bfloat16), ('clips', 'context'), axis...]
    scatter-add x27 -> x0, local copies, waits for them, and re-layouts: 54.1 us -> none  [conv_backward(): padded_grad.at[offset:offset + rows_here]]
    unnamed x32 -> x25, waiting for transfers between devices: 148 us -> 119 us
    psum x2 -> x1, blocking collectives: 44.9 us -> 18.7 us  [local(): table_grad = lax.psum(table_grad, 'tensor')]
    all_gather x2, waiting for transfers between devices: 52.7 us -> 27.6 us  [fetch(): lax.all_gather(weight_out.astype(jnp.bfloat16), ('clips', 'context'), axi...]
    reduce_scatter x1, waiting for transfers between devices: 23.4 us -> 0.02 us  [attend_backward(): lax.psum_scatter(key_grad, 'context', scatter_dimension=1, tiled=True)]
  transfers between devices with their start and end apart: 28 -> 21, of which waited for: 27 -> 12; matrix products, arithmetic and copies ran while one was open for 8% -> 10% of each run, Pallas kernels for 0% -> 21%
where the time goes in v2:
time: 911 us; the launch traced here: 901 us
  waiting for transfers between devices  356 us (39%)
  Pallas kernels  311 us (34%)
  local copies, waits for them, and re-layouts  64.3 us (7%)
  blocking collectives  62.9 us (7%)
  matrix products  55.5 us (6%)
  other arithmetic  30.7 us (3%)
  between operations  16.8 us (2%)
    pallas_call x8, Pallas kernels, sum_call(): pl.pallas_call(kernel, out_shape=tuple((jax.ShapeDtypeStruct(shape, kind)...  264 us
    unnamed x25, waiting for transfers between devices  119 us
    reduce_scatter x2, waiting for transfers between devices, scatter_sum(): lax.psum_scatter(grad.astype(jnp.bfloat16), ('clips', 'context'), scatter...  77 us
    unnamed x379, local copies, waits for them, and re-layouts  59.8 us
    psum x1, waiting for transfers between devices, local(): lax.psum((grad_gain_first, grad_gain_attend, table_grad, grad_gain_convol...  56.4 us
    pallas_call x1, Pallas kernels, attention_backward(): pl.pallas_call(backward_kernel, out_shape=(jax.ShapeDtypeStruct((rows, wi...  31.2 us
    all_gather x4, waiting for transfers between devices, fetch(): lax.all_gather(weight_in.astype(jnp.bfloat16), ('clips', 'context'), axis...  28.5 us
    all_gather x2, waiting for transfers between devices, fetch(): lax.all_gather(weight_out.astype(jnp.bfloat16), ('clips', 'context'), axi...  27.6 us
  transfers between devices with their start and end apart: 21, of which 12 were waited for; matrix products, arithmetic and copies ran while one was open for 10% of the time, Pallas kernels for 21%

profile of v2, /device:TPU:0, one launch (start us, length us, event | category | flops | bytes accessed | tf_op | source)
XLA Modules:
  0.0 900.9 jit_solution(1744432061682274069)
XLA Ops:
  7.3 1.9 convert_element_type.158
  9.2 1.8 convert_element_type.161
  12.5 28.5 %all-gather.21.cloned.1.call-done = bf16[1024,1024]{1,0:T(8,128)(2,1)} async-done(((bf16[128,1024]{1,0:T(8,128)(2,1)}), bf16[1024,1024]{1,0:T(8,128)(2,1)}) %all-gather.21.cloned.1.call-update) | async-done | bytes 2097168 | tf_op jit(solution)/shard_map/all_gather | solution.py:53
  41.0 2.9 fusion.15
  44.0 27.6 %all-gather.13.cloned.1.call-done = bf16[1024,1024]{1,0:T(8,128)(2,1)} async-done(((bf16[1024,128]{1,0:T(8,128)(2,1)}), bf16[1024,1024]{1,0:T(8,128)(2,1)}) %all-gather.13.cloned.1.call-update) | async-done | bytes 2097168 | tf_op jit(solution)/shard_map/all_gather | solution.py:54
  71.6 2.9 convolution_convert_fusion.8.partial_ref
  74.6 34.5 %forward_sum_1.1 = (f32[512,1024]{1,0:T(8,128)S(1)}, bf16[512,1024]{1,0:T(8,128)(2,1)S(1)}) custom-call(bf16[512,1024]{1,0:T(8,128)(2,1)S(1)} %convolution_convert_fusion.8.partial_ref, bf16[512,1024]{1,0:T(8,128)(2,1)S(1)} %bitcast.207, f32[1,1024]{1,0:T(1,128)S(1)} %bitcast.225), custom_call_target="tpu_custom_call" | custom-call | flops 60000002048 | bytes 100000000 | tf_op jit(solution)/shard_map/forward_sum_1/pallas_call | solution.py:189
  109.0 1.3 copy-done.39
  111.3 2.4 fusion.13
  118.8 12.3 %all_gather.35 = bf16[256,1024]{1,0:T(8,128)(2,1)S(1)} all-gather(bf16[256,128]{1,0:T(8,128)(2,1)S(1)} %convert_element_type.167), channel_id=1, replica_groups=mesh['clips'=2,'context'=4,'tensor'=4] {'clips','context'}, dimensions={1}, use_global_device_ids=true | all-gather | bytes 589824 | tf_op jit(solution)/shard_map/all_gather | solution.py:54
  132.2 18.4 %all-gather.23.cloned.1.call-done = bf16[1,2048,256]{2,1,0:T(8,128)(2,1)} async-done(((bf16[1,512,256]{2,1,0:T(8,128)(2,1)}), bf16[1,2048,256]{2,1,0:T(8,128)(2,1)}) %all-gather.23.cloned.1.call-update) | async-done | bytes 1048592 | tf_op jit(solution)/shard_map/all_gather | solution.py:511
  153.1 16.0 %attention_forward.1 = (bf16[512,256]{1,0:T(8,128)(2,1)S(1)}, f32[512,256]{1,0:T(8,128)S(1)}) custom-call(s32[1]{0:T(128)} %bitcast.1.pos_ref, bf16[512,256]{1,0:T(8,128)(2,1)S(1)} %get-tuple-element.166.q_ref, bf16[2048,256]{1,0:T(8,128)(2,1)S(1)} %bitcast.218, bf16[2048,256]{1,0:T(8,128)(2,1)S(1)} %bitcast.216, ...), custom_call_target="tpu_custom_call" | custom-call | flops 2147483648 | bytes 2621440 | tf_op jit(solution)/shard_map/attention_forward/pallas_call | solution.py:355
  170.2 34.5 %forward_sum_2.1 = (f32[512,1024]{1,0:T(8,128)S(1)}, bf16[512,1024]{1,0:T(8,128)(2,1)S(1)}) custom-call(bf16[512,1024]{1,0:T(8,128)(2,1)S(1)} %convolution_convert_fusion.7.partial_ref, f32[512,1024]{1,0:T(8,128)S(1)} %copy-done.40, f32[1,1024]{1,0:T(1,128)S(1)} %bitcast.223), custom_call_target="tpu_custom_call" | custom-call | flops 60000002048 | bytes 100000000 | tf_op jit(solution)/shard_map/forward_sum_2/pallas_call | solution.py:189
  206.0 2.3 convolution_bitcast_fusion
  210.6 10.9 %all_gather.37 = bf16[256,1024]{1,0:T(8,128)(2,1)S(1)} all-gather(bf16[256,128]{1,0:T(8,128)(2,1)S(1)} %convert_element_type.171), channel_id=1, replica_groups=mesh['clips'=2,'context'=4,'tensor'=4] {'clips','context'}, dimensions={1}, use_global_device_ids=true | all-gather | bytes 589824 | tf_op jit(solution)/shard_map/all_gather | solution.py:54
  221.8 3.2 fusion.164
  225.0 10.0 %all-reduce.2 = (f32[512]{0:T(512)S(1)}, f32[512]{0:T(512)S(1)}) all-reduce(f32[512]{0:T(512)S(1)} %get-tuple-element.145, f32[512]{0:T(512)S(1)} %get-tuple-element.144), channel_id=1, replica_groups=mesh['clips'=2,'context'=4,'tensor'=4] {'tensor'}, use_global_device_ids=true, to_apply=%region_5.6 | all-reduce | flops 1024 | bytes 8192 | tf_op jit(solution)/shard_map/psum | solution.py:548
  235.6 1.7 copy-done.45
  237.3 32.1 %forward_sum_3.1 = (f32[512,1024]{1,0:T(8,128)S(1)}, bf16[512,1024]{1,0:T(8,128)(2,1)S(1)}) custom-call(bf16[512,1024]{1,0:T(8,128)(2,1)S(1)} %convolution_convert_fusion.6.partial_ref, f32[512,1024]{1,0:T(8,128)S(1)} %copy-done.45, f32[1,1024]{1,0:T(1,128)S(1)} %bitcast.221), custom_call_target="tpu_custom_call" | custom-call | flops 60000002048 | bytes 100000000 | tf_op jit(solution)/shard_map/forward_sum_3/pallas_call | solution.py:189
  269.5 1.3 copy-done.51
  271.7 4.3 fusion.169
  276.0 3.6 convolution_convert_fusion.5.partial_ref
  279.7 30.7 %turn_sum_4.1 = (bf16[512,1024]{1,0:T(8,128)(2,1)S(1)}, f32[512,1024]{1,0:T(8,128)S(1)}, bf16[512,1024]{1,0:T(8,128)(2,1)S(1)}, f32[8,1024]{1,0:T(8,128)S(1)}) custom-call(bf16[512,1024]{1,0:T(8,128)(2,1)S(1)} %convolution_convert_fusion.5.partial_ref, f32[512,1024]{1,0:T(8,128)S(1)} %copy-done.52, f32[1,1024]{1,0:T(1,128)S(1)} %bitcast.220, ...), custom_call_target="tpu_custom_call" | custom-call | flops 60000002048 | bytes 100000000 | tf_op jit(solution)/shard_map/turn_sum_4/pallas_call | solution.py:189
  311.4 1.7 fusion.7
  314.5 30.3 %backward_sum_5.1 = (f32[512,1024]{1,0:T(8,128)S(1)}, bf16[512,1024]{1,0:T(8,128)(2,1)S(1)}, f32[8,1024]{1,0:T(8,128)S(1)}) custom-call(bf16[512,1024]{1,0:T(8,128)(2,1)S(1)} %convolution_convert_fusion.4.partial_ref, f32[512,1024]{1,0:T(8,128)S(1)} %copy-done.52, f32[1,1024]{1,0:T(1,128)S(1)} %bitcast.222, f32[512,1024]{1,0:T(8,128)S(1)} %get-tuple-element.55.refs_2_), custom_call_target="tpu_custom_call" | custom-call | flops 60000002048 | bytes 100000000 | tf_op jit(solution)/shard_map/backward_sum_5/pallas_call | solution.py:189
  344.9 2.3 multiply_reduce_fusion
  347.5 11.0 %all-reduce.1 = (f32[512]{0:T(512)S(1)}, f32[512]{0:T(512)S(1)}) all-reduce(f32[512]{0:T(512)S(1)} %get-tuple-element.141, f32[512]{0:T(512)S(1)} %get-tuple-element.143), channel_id=1, replica_groups=mesh['clips'=2,'context'=4,'tensor'=4] {'tensor'}, use_global_device_ids=true, to_apply=%region_9.10 | all-reduce | flops 1024 | bytes 8192 | tf_op jit(solution)/shard_map/psum | solution.py:571
  358.5 2.6 multiply_reduce_fusion.2
  362.5 1.6 collective-permute-done.1
  364.4 3.6 fusion.155
  368.1 1.5 fusion.156
  370.8 33.0 %backward_sum_6.1 = (f32[512,1024]{1,0:T(8,128)S(1)}, bf16[512,1024]{1,0:T(8,128)(2,1)S(1)}, f32[8,1024]{1,0:T(8,128)S(1)}) custom-call(bf16[512,1024]{1,0:T(8,128)(2,1)S(1)} %bitcast_convert_fusion.1.partial_ref, f32[512,1024]{1,0:T(8,128)S(1)} %copy-done.46, f32[1,1024]{1,0:T(1,128)S(1)} %bitcast.224, f32[512,1024]{1,0:T(8,128)S(1)} %copy-done.50), custom_call_target="tpu_custom_call" | custom-call | flops 60000002048 | bytes 100000000 | tf_op jit(solution)/shard_map/backward_sum_6/pallas_call | solution.py:189
  404.4 1.5 copy-done.47
  412.6 31.2 %attention_backward.1 = (bf16[512,256]{1,0:T(8,128)(2,1)S(1)}, bf16[256,2048]{1,0:T(8,128)(2,1)}, bf16[256,2048]{1,0:T(8,128)(2,1)}, f32[64,512]{1,0:T(8,128)S(1)}, f32[8,128]{1,0:T(8,128)S(1)}) custom-call(s32[1]{0:T(128)} %bitcast.1.pos_ref, bf16[512,256]{1,0:T(8,128)(2,1)S(1)} %copy-done.6, bf16[256,512]{1,0:T(8,128)(2,1)S(1)} %copy.49.qt_ref, ...), custom_call_target="tpu_custom_call" | custom-call | flops 5368709120 | bytes 5242880 | tf_op jit(solution)/shard_map/attention_backward/pallas_call | solution.py:467
  444.8 2.7 convolution_convert_fusion.11
  447.5 2.1 copy.69
  451.2 2.1 fusion.12
  455.6 4.2 convolution_convert_fusion
  459.8 4.0 copy.71
  465.3 2.6 convert_bitcast_fusion
  468.1 26.7 %reduce-scatter.25.cloned.1.call-done = bf16[256,512]{1,0:T(8,128)(2,1)} async-done(((bf16[256,2048]{1,0:T(8,128)(2,1)}), bf16[256,512]{1,0:T(8,128)(2,1)}) %reduce-scatter.25.cloned.1.call-update) | async-done | bytes 262160 | tf_op jit(solution)/shard_map/reduce_scatter | solution.py:531
  494.9 3.2 fusion.11
  498.0 2.9 copy.63
  501.0 1.5 copy.73
  502.8 2.8 bitcast_convert_fusion.partial_ref
  505.8 33.8 %backward_sum_7.1 = (f32[512,1024]{1,0:T(8,128)S(1)}, bf16[512,1024]{1,0:T(8,128)(2,1)S(1)}, f32[8,1024]{1,0:T(8,128)S(1)}) custom-call(bf16[512,1024]{1,0:T(8,128)(2,1)S(1)} %bitcast_convert_fusion.partial_ref, f32[512,1024]{1,0:T(8,128)S(1)} %copy-done.41, f32[1,1024]{1,0:T(1,128)S(1)} %bitcast.226, f32[512,1024]{1,0:T(8,128)S(1)} %copy-done.48), custom_call_target="tpu_custom_call" | custom-call | flops 60000002048 | bytes 100000000 | tf_op jit(solution)/shard_map/backward_sum_7/pallas_call | solution.py:189
  539.6 1.7 fusion.10
  542.3 2.8 convert_bitcast_fusion.1
  548.6 2.5 stack.158
  552.4 18.7 %psum.97 = f32[73,64]{0,1:T(8,128)} all-reduce(f32[73,64]{0,1:T(8,128)S(1)} %pad_maximum_fusion.8), channel_id=1, replica_groups=mesh['clips'=2,'context'=4,'tensor'=4] {'tensor'}, use_global_device_ids=true, to_apply=%region_22.23 | all-reduce | flops 4672 | bytes 37376 | tf_op jit(solution)/shard_map/psum | solution.py:646
  574.4 35.4 %reduce-scatter.37.cloned.1.call-done = bf16[128,512]{1,0:T(8,128)(2,1)} async-done(((bf16[1024,512]{1,0:T(8,128)(2,1)}), bf16[128,512]{1,0:T(8,128)(2,1)}) %reduce-scatter.37.cloned.1.call-update) | async-done | bytes 131088
  611.6 4.4 convolution_convert_fusion.1
  616.0 3.9 copy.61
  621.7 2.7 convolution_convert_fusion.3.partial_ref
  624.4 34.9 %backward_sum_8.1 = (f32[512,1024]{1,0:T(8,128)S(1)}, bf16[512,1024]{1,0:T(8,128)(2,1)}, f32[8,1024]{1,0:T(8,128)S(1)}) custom-call(bf16[512,1024]{1,0:T(8,128)(2,1)S(1)} %convolution_convert_fusion.3.partial_ref, bf16[512,1024]{1,0:T(8,128)(2,1)S(1)} %bitcast.208, f32[1,1024]{1,0:T(1,128)S(1)} %bitcast.227, f32[512,1024]{1,0:T(8,128)S(1)} %copy-done.43), custom_call_target="tpu_custom_call" | custom-call | flops 60000002048 | bytes 100000000 | tf_op jit(solution)/shard_map/backward_sum_8/pallas_call | solution.py:189
  662.0 36.4 %reduce-scatter.29.cloned.1.call-done = bf16[1,128,1024]{2,1,0:T(8,128)(2,1)} async-done(((bf16[1,1024,1024]{2,1,0:T(8,128)(2,1)}), bf16[1,128,1024]{2,1,0:T(8,128)(2,1)}) %reduce-scatter.29.cloned.1.call-update) | async-done | bytes 262160 | tf_op jit(solution)/shard_map/reduce_scatter | solution.py:59
  698.4 1.8 bitcast_convert_fusion.2
  700.2 39.7 %reduce-scatter.33.cloned.1.call-done = bf16[128,768]{1,0:T(8,128)(2,1)} async-done(((bf16[1024,768]{1,0:T(8,128)(2,1)}), bf16[128,768]{1,0:T(8,128)(2,1)}) %reduce-scatter.33.cloned.1.call-update) | async-done | bytes 196624
  741.8 1.8 copy.56
  743.6 40.6 %reduce-scatter.27.cloned.1.call-done = bf16[1,128,1024]{2,1,0:T(8,128)(2,1)} async-done(((bf16[1,1024,1024]{2,1,0:T(8,128)(2,1)}), bf16[1,128,1024]{2,1,0:T(8,128)(2,1)}) %reduce-scatter.27.cloned.1.call-update) | async-done | bytes 262160 | tf_op jit(solution)/shard_map/reduce_scatter | solution.py:59
  784.2 1.8 bitcast_convert_fusion.3
  786.0 42.5 %reduce-scatter.31.cloned.1.call-done = bf16[128,1024]{1,0:T(8,128)(2,1)} async-done(((bf16[1024,1024]{1,0:T(8,128)(2,1)}), bf16[128,1024]{1,0:T(8,128)(2,1)}) %reduce-scatter.31.cloned.1.call-update) | async-done | bytes 262160
  830.4 56.4 %all-reduce.5.cloned.1.call-done = (f32[1024]{0:T(1024)}, f32[1024]{0:T(1024)}, f32[73,64]{0,1:T(8,128)}, f32[1024]{0:T(1024)}, f32[31,256]{1,0:T(8,128)}, /*ind...) async-done(((f32[1024]{0:T(1024)}, f32[1024]{0:T(1024)}, f32[73,64]{0,1:T(8,128)}, f32[1024]{0:T(1024)}, f32[31,256]{1,0:T(8,128)}, /*index=5*/f32[256]{0:T(256)}, f32[1024]{0:T(1024)}, ...) | async-done | bytes 71952 | tf_op jit(solution)/shard_map/psum | solution.py:647
  887.8 1.3 copy.86
  (469 shorter events, 61.1 us)
Async XLA Ops:
  7.2 33.8 %all-gather.21.cloned.1.call-start = ((), (), s32[]{:S(2)}) async-start(), calls=%async_computation.18 | async-start | bytes 2359296 | tf_op jit(solution)/shard_map/all_gather | solution.py:53
  9.1 31.9 %copy-start.27 = (f32[1024]{0:T(1024)S(1)}, f32[1024]{0:T(1024)}, u32[]{:S(2)}) copy-start(f32[1024]{0:T(1024)} %param.19) | copy-start | bytes 12292
  9.2 62.4 %all-gather.13.cloned.1.call-start = ((), (), s32[]{:S(2)}) async-start(), calls=%async_computation.10 | async-start | bytes 2359296 | tf_op jit(solution)/shard_map/all_gather | solution.py:54
  11.0 99.3 %all-gather.15.cloned.1.call-start = ((), (), s32[]{:S(2)}) async-start(), calls=%async_computation.11 | async-start | bytes 1769472 | tf_op jit(solution)/shard_map/all_gather | solution.py:53
  11.8 120.4 %all-gather.25.cloned.1.call-start = ((), (), s32[]{:S(2)}) async-start(), calls=%async_computation.20 | async-start | bytes 1310720 | tf_op jit(solution)/shard_map/all_gather | solution.py:512
  12.1 31.9 %copy-start.139 = (f32[512]{0:T(512)}, f32[512]{0:T(512)S(1)}, u32[]{:S(2)}) copy-start(f32[512]{0:T(512)S(1)} %broadcast_multiply_fusion.3) | copy-start | bytes 6148
  12.5 31.4 %copy-start.159 = (f32[512]{0:T(512)}, f32[512]{0:T(512)S(1)}, u32[]{:S(2)}) copy-start(f32[512]{0:T(512)S(1)} %add_rsqrt_fusion.1) | copy-start | bytes 6148
  43.9 30.6 %copy-start.170 = (f32[512,1024]{1,0:T(8,128)}, f32[512,1024]{1,0:T(8,128)S(1)}, u32[]{:S(2)}) copy-start(f32[512,1024]{1,0:T(8,128)S(1)} %fusion.15) | copy-start | bytes 6291460
  44.0 30.6 %copy-start.25 = (f32[1024]{0:T(1024)S(1)}, f32[1024]{0:T(1024)}, u32[]{:S(2)}) copy-start(f32[1024]{0:T(1024)} %param.22) | copy-start | bytes 12292
  114.7 35.9 %copy-start.5 = (bf16[512,256]{1,0:T(8,128)(2,1)}, bf16[512,256]{1,0:T(8,128)(2,1)S(1)}, u32[]{:S(2)}) copy-start(bf16[512,256]{1,0:T(8,128)(2,1)S(1)} %get-tuple-element.166.q_ref) | copy-start | bytes 786436
  114.7 35.9 %all-gather.23.cloned.1.call-start = ((), (), s32[]{:S(2)}) async-start(), calls=%async_computation.19 | async-start | bytes 1310720 | tf_op jit(solution)/shard_map/all_gather | solution.py:511
  115.3 90.7 %all-gather.17.cloned.1.call-start = ((), (), s32[]{:S(2)}) async-start(), calls=%async_computation.12 | async-start | bytes 1179648 | tf_op jit(solution)/shard_map/all_gather | solution.py:53
  116.0 154.7 %all-gather.27.cloned.1.call-start = ((), (), s32[]{:S(2)}) async-start(), calls=%async_computation.21 | async-start | bytes 2359296 | tf_op jit(solution)/shard_map/all_gather | solution.py:53
  116.9 159.1 %all-gather.19.cloned.1.call-start = ((), (), s32[]{:S(2)}) async-start(), calls=%async_computation.13 | async-start | bytes 2359296 | tf_op jit(solution)/shard_map/all_gather | solution.py:54
  117.7 350.5 %reduce-scatter.23.cloned.1.call-start = ((), (), s32[]{:S(2)}) async-start(), calls=%async_computation.14 | async-start | bytes 1310720 | tf_op jit(solution)/shard_map/reduce_scatter | solution.py:530
  117.8 103.7 %copy-start.83 = (f32[1,256]{1,0:T(1,128)}, f32[1,256]{1,0:T(1,128)S(1)}, u32[]{:S(2)}) copy-start(f32[1,256]{1,0:T(1,128)S(1)} %get-tuple-element.186) | copy-start | bytes 3076
  117.8 103.7 %copy-start.85 = (f32[1,256]{1,0:T(1,128)}, f32[1,256]{1,0:T(1,128)S(1)}, u32[]{:S(2)}) copy-start(f32[1,256]{1,0:T(1,128)S(1)} %get-tuple-element.187) | copy-start | bytes 3076
  117.8 103.7 %copy-start.87 = (f32[1,256]{1,0:T(1,128)}, f32[1,256]{1,0:T(1,128)S(1)}, u32[]{:S(2)}) copy-start(f32[1,256]{1,0:T(1,128)S(1)} %get-tuple-element.188) | copy-start | bytes 3076
  117.8 103.7 %copy-start.89 = (f32[1,256]{1,0:T(1,128)}, f32[1,256]{1,0:T(1,128)S(1)}, u32[]{:S(2)}) copy-start(f32[1,256]{1,0:T(1,128)S(1)} %get-tuple-element.189) | copy-start | bytes 3076
  117.8 103.7 %copy-start.91 = (f32[1,256]{1,0:T(1,128)}, f32[1,256]{1,0:T(1,128)S(1)}, u32[]{:S(2)}) copy-start(f32[1,256]{1,0:T(1,128)S(1)} %get-tuple-element.190) | copy-start | bytes 3076
  117.8 103.7 %copy-start.93 = (f32[1,256]{1,0:T(1,128)}, f32[1,256]{1,0:T(1,128)S(1)}, u32[]{:S(2)}) copy-start(f32[1,256]{1,0:T(1,128)S(1)} %get-tuple-element.191) | copy-start | bytes 3076
  117.8 103.7 %copy-start.95 = (f32[1,256]{1,0:T(1,128)}, f32[1,256]{1,0:T(1,128)S(1)}, u32[]{:S(2)}) copy-start(f32[1,256]{1,0:T(1,128)S(1)} %get-tuple-element.192) | copy-start | bytes 3076
  117.8 103.7 %copy-start.97 = (f32[1,256]{1,0:T(1,128)}, f32[1,256]{1,0:T(1,128)S(1)}, u32[]{:S(2)}) copy-start(f32[1,256]{1,0:T(1,128)S(1)} %get-tuple-element.193) | copy-start | bytes 3076
  117.8 103.7 %copy-start.99 = (f32[1,256]{1,0:T(1,128)}, f32[1,256]{1,0:T(1,128)S(1)}, u32[]{:S(2)}) copy-start(f32[1,256]{1,0:T(1,128)S(1)} %get-tuple-element.194) | copy-start | bytes 3076
  117.9 103.7 %copy-start.101 = (f32[1,256]{1,0:T(1,128)}, f32[1,256]{1,0:T(1,128)S(1)}, u32[]{:S(2)}) copy-start(f32[1,256]{1,0:T(1,128)S(1)} %get-tuple-element.195) | copy-start | bytes 3076
  117.9 103.7 %copy-start.103 = (f32[1,256]{1,0:T(1,128)}, f32[1,256]{1,0:T(1,128)S(1)}, u32[]{:S(2)}) copy-start(f32[1,256]{1,0:T(1,128)S(1)} %get-tuple-element.196) | copy-start | bytes 3076
  117.9 103.7 %copy-start.105 = (f32[1,256]{1,0:T(1,128)}, f32[1,256]{1,0:T(1,128)S(1)}, u32[]{:S(2)}) copy-start(f32[1,256]{1,0:T(1,128)S(1)} %get-tuple-element.197) | copy-start | bytes 3076
  118.5 103.1 %copy-start.107 = (f32[1,256]{1,0:T(1,128)}, f32[1,256]{1,0:T(1,128)S(1)}, u32[]{:S(2)}) copy-start(f32[1,256]{1,0:T(1,128)S(1)} %get-tuple-element.167) | copy-start | bytes 3076
  118.5 103.1 %copy-start.109 = (f32[1,256]{1,0:T(1,128)}, f32[1,256]{1,0:T(1,128)S(1)}, u32[]{:S(2)}) copy-start(f32[1,256]{1,0:T(1,128)S(1)} %get-tuple-element.168) | copy-start | bytes 3076
  118.5 103.2 %copy-start.111 = (f32[1,256]{1,0:T(1,128)}, f32[1,256]{1,0:T(1,128)S(1)}, u32[]{:S(2)}) copy-start(f32[1,256]{1,0:T(1,128)S(1)} %get-tuple-element.169) | copy-start | bytes 3076
  118.5 103.2 %copy-start.113 = (f32[1,256]{1,0:T(1,128)}, f32[1,256]{1,0:T(1,128)S(1)}, u32[]{:S(2)}) copy-start(f32[1,256]{1,0:T(1,128)S(1)} %get-tuple-element.170) | copy-start | bytes 3076
  118.5 103.2 %copy-start.115 = (f32[1,256]{1,0:T(1,128)}, f32[1,256]{1,0:T(1,128)S(1)}, u32[]{:S(2)}) copy-start(f32[1,256]{1,0:T(1,128)S(1)} %get-tuple-element.171) | copy-start | bytes 3076
  118.5 103.2 %copy-start.117 = (f32[1,256]{1,0:T(1,128)}, f32[1,256]{1,0:T(1,128)S(1)}, u32[]{:S(2)}) copy-start(f32[1,256]{1,0:T(1,128)S(1)} %get-tuple-element.172) | copy-start | bytes 3076
  118.5 103.2 %copy-start.119 = (f32[1,256]{1,0:T(1,128)}, f32[1,256]{1,0:T(1,128)S(1)}, u32[]{:S(2)}) copy-start(f32[1,256]{1,0:T(1,128)S(1)} %get-tuple-element.173) | copy-start | bytes 3076
  118.5 103.2 %copy-start.121 = (f32[1,256]{1,0:T(1,128)}, f32[1,256]{1,0:T(1,128)S(1)}, u32[]{:S(2)}) copy-start(f32[1,256]{1,0:T(1,128)S(1)} %get-tuple-element.174) | copy-start | bytes 3076
  118.5 103.2 %copy-start.123 = (f32[1,256]{1,0:T(1,128)}, f32[1,256]{1,0:T(1,128)S(1)}, u32[]{:S(2)}) copy-start(f32[1,256]{1,0:T(1,128)S(1)} %get-tuple-element.175) | copy-start | bytes 3076
  118.5 103.2 %copy-start.125 = (f32[1,256]{1,0:T(1,128)}, f32[1,256]{1,0:T(1,128)S(1)}, u32[]{:S(2)}) copy-start(f32[1,256]{1,0:T(1,128)S(1)} %get-tuple-element.176) | copy-start | bytes 3076
  118.5 103.2 %copy-start.127 = (f32[1,256]{1,0:T(1,128)}, f32[1,256]{1,0:T(1,128)S(1)}, u32[]{:S(2)}) copy-start(f32[1,256]{1,0:T(1,128)S(1)} %get-tuple-element.177) | copy-start | bytes 3076
  118.5 103.2 %copy-start.129 = (f32[1,256]{1,0:T(1,128)}, f32[1,256]{1,0:T(1,128)S(1)}, u32[]{:S(2)}) copy-start(f32[1,256]{1,0:T(1,128)S(1)} %get-tuple-element.178) | copy-start | bytes 3076
  118.6 103.2 %copy-start.131 = (f32[1,256]{1,0:T(1,128)}, f32[1,256]{1,0:T(1,128)S(1)}, u32[]{:S(2)}) copy-start(f32[1,256]{1,0:T(1,128)S(1)} %get-tuple-element.179) | copy-start | bytes 3076
  118.6 103.2 %copy-start.133 = (f32[1,256]{1,0:T(1,128)}, f32[1,256]{1,0:T(1,128)S(1)}, u32[]{:S(2)}) copy-start(f32[1,256]{1,0:T(1,128)S(1)} %get-tuple-element.180) | copy-start | bytes 3076
  118.6 103.2 %copy-start.135 = (f32[1,256]{1,0:T(1,128)}, f32[1,256]{1,0:T(1,128)S(1)}, u32[]{:S(2)}) copy-start(f32[1,256]{1,0:T(1,128)S(1)} %get-tuple-element.181) | copy-start | bytes 3076
  118.6 103.2 %copy-start.137 = (f32[1,256]{1,0:T(1,128)}, f32[1,256]{1,0:T(1,128)S(1)}, u32[]{:S(2)}) copy-start(f32[1,256]{1,0:T(1,128)S(1)} %get-tuple-element.182) | copy-start | bytes 3076
  131.0 38.0 %copy-start.62 = (bf16[256,1024]{1,0:T(8,128)(2,1)}, bf16[256,1024]{1,0:T(8,128)(2,1)S(1)}, u32[]{:S(2)}) copy-start(bf16[256,1024]{1,0:T(8,128)(2,1)S(1)} %all_gather.35) | copy-start | bytes 1572868
  131.2 37.9 %copy-start.8 = (bf16[512,128]{1,0:T(8,128)(2,1)}, bf16[512,128]{1,0:T(8,128)(2,1)S(1)}, u32[]{:S(2)}) copy-start(bf16[512,128]{1,0:T(8,128)(2,1)S(1)} %maximum_maximum_fusion.span_ref) | copy-start | bytes 393220
  209.3 12.2 %collective-permute-start = (f32[30,256]{1,0:T(8,128)S(1)}, f32[30,256]{1,0:T(8,128)S(1)}, u32[]{:S(2)}, u32[]{:S(2)}) collective-permute-start(f32[30,256]{1,0:T(8,128)S(1)} %slice.498), channel_id=1, source_target_pairs={{0,4},{4,8},{8,12},{1,5},{5,9},{9,13},{2,6},{6,10},{10,14},{3,7},{... | collective-permute-start | bytes 92168 | tf_op jit(solution)/shard_map/ppermute | solution.py:21
  279.7 31.7 %copy-start.167 = (bf16[1024,1024]{1,0:T(8,128)(2,1)S(1)}, bf16[1024,1024]{1,0:T(8,128)(2,1)}, u32[]{:S(2)}) copy-start(bf16[1024,1024]{1,0:T(8,128)(2,1)} %all-gather.19.cloned.1.call-done) | copy-start | bytes 6291460
  279.7 31.7 %copy-start.169 = (f32[512,1024]{1,0:T(8,128)S(1)}, f32[512,1024]{1,0:T(8,128)}, u32[]{:S(2)}) copy-start(f32[512,1024]{1,0:T(8,128)} %fusion.169) | copy-start | bytes 6291460
  314.4 30.4 %copy-start.60 = (f32[512,256]{1,0:T(8,128)S(1)}, f32[512,256]{1,0:T(8,128)}, u32[]{:S(2)}) copy-start(f32[512,256]{1,0:T(8,128)} %copy-done.59) | copy-start | bytes 1572868
  361.1 3.1 collective-permute-start.1
  370.8 35.1 %copy-start.63 = (bf16[256,1024]{1,0:T(8,128)(2,1)S(1)}, bf16[256,1024]{1,0:T(8,128)(2,1)}, u32[]{:S(2)}) copy-start(bf16[256,1024]{1,0:T(8,128)(2,1)} %copy-done.62) | copy-start | bytes 1572868
  443.8 51.1 %reduce-scatter.25.cloned.1.call-start = ((), (), s32[]{:S(2)}) async-start(), calls=%async_computation.15 | async-start | bytes 1310720 | tf_op jit(solution)/shard_map/reduce_scatter | solution.py:531
  444.3 126.8 %reduce-scatter.39.cloned.1.call-start = ((), (), s32[]{:S(2)}) async-start(), calls=%async_computation.26 | async-start | bytes 589824
  449.6 123.1 %reduce-scatter.35.cloned.1.call-start = ((), (), s32[]{:S(2)}) async-start(), calls=%async_computation.24 | async-start | bytes 589824
  451.1 158.6 %reduce-scatter.37.cloned.1.call-start = ((), (), s32[]{:S(2)}) async-start(), calls=%async_computation.25 | async-start | bytes 1179648
  455.4 204.5 %reduce-scatter.41.cloned.1.call-start = ((), (), s32[]{:S(2)}) async-start(), calls=%async_computation.27 | async-start | bytes 2359296
  463.8 234.6 %reduce-scatter.29.cloned.1.call-start = ((), (), s32[]{:S(2)}) async-start(), calls=%async_computation.17 | async-start | bytes 2359296 | tf_op jit(solution)/shard_map/reduce_scatter | solution.py:59
  467.9 272.0 %reduce-scatter.33.cloned.1.call-start = ((), (), s32[]{:S(2)}) async-start(), calls=%async_computation.23 | async-start | bytes 1769472
  502.5 281.7 %reduce-scatter.27.cloned.1.call-start = ((), (), s32[]{:S(2)}) async-start(), calls=%async_computation.16 | async-start | bytes 2359296 | tf_op jit(solution)/shard_map/reduce_scatter | solution.py:59
  505.8 33.8 %copy-start.165 = (bf16[1024,1024]{1,0:T(8,128)(2,1)S(1)}, bf16[1024,1024]{1,0:T(8,128)(2,1)}, u32[]{:S(2)}) copy-start(bf16[1024,1024]{1,0:T(8,128)(2,1)} %all-gather.13.cloned.1.call-done) | copy-start | bytes 6291460
  505.8 33.8 %copy-start.171 = (f32[512,1024]{1,0:T(8,128)S(1)}, f32[512,1024]{1,0:T(8,128)}, u32[]{:S(2)}) copy-start(f32[512,1024]{1,0:T(8,128)} %copy-done.170) | copy-start | bytes 6291460
  545.3 283.2 %reduce-scatter.31.cloned.1.call-start = ((), (), s32[]{:S(2)}) async-start(), calls=%async_computation.22 | async-start | bytes 2359296
  620.6 266.2 %all-reduce.5.cloned.1.call-start = ((), (), s32[]{:S(2)}) async-start(), calls=%async_computation.28 | async-start | bytes 174080 | tf_op jit(solution)/shard_map/psum | solution.py:647
  661.9 224.8 %copy-start.4 = (bf16[512,1024]{1,0:T(8,128)(2,1)S(1)}, bf16[512,1024]{1,0:T(8,128)(2,1)}, u32[]{:S(2)}) copy-start(bf16[512,1024]{1,0:T(8,128)(2,1)} %copy-done.3) | copy-start | bytes 3145732
  (132 other events, 993.8 us)
Sparse Core Ops, SparseCore 0:
  10.5 30.4 all-gather.20
  43.5 28.0 all-gather.12
  74.1 25.6 all-gather.14
  114.8 17.3 all-gather.24
  134.2 16.3 all-gather.22
  152.9 23.3 all-gather.16
  178.8 27.7 all-gather.26
  209.1 28.1 all-gather.18
  443.9 23.7 reduce-scatter.22
  470.0 24.7 reduce-scatter.24
  498.5 34.2 reduce-scatter.38
  536.3 34.2 reduce-scatter.34
  573.7 35.9 reduce-scatter.36
  612.9 41.1 reduce-scatter.40
  657.2 41.1 reduce-scatter.28
  701.5 38.3 reduce-scatter.32
  743.0 41.1 reduce-scatter.26
  787.3 41.1 reduce-scatter.30
  834.1 52.6 all-reduce.4

commit v3 on v2

--- a/solution.py
+++ b/solution.py
@@ -7,6 +7,7 @@
 from jax.experimental.pallas import tpu as pltpu
 from jax.sharding import PartitionSpec as P
 
+CLIPS, CONTEXT, TENSOR = "clips", "context", "tensor"
 D = 1024
 HEAD_DIM = 64
 LEFT = 64
@@ -50,35 +51,359 @@
 
 def fetch(weight_in, weight_out):
     return (
-        lax.all_gather(weight_in.astype(jnp.bfloat16), ("clips", "context"), axis=1, tiled=True),
-        lax.all_gather(weight_out.astype(jnp.bfloat16), ("clips", "context"), axis=1, tiled=True),
+        lax.all_gather(weight_in.astype(jnp.bfloat16), (CLIPS, CONTEXT), axis=weight_in.ndim - 2, tiled=True),
+        lax.all_gather(weight_out.astype(jnp.bfloat16), (CLIPS, CONTEXT), axis=1, tiled=True),
     )
 
 
 def scatter_sum(grad, axis):
     summed = lax.psum_scatter(
-        grad.astype(jnp.bfloat16), ("clips", "context"), scatter_dimension=axis, tiled=True
+        grad.astype(jnp.bfloat16), (CLIPS, CONTEXT), scatter_dimension=axis, tiled=True
     )
     return summed.astype(jnp.float32)
 
 
 def send_grads(grad_in, grad_out):
-    return (scatter_sum(grad_in, 1), scatter_sum(grad_out, 1))
+    return (scatter_sum(grad_in, grad_in.ndim - 2), scatter_sum(grad_out, 1))
 
 
 MESH_ID = pl.DeviceIdType.MESH
-CHUNKS = 32
-LAG = 5
-
-
-def line_sum(axis, partial_ref, acc_ref, from_end, from_mid, total_ref, send_sem, recv_sem, finish):
+CHUNKS = 16
+LAG = 3
+FULL, TOP, BOTTOM = 0, 1, 2
+FIRST, ATTEND, CONVOLVE, SECOND = range(4)
+
+
+def near():
+    across_clips = lax.axis_index(CLIPS)
+    along = lax.axis_index(CONTEXT)
+    deep, core = along // 2, along % 2
+    devices = (
+        {CLIPS: 1 - across_clips},
+        {CONTEXT: (1 - deep) * 2 + core},
+        {CONTEXT: deep * 2 + 1 - core},
+    )
+    return (across_clips, deep, core), devices
+
+
+def greet(devices):
+    barrier = pltpu.get_barrier_semaphore()
+    for device in devices:
+        pl.semaphore_signal(barrier, inc=1, device_id=device, device_id_type=MESH_ID)
+    pl.semaphore_wait(barrier, len(devices))
+
+
+def part_of(ref, wide, count, shard, part):
+    if wide:
+        size = ref.shape[-1] // count
+        rows = ref.shape[-2]
+        along = slice(None) if part == FULL else pl.ds((part - 1) * (rows // 2), rows // 2)
+        return ref.at[along, pl.ds(pl.multiple_of(shard * size, 128), size)]
+    size = ref.shape[-2] // count
+    start, length = shard * size, size
+    if part != FULL:
+        length = size // 2
+        start = start + (part - 1) * length
+    window = pl.ds(pl.multiple_of(start, 16), length)
+    return ref.at[window] if len(ref.shape) == 2 else ref.at[:, window]
+
+
+def half_of(ref, part):
+    length = ref.shape[-2] // 2
+    window = pl.ds((part - 1) * length, length)
+    return ref.at[window] if len(ref.shape) == 2 else ref.at[:, window]
+
+
+class Gather:
+    copies = 9
+    line = False
+
+    def __init__(self, wide, shard_shape):
+        self.wide = wide
+        self.shape = shard_shape[:-2] + (
+            (shard_shape[-2], shard_shape[-1] * 8) if wide else (shard_shape[-2] * 8, shard_shape[-1])
+        )
+
+    def outs(self):
+        return [(self.shape, jnp.bfloat16)]
+
+    def scratch(self):
+        return [pltpu.SemaphoreType.DMA((self.copies,)), pltpu.SemaphoreType.DMA((self.copies,)), pltpu.SemaphoreType.DMA]
+
+    def bind(self, ins, outs, scratch):
+        (shard_ref,), (full_ref,) = ins, outs
+        send, recv, own_sem = scratch
+        (x, y, core), (to_x, to_y, to_core) = near()
+        shard = lambda a, b: a * 4 + b * 2 + core
+        own, at_x, at_y, at_far = shard(x, y), shard(1 - x, y), shard(x, 1 - y), shard(1 - x, 1 - y)
+        place = lambda which, part: part_of(full_ref, self.wide, 8, which, part)
+
+        def copy(index, source, which, part, device):
+            return pltpu.make_async_remote_copy(
+                src_ref=source, dst_ref=place(which, part), send_sem=send.at[index], recv_sem=recv.at[index],
+                device_id=device, device_id_type=MESH_ID,
+            )
+
+        passed = lambda index, which, part, device: copy(index, place(which, part), which, part, device)
+        moves = [
+            copy(0, shard_ref, own, FULL, to_x),
+            copy(1, shard_ref, own, FULL, to_y),
+            copy(2, shard_ref, own, FULL, to_core),
+            passed(3, at_x, TOP, to_y),
+            passed(4, at_x, FULL, to_core),
+            passed(5, at_y, BOTTOM, to_x),
+            passed(6, at_y, FULL, to_core),
+            passed(7, at_far, TOP, to_core),
+            passed(8, at_far, BOTTOM, to_core),
+        ]
+        mine = pltpu.make_async_copy(shard_ref, place(own, FULL), own_sem)
+
+        def begin():
+            for index in (0, 1, 2):
+                moves[index].start()
+            mine.start()
+
+        def second():
+            moves[0].wait_recv()
+            moves[3].start()
+            moves[4].start()
+            moves[1].wait_recv()
+            moves[5].start()
+            moves[6].start()
+
+        def third():
+            moves[3].wait_recv()
+            moves[7].start()
+            moves[5].wait_recv()
+            moves[8].start()
+
+        def last():
+            for index in (2, 4, 6, 7, 8):
+                moves[index].wait_recv()
+            mine.wait()
+            for move in moves:
+                move.wait_send()
+
+        return begin, [second, third], last
+
+
+class Scatter:
+    copies = 8
+    line = False
+
+    def __init__(self, wide, full_shape):
+        self.wide = wide
+        self.shape = full_shape[:-2] + (
+            (full_shape[-2], full_shape[-1] // 8) if wide else (full_shape[-2] // 8, full_shape[-1])
+        )
+
+    def outs(self):
+        return [(self.shape, jnp.float32)]
+
+    def scratch(self):
+        half = self.shape[:-2] + (self.shape[-2] // 2, self.shape[-1])
+        return [
+            pltpu.VMEM((4,) + self.shape, jnp.bfloat16),
+            pltpu.VMEM((4,) + self.shape, jnp.bfloat16),
+            pltpu.VMEM((2,) + self.shape, jnp.bfloat16),
+            pltpu.VMEM((2,) + half, jnp.bfloat16),
+            pltpu.SemaphoreType.DMA((self.copies,)),
+            pltpu.SemaphoreType.DMA((self.copies,)),
+        ]
+
+    def bind(self, ins, outs, scratch):
+        (full_ref,), (out_ref,) = ins, outs
+        from_core, pair, whole, halves, send, recv = scratch
+        (x, y, core), (to_x, to_y, to_core) = near()
+
+        def copy(index, source, target, device):
+            return pltpu.make_async_remote_copy(
+                src_ref=source, dst_ref=target, send_sem=send.at[index], recv_sem=recv.at[index],
+                device_id=device, device_id_type=MESH_ID,
+            )
+
+        place = lambda slot, at_core: part_of(full_ref, self.wide, 8, slot * 2 + at_core, FULL)
+        own, at_x, at_y, at_far = x * 2 + y, (1 - x) * 2 + y, x * 2 + 1 - y, (1 - x) * 2 + 1 - y
+        moves = [copy(slot, place(slot, 1 - core), from_core.at[slot], to_core) for slot in range(4)]
+        moves += [
+            copy(4, half_of(pair.at[at_far], TOP), halves.at[0], to_x),
+            copy(5, half_of(pair.at[at_far], BOTTOM), halves.at[1], to_y),
+            copy(6, pair.at[at_x], whole.at[0], to_x),
+            copy(7, pair.at[at_y], whole.at[1], to_y),
+        ]
+        wide = lambda ref: ref[...].astype(jnp.float32)
+
+        def begin():
+            for slot in range(4):
+                moves[slot].start()
+
+        def second():
+            for slot in range(4):
+                moves[slot].wait_recv()
+                pair[slot] = (wide(place(slot, core)) + wide(from_core.at[slot])).astype(jnp.bfloat16)
+            moves[4].start()
+            moves[5].start()
+
+        def third():
+            moves[4].wait_recv()
+            target = half_of(pair.at[at_y], TOP)
+            target[...] = (wide(target) + wide(halves.at[0])).astype(jnp.bfloat16)
+            moves[7].start()
+            moves[5].wait_recv()
+            target = half_of(pair.at[at_x], BOTTOM)
+            target[...] = (wide(target) + wide(halves.at[1])).astype(jnp.bfloat16)
+            moves[6].start()
+
+        def last():
+            moves[6].wait_recv()
+            moves[7].wait_recv()
+            out_ref[...] = wide(pair.at[own]) + wide(whole.at[0]) + wide(whole.at[1])
+            for move in moves:
+                move.wait_send()
+
+        return begin, [second, third], last
+
+
+class PlaneSum:
+    line = False
+
+    def __init__(self, shape):
+        self.shape = shape
+
+    def outs(self):
+        return [(self.shape, jnp.float32)]
+
+    def scratch(self):
+        return [
+            pltpu.VMEM((3,) + self.shape, jnp.float32),
+            pltpu.VMEM((2,) + self.shape, jnp.float32),
+            pltpu.SemaphoreType.DMA((3,)),
+            pltpu.SemaphoreType.DMA((3,)),
+        ]
+
+    def bind(self, ins, outs, scratch):
+        (value_ref,), (out_ref,) = ins, outs
+        slots, totals, send, recv = scratch
+        to_x, to_y, to_core = near()[1]
+        moves = [
+            pltpu.make_async_remote_copy(
+                src_ref=source, dst_ref=slots.at[index], send_sem=send.at[index], recv_sem=recv.at[index],
+                device_id=device, device_id_type=MESH_ID,
+            )
+            for index, (source, device) in enumerate(
+                ((value_ref, to_core), (totals.at[0], to_y), (totals.at[1], to_x))
+            )
+        ]
+
+        def begin():
+            moves[0].start()
+
+        def second():
+            moves[0].wait_recv()
+            totals[0] = value_ref[...] + slots[0]
+            moves[1].start()
+
+        def third():
+            moves[1].wait_recv()
+            totals[1] = totals[0] + slots[1]
+            moves[2].start()
+
+        def last():
+            moves[2].wait_recv()
+            out_ref[...] = totals[1] + slots[2]
+            for move in moves:
+                move.wait_send()
+
+        return begin, [second, third], last
+
+
+class LineSum:
+    line = True
+
+    def __init__(self, shape):
+        self.shape = shape
+
+    def outs(self):
+        return [(self.shape, jnp.float32)]
+
+    def scratch(self):
+        return [
+            pltpu.VMEM((4,) + self.shape, jnp.float32),
+            pltpu.SemaphoreType.DMA((4,)),
+            pltpu.SemaphoreType.DMA((4,)),
+        ]
+
+    def bind(self, ins, outs, scratch):
+        (value_ref,), (out_ref,) = ins, outs
+        slots, send, recv = scratch
+        at = lax.axis_index(TENSOR)
+
+        def copy(step, slot):
+            return pltpu.make_async_remote_copy(
+                src_ref=value_ref, dst_ref=slots.at[slot], send_sem=send.at[step], recv_sem=recv.at[slot],
+                device_id={TENSOR: (at + step) % 4}, device_id_type=MESH_ID,
+            )
+
+        def begin():
+            for step in range(1, 4):
+                copy(step, at).start()
+            slots[at] = value_ref[...]
+
+        def last():
+            for step in range(1, 4):
+                copy(step, (at + step) % 4).wait_recv()
+            out_ref[...] = slots[0] + slots[1] + slots[2] + slots[3]
+            for step in range(1, 4):
+                copy(step, at).wait_send()
+
+        return begin, [lambda: None, lambda: None], last
+
+
+def bind_all(tasks, ins, outs, scratch):
+    begins, middles, lasts = [], [], []
+    for task, task_in, task_out in zip(tasks, ins, outs):
+        count = len(task.scratch())
+        begin, steps, last = task.bind((task_in,), (task_out,), scratch[:count])
+        scratch = scratch[count:]
+        begins.append(begin)
+        middles.append(steps)
+        lasts.append(last)
+    return begins, [step for turn in zip(*middles) for step in turn], lasts
+
+
+def plane_call(cid, tasks, operands):
+    vmem = pl.BlockSpec(memory_space=pltpu.VMEM)
+    outs = [out for task in tasks for out in task.outs()]
+
+    def kernel(*refs):
+        n = len(tasks)
+        greet(near()[1])
+        begins, steps, lasts = bind_all(tasks, refs[:n], refs[n : 2 * n], refs[2 * n :])
+        for step in begins + steps + lasts:
+            step()
+
+    return pl.pallas_call(
+        kernel,
+        out_shape=tuple(jax.ShapeDtypeStruct(shape, kind) for shape, kind in outs),
+        in_specs=[vmem] * len(operands),
+        out_specs=(vmem,) * len(outs),
+        scratch_shapes=[piece for task in tasks for piece in task.scratch()],
+        compiler_params=pltpu.CompilerParams(collective_id=cid, has_side_effects=True, vmem_limit_bytes=12 << 20),
+        cost_estimate=pl.CostEstimate(flops=30_000_000_000, bytes_accessed=50_000_000, transcendentals=0),
+        name=f"call_{cid}",
+    )(*operands)
+
+
+def line_sum(axis, partial_ref, acc_ref, from_end, from_mid, total_ref, send_sem, recv_sem, finish, others, whole_line, begins, steps, lasts):
     at = lax.axis_index(axis)
     low = at < 2
     end = jnp.where(low, 0, 3)
     mid = jnp.where(low, 1, 2)
     other = jnp.where(low, 2, 1)
     is_mid = at == mid
+    rest = [{axis: (at + step) % 4} for step in range(1, 4)]
     size = partial_ref.shape[0] // CHUNKS
+    gap = (CHUNKS - LAG) // (len(steps) + 1)
 
     def rows(chunk):
         return pl.ds(pl.multiple_of(chunk * size, size), size)
@@ -96,19 +421,23 @@
     inward = lambda chunk: hop(0, chunk, partial_ref, from_end, mid)
     across = lambda chunk: hop(1, chunk, acc_ref, from_mid, other)
     outward = lambda chunk: hop(2, chunk, total_ref, total_ref, end)
-    barrier = pltpu.get_barrier_semaphore()
 
     def loop(low, high, body):
         def step(chunk, carry):
             body(chunk)
             return carry
+
         lax.fori_loop(low, high, step, 0)
+
+    def beside(chunk):
+        for index, step in enumerate(steps):
+            pl.when(chunk == LAG + (index + 1) * gap)(step)
 
     @pl.when(is_mid)
     def _():
-        pl.semaphore_signal(barrier, inc=1, device_id={axis: end}, device_id_type=MESH_ID)
-        pl.semaphore_signal(barrier, inc=1, device_id={axis: other}, device_id_type=MESH_ID)
-        pl.semaphore_wait(barrier, 2)
+        greet((rest if whole_line else [{axis: end}, {axis: other}]) + others)
+        for begin in begins:
+            begin()
 
         def first(chunk):
             inward(chunk).wait_recv()
@@ -126,6 +455,7 @@
         def both(chunk):
             first(chunk)
             second(chunk - LAG)
+            beside(chunk)
 
         loop(0, LAG, first)
         loop(LAG, CHUNKS, both)
@@ -139,16 +469,21 @@
 
     @pl.when(jnp.logical_not(is_mid))
     def _():
-        pl.semaphore_signal(barrier, inc=1, device_id={axis: mid}, device_id_type=MESH_ID)
-        pl.semaphore_wait(barrier, 1)
+        greet((rest if whole_line else [{axis: mid}]) + others)
         loop(0, CHUNKS, lambda chunk: inward(chunk).start())
+        for begin in begins:
+            begin()
 
         def receive(chunk):
+            beside(chunk + LAG)
             outward(chunk).wait_recv()
             finish(rows(chunk))
 
         loop(0, CHUNKS, receive)
         loop(0, CHUNKS, lambda chunk: inward(chunk).wait_send())
+
+    for last in lasts:
+        last()
 
 
 def unit_rows(rows_in):
@@ -174,32 +509,50 @@
     return total
 
 
-def sum_call(body, name, cid, partial, operands, outs):
+def sum_call(body, cid, partial, operands, outs, tasks, task_operands):
     rows, width = partial.shape
     chunk_shape = pltpu.VMEM((rows, width), jnp.bfloat16)
     vmem = pl.BlockSpec(memory_space=pltpu.VMEM)
+    task_outs = [out for task in tasks for out in task.outs()]
+    grant = (30 if any(isinstance(task, Scatter) for task in tasks) else 22) << 20
+    pieces = [piece for task in tasks for piece in task.scratch()]
 
     def kernel(partial_ref, *refs):
-        ins, results = refs[: len(operands)], refs[len(operands) : len(operands) + len(outs)]
-        acc, from_end, from_mid, total, send_sem, recv_sem = refs[len(operands) + len(outs) :]
+        def take(count):
+            nonlocal refs
+            taken, refs = refs[:count], refs[count:]
+            return taken
+
+        ins, task_ins = take(len(operands)), take(len(tasks))
+        results, task_results = take(len(outs)), take(len(tasks))
+        acc, from_end, from_mid, total, send_sem, recv_sem = take(6)
+        begins, steps, lasts, others = [], [], [], []
+        if tasks:
+            others = list(near()[1])
+            begins, steps, lasts = bind_all(tasks, task_ins, task_results, refs)
         start, finish = body(total, ins, results)
         start()
-        line_sum("tensor", partial_ref, acc, from_end, from_mid, total, send_sem, recv_sem, finish)
-
-    return pl.pallas_call(
+        line_sum(
+            TENSOR, partial_ref, acc, from_end, from_mid, total, send_sem, recv_sem, finish, others,
+            any(task.line for task in tasks), begins, steps, lasts,
+        )
+
+    got = pl.pallas_call(
         kernel,
-        out_shape=tuple(jax.ShapeDtypeStruct(shape, kind) for shape, kind in outs),
-        in_specs=[vmem] * (1 + len(operands)),
-        out_specs=(vmem,) * len(outs),
+        out_shape=tuple(jax.ShapeDtypeStruct(shape, kind) for shape, kind in list(outs) + task_outs),
+        in_specs=[vmem] * (1 + len(operands) + len(tasks)),
+        out_specs=(vmem,) * (len(outs) + len(tasks)),
         scratch_shapes=[chunk_shape] * 4
-        + [pltpu.SemaphoreType.DMA((3, CHUNKS)), pltpu.SemaphoreType.DMA((3, CHUNKS))],
-        compiler_params=pltpu.CompilerParams(collective_id=cid, has_side_effects=True, vmem_limit_bytes=40 << 20),
+        + [pltpu.SemaphoreType.DMA((3, CHUNKS)), pltpu.SemaphoreType.DMA((3, CHUNKS))]
+        + pieces,
+        compiler_params=pltpu.CompilerParams(collective_id=cid, has_side_effects=True, vmem_limit_bytes=grant),
         cost_estimate=pl.CostEstimate(flops=60_000_000_000, bytes_accessed=100_000_000, transcendentals=0),
-        name=name,
-    )(partial, *operands)
-
-
-def forward_sum(cid, partial, rows_in, gain, scale):
+        name=f"call_{cid}",
+    )(partial, *operands, *task_operands)
+    return got[: len(outs)], got[len(outs) :]
+
+
+def forward_sum(cid, partial, rows_in, gain, scale, tasks=(), task_operands=()):
     def body(total, ins, results):
         x_ref, gain_ref = ins
         x_out, a_out = results
@@ -212,7 +565,10 @@
         return lambda: None, finish
 
     shape = partial.shape
-    return sum_call(body, f"forward_sum_{cid}", cid, partial, (rows_in, gain.reshape(1, -1)), ((shape, jnp.float32), (shape, jnp.bfloat16)))
+    return sum_call(
+        body, cid, partial, (rows_in, gain.reshape(1, -1)),
+        ((shape, jnp.float32), (shape, jnp.bfloat16)), tasks, task_operands,
+    )
 
 
 def turn_sum(cid, partial, rows_in, gain, cotangent):
@@ -236,14 +592,14 @@
         return start, finish
 
     shape = partial.shape
-    out, d, half, gain_grad = sum_call(
-        body, f"turn_sum_{cid}", cid, partial, (rows_in, gain.reshape(1, -1), cotangent),
-        ((shape, jnp.bfloat16), (shape, jnp.float32), (shape, jnp.bfloat16), ((8, shape[1]), jnp.float32)),
-    )
-    return out, d, half, jnp.sum(gain_grad, axis=0)
-
-
-def backward_sum(cid, partial, rows_in, gain, upstream, scale):
+    (out, d, half, gain_grad), _ = sum_call(
+        body, cid, partial, (rows_in, gain.reshape(1, -1), cotangent),
+        ((shape, jnp.bfloat16), (shape, jnp.float32), (shape, jnp.bfloat16), ((8, shape[1]), jnp.float32)), (), (),
+    )
+    return out, d, half, gain_grad
+
+
+def backward_sum(cid, partial, rows_in, gain, upstream, scale, tasks=(), task_operands=()):
     def body(total, ins, results):
         x_ref, gain_ref, up_ref = ins
         d_ref, half_ref, gain_grad_ref = results
@@ -262,11 +618,162 @@
         return start, finish
 
     shape = partial.shape
-    d, half, gain_grad = sum_call(
-        body, f"backward_sum_{cid}", cid, partial, (rows_in, gain.reshape(1, -1), upstream),
-        ((shape, jnp.float32), (shape, jnp.bfloat16), ((8, shape[1]), jnp.float32)),
-    )
-    return d, half, jnp.sum(gain_grad, axis=0)
+    return sum_call(
+        body, cid, partial, (rows_in, gain.reshape(1, -1), upstream),
+        ((shape, jnp.float32), (shape, jnp.bfloat16), ((8, shape[1]), jnp.float32)), tasks, task_operands,
+    )
+
+
+def context_places():
+    along = lax.axis_index(CONTEXT)
+    deep, core = along // 2, along % 2
+    return deep, core, {CONTEXT: (1 - deep) * 2 + core}, {CONTEXT: deep * 2 + 1 - core}
+
+
+def context_call(kernel, cid, operands, outs, scratch, ready=20_000_000_000):
+    vmem = pl.BlockSpec(memory_space=pltpu.VMEM)
+    return pl.pallas_call(
+        kernel,
+        out_shape=tuple(jax.ShapeDtypeStruct(shape, kind) for shape, kind in outs),
+        in_specs=[vmem] * len(operands),
+        out_specs=(vmem,) * len(outs),
+        scratch_shapes=scratch,
+        compiler_params=pltpu.CompilerParams(collective_id=cid, has_side_effects=True, vmem_limit_bytes=12 << 20),
+        cost_estimate=pl.CostEstimate(flops=ready, bytes_accessed=30_000_000, transcendentals=0),
+        name=f"call_{cid}",
+    )(*operands)
+
+
+def gather_context(cid, first, second):
+    rows, width = first.shape
+
+    def kernel(first_ref, second_ref, first_out, second_out, send, recv, own_sem):
+        deep, core, to_y, to_core = context_places()
+        greet([to_y, to_core])
+
+        def block(ref, which):
+            return ref.at[pl.ds(pl.multiple_of(which * rows, rows), rows)]
+
+        def copy(index, source, target, device):
+            return pltpu.make_async_remote_copy(
+                src_ref=source, dst_ref=target, send_sem=send.at[index], recv_sem=recv.at[index],
+                device_id=device, device_id_type=MESH_ID,
+            )
+
+        own, beyond = deep * 2 + core, (1 - deep) * 2 + core
+        pairs = ((first_ref, first_out), (second_ref, second_out))
+        out_y = [copy(i, source, block(full, own), to_y) for i, (source, full) in enumerate(pairs)]
+        out_core = [copy(2 + i, source, block(full, own), to_core) for i, (source, full) in enumerate(pairs)]
+        passed = [copy(4 + i, block(full, beyond), block(full, beyond), to_core) for i, (source, full) in enumerate(pairs)]
+        mine = [pltpu.make_async_copy(source, block(full, own), own_sem.at[i]) for i, (source, full) in enumerate(pairs)]
+        for move in out_y + out_core + mine:
+            move.start()
+        for arrived, onward in zip(out_y, passed):
+            arrived.wait_recv()
+            onward.start()
+        for move in out_core + passed:
+            move.wait_recv()
+        for move in mine:
+            move.wait()
+        for move in out_y + out_core + passed:
+            move.wait_send()
+
+    full = ((4 * rows, width), first.dtype)
+    return context_call(
+        kernel, cid, (first, second), (full, full),
+        [pltpu.SemaphoreType.DMA((6,)), pltpu.SemaphoreType.DMA((6,)), pltpu.SemaphoreType.DMA((2,))],
+    )
+
+
+def scatter_context(cid, first, second):
+    rows, width = first.shape
+    part = width // 4
+
+    def kernel(first_ref, second_ref, first_out, second_out, from_core, pair, from_y, send, recv):
+        deep, core, to_y, to_core = context_places()
+        greet([to_y, to_core])
+
+        def block(ref, which):
+            return ref.at[:, pl.ds(pl.multiple_of(which * part, 128), part)]
+
+        def copy(index, source, target, device):
+            return pltpu.make_async_remote_copy(
+                src_ref=source, dst_ref=target, send_sem=send.at[index], recv_sem=recv.at[index],
+                device_id=device, device_id_type=MESH_ID,
+            )
+
+        wide = lambda ref: ref[...].astype(jnp.float32)
+        sources, targets = (first_ref, second_ref), (first_out, second_out)
+        far, close = 1 - deep, deep
+        inner, outer = [], []
+        for i, source in enumerate(sources):
+            for j, at in enumerate((far, close)):
+                inner.append(copy(2 * i + j, block(source, at * 2 + 1 - core), from_core.at[2 * i + j], to_core))
+            outer.append(copy(4 + i, pair.at[2 * i], from_y.at[i], to_y))
+        for at in (0, 2, 1, 3):
+            inner[at].start()
+        for i, source in enumerate(sources):
+            inner[2 * i].wait_recv()
+            pair[2 * i] = (wide(block(source, far * 2 + core)) + wide(from_core.at[2 * i])).astype(jnp.bfloat16)
+            outer[i].start()
+        for i, source in enumerate(sources):
+            inner[2 * i + 1].wait_recv()
+            pair[2 * i + 1] = (wide(block(source, close * 2 + core)) + wide(from_core.at[2 * i + 1])).astype(jnp.bfloat16)
+        for i, target in enumerate(targets):
+            outer[i].wait_recv()
+            target[...] = (wide(pair.at[2 * i + 1]) + wide(from_y.at[i])).astype(target.dtype)
+        for move in inner + outer:
+            move.wait_send()
+
+    out = ((rows, part), jnp.bfloat16)
+    piece = (rows, part)
+    return context_call(
+        kernel, cid, (first, second), (out, out),
+        [
+            pltpu.VMEM((4,) + piece, jnp.bfloat16),
+            pltpu.VMEM((4,) + piece, jnp.bfloat16),
+            pltpu.VMEM((2,) + piece, jnp.bfloat16),
+            pltpu.SemaphoreType.DMA((6,)),
+            pltpu.SemaphoreType.DMA((6,)),
+        ],
+    )
+
+
+def line_total(cid, value):
+    count = lax.axis_size(TENSOR)
+
+    def kernel(value_ref, out_ref, slots, send, recv):
+        at = lax.axis_index(TENSOR)
+        others = [{TENSOR: (at + step) % count} for step in range(1, count)]
+        greet(others)
+        moves = [
+            pltpu.make_async_remote_copy(
+                src_ref=value_ref, dst_ref=slots.at[step], send_sem=send.at[step], recv_sem=recv.at[step],
+                device_id=device, device_id_type=MESH_ID,
+            )
+            for step, device in enumerate(others)
+        ]
+        for move in moves:
+            move.start()
+        for move in moves:
+            move.wait_recv()
+        total = value_ref[...]
+        for step in range(count - 1):
+            total = total + slots[step]
+        out_ref[...] = total
+        for move in moves:
+            move.wait_send()
+
+    (total,) = context_call(
+        kernel, cid, (value,), ((value.shape, jnp.float32),),
+        [
+            pltpu.VMEM((count - 1,) + value.shape, jnp.float32),
+            pltpu.SemaphoreType.DMA((count - 1,)),
+            pltpu.SemaphoreType.DMA((count - 1,)),
+        ],
+        5_000_000_000,
+    )
+    return total
 
 
 def feed(normed, weight_in, weight_out):
@@ -369,7 +876,7 @@
                 pltpu.VMEM((QB, keys), jnp.bfloat16),
             ],
         ),
-        compiler_params=pltpu.CompilerParams(vmem_limit_bytes=40 << 20),
+        compiler_params=pltpu.CompilerParams(vmem_limit_bytes=20 << 20),
         cost_estimate=pl.CostEstimate(flops=8 * rows * keys * width, bytes_accessed=4 * (keys + rows) * width, transcendentals=0),
         name="attention_forward",
     )(position.reshape(1), q, k, v, span)
@@ -489,7 +996,7 @@
                 pltpu.VMEM((two, keys), jnp.float32),
             ],
         ),
-        compiler_params=pltpu.CompilerParams(vmem_limit_bytes=40 << 20),
+        compiler_params=pltpu.CompilerParams(vmem_limit_bytes=20 << 20),
         cost_estimate=pl.CostEstimate(flops=20 * rows * keys * width, bytes_accessed=8 * (keys + rows) * width, transcendentals=0),
         name="attention_backward",
     )(position.reshape(1), q, q_t, g, g_t, o, lse, k, v, span)
@@ -507,10 +1014,7 @@
     projected = jnp.einsum(
         "td,kde->kte", normed, weight_in, preferred_element_type=jnp.float32
     ).astype(jnp.bfloat16)
-    key_rows, value_rows = (
-        lax.all_gather(projected[1], "context", axis=0, tiled=True),
-        lax.all_gather(projected[2], "context", axis=0, tiled=True),
-    )
+    key_rows, value_rows = gather_context(10, projected[1], projected[2])
     queries = projected[0] * jnp.bfloat16(1.0 / math.sqrt(HEAD_DIM))
     span = span_table(relative)
     mixed, log_total = attention_forward(position, queries, key_rows, value_rows, span)
@@ -527,12 +1031,16 @@
     query_grad, key_grad, value_grad, table_grad = attention_backward(
         position, queries, queries.T, mixed_grad, mixed_grad.T, mixed, log_total, key_rows, value_rows, span
     )
-    key_grad = lax.psum_scatter(key_grad, "context", scatter_dimension=1, tiled=True)
-    value_grad = lax.psum_scatter(value_grad, "context", scatter_dimension=1, tiled=True)
+    key_grad, value_grad = scatter_context(11, key_grad, value_grad)
     stacked = jnp.stack([query_grad, key_grad.T, value_grad.T])
     grad_in = jnp.einsum("td,kte->kde", normed, stacked, preferred_element_type=jnp.float32)
     partial_sum = jnp.einsum("kte,kde->td", stacked, weight_in, preferred_element_type=jnp.float32)
     return (partial_sum.astype(jnp.bfloat16), table_grad, grad_in, grad_out)
+
+
+def channel_sums(cid, first, second):
+    total = line_total(cid, jnp.concatenate([first, second]).reshape(-1, 128)).reshape(2, -1)
+    return total[0], total[1]
 
 
 def conv_forward(normed, weight_in, weight_out, depthwise, gain_middle):
@@ -540,14 +1048,12 @@
     gated = gate_unit(projected[0], projected[1])
     rows_here = gated.shape[0]
     reach_rows = depthwise.shape[0] - 1
-    edge_rows = shifted_2(gated[rows_here - reach_rows :], "context", 1)
+    edge_rows = shifted_2(gated[rows_here - reach_rows :], CONTEXT, 1)
     padded = jnp.concatenate([edge_rows, gated], axis=0)
     mixed = depthwise[0] * padded[0:rows_here]
     for offset in range(1, reach_rows + 1):
         mixed = mixed + depthwise[offset] * padded[offset : offset + rows_here]
-    row_sums, row_squares = lax.psum(
-        (jnp.sum(mixed, axis=1), jnp.sum(mixed * mixed, axis=1)), "tensor"
-    )
+    row_sums, row_squares = channel_sums(12, jnp.sum(mixed, axis=1), jnp.sum(mixed * mixed, axis=1))
     row_mean = row_sums / D
     inverse = lax.rsqrt(row_squares / D - row_mean * row_mean + epsilon)
     scaled = (mixed - row_mean[:, None]) * inverse[:, None]
@@ -568,13 +1074,11 @@
     shaped_grad = pullback(dot_outer(branch_grad, weight_out))[0]
     middle_grad = jnp.sum(shaped_grad * scaled, axis=0)
     scaled_grad = shaped_grad * gain_middle
-    first_sum, second_sum = lax.psum(
-        (jnp.sum(scaled_grad, axis=1), jnp.sum(scaled_grad * scaled, axis=1)), "tensor"
-    )
+    first_sum, second_sum = channel_sums(13, jnp.sum(scaled_grad, axis=1), jnp.sum(scaled_grad * scaled, axis=1))
     mixed_grad = inverse[:, None] * (
         scaled_grad - first_sum[:, None] / D - scaled * (second_sum[:, None] / D)
     )
-    next_rows = shifted_2(mixed_grad[:reach_rows], "context", -1)
+    next_rows = shifted_2(mixed_grad[:reach_rows], CONTEXT, -1)
     padded_grad = jnp.concatenate([mixed_grad, next_rows], axis=0)
     gated_grad = depthwise[reach_rows] * padded_grad[0:rows_here]
     for offset in range(1, reach_rows + 1):
@@ -613,115 +1117,164 @@
     gain_final,
     cotangent,
 ):
-    position = lax.axis_index("context")
+    position = lax.axis_index(CONTEXT)
     start_rows = inputs[0]
-    first_in, first_out = fetch(first_in[None], first_out)
-    attend_in, attend_out = fetch(attend_in, attend_out)
-    convolve_in, convolve_out = fetch(convolve_in, convolve_out)
-    second_in, second_out = fetch(second_in[None], second_out)
-    first_in, second_in = first_in[0], second_in[0]
+    small_plane = lax.axis_size(CLIPS) == 2
+    weights = {
+        FIRST: (first_in, first_out),
+        ATTEND: (attend_in, attend_out),
+        CONVOLVE: (convolve_in, convolve_out),
+        SECOND: (second_in, second_out),
+    }
+    held, grads = {}, {}
+
+    def collecting(name):
+        if not small_plane:
+            return (), ()
+        pair = tuple(weight.astype(jnp.bfloat16) for weight in weights[name])
+        return tuple(Gather(wide, weight.shape) for wide, weight in zip((False, True), pair)), pair
+
+    def collect(name, gathered):
+        held[name] = gathered if small_plane else fetch(*weights[name])
+
+    def spreading(grad_in, grad_out):
+        if not small_plane:
+            return (), ()
+        pair = (grad_in.astype(jnp.bfloat16), grad_out.astype(jnp.bfloat16))
+        return tuple(Scatter(wide, grad.shape) for wide, grad in zip((False, True), pair)), pair
+
+    def with_small(rest, kind, value):
+        if not small_plane:
+            return rest
+        return rest[0] + (kind(value.shape),), rest[1] + (value,)
+
+    def spread(name, scattered, grad_in, grad_out):
+        grads[name] = scattered if small_plane else send_grads(grad_in, grad_out)
+
+    tasks, pair = collecting(FIRST)
+    collect(FIRST, plane_call(9, tasks, pair) if small_plane else None)
     normed = layer_norm(start_rows.astype(jnp.float32), gain_first).astype(jnp.bfloat16)
-    branch, first_saved = feed(normed, first_in, first_out)
-    after_first, normed = forward_sum(1, branch, start_rows, gain_attend, 0.5)
-    branch, attend_saved = attend_forward(normed, attend_in, attend_out, relative, position)
-    after_attend, normed = forward_sum(2, branch, after_first, gain_convolve, 1.0)
-    branch, convolve_saved = conv_forward(normed, convolve_in, convolve_out, depthwise, gain_middle)
-    after_convolve, normed = forward_sum(3, branch, after_attend, gain_second, 1.0)
-    branch, second_saved = feed(normed, second_in, second_out)
+    branch, first_saved = feed(normed, *held[FIRST])
+    (after_first, normed), got = forward_sum(1, branch, start_rows, gain_attend, 0.5, *collecting(ATTEND))
+    collect(ATTEND, got)
+    branch, attend_saved = attend_forward(normed, *held[ATTEND], relative, position)
+    (after_attend, normed), got = forward_sum(2, branch, after_first, gain_convolve, 1.0, *collecting(CONVOLVE))
+    collect(CONVOLVE, got)
+    branch, convolve_saved = conv_forward(normed, *held[CONVOLVE], depthwise, gain_middle)
+    (after_convolve, normed), got = forward_sum(3, branch, after_attend, gain_second, 1.0, *collecting(SECOND))
+    collect(SECOND, got)
+    branch, second_saved = feed(normed, *held[SECOND])
     final_out, upstream, branch_grad, grad_final = turn_sum(4, branch, after_convolve, gain_final, cotangent[0])
-    branch, grad_in, grad_out = feed_back(second_in, second_out, second_saved, branch_grad)
-    second_grads = send_grads(grad_in[None], grad_out)
-    upstream, branch_grad, grad_gain_second = backward_sum(5, branch, after_convolve, gain_second, upstream, 1.0)
-    branch, grad_in, grad_out, grad_middle, grad_depth = conv_backward(
-        convolve_in, convolve_out, depthwise, gain_middle, convolve_saved, branch_grad
-    )
-    convolve_grads = send_grads(grad_in, grad_out)
-    upstream, branch_grad, grad_gain_convolve = backward_sum(6, branch, after_attend, gain_convolve, upstream, 1.0)
-    branch, table_grad, grad_in, grad_out = attend_backward(attend_in, attend_out, position, attend_saved, branch_grad)
-    attend_grads = send_grads(grad_in, grad_out)
-    upstream, branch_grad, grad_gain_attend = backward_sum(7, branch, after_first, gain_attend, upstream, 0.5)
-    branch, grad_in, grad_out = feed_back(first_in, first_out, first_saved, branch_grad)
-    first_grads = send_grads(grad_in[None], grad_out)
-    upstream, branch_grad, grad_gain_first = backward_sum(8, branch, start_rows, gain_first, upstream, 1.0)
-    table_grad = lax.psum(table_grad, "tensor")
-    smalls = lax.psum(
-        (
-            grad_gain_first,
-            grad_gain_attend,
-            table_grad,
-            grad_gain_convolve,
-            grad_depth,
-            grad_middle,
-            grad_gain_second,
-            grad_final,
-        ),
-        ("clips", "context"),
-    )
+    branch, *pair = feed_back(*held[SECOND], second_saved, branch_grad)
+    (upstream, branch_grad, grad_gain_second), got = backward_sum(
+        5, branch, after_convolve, gain_second, upstream, 1.0, *spreading(*pair)
+    )
+    spread(SECOND, got, *pair)
+    branch, *pair, grad_middle, grad_depth = conv_backward(
+        *held[CONVOLVE], depthwise, gain_middle, convolve_saved, branch_grad
+    )
+    (upstream, branch_grad, grad_gain_convolve), got = backward_sum(
+        6, branch, after_attend, gain_convolve, upstream, 1.0, *spreading(*pair)
+    )
+    spread(CONVOLVE, got, *pair)
+    branch, table_grad, *pair = attend_backward(*held[ATTEND], position, attend_saved, branch_grad)
+    shared = jnp.pad(table_grad.reshape(-1), (0, -table_grad.size % 1024)).reshape(-1, 128)
+    (upstream, branch_grad, grad_gain_attend), got = backward_sum(
+        7, branch, after_first, gain_attend, upstream, 0.5, *with_small(spreading(*pair), LineSum, shared)
+    )
+    spread(ATTEND, got[:2], *pair)
+    branch, *pair = feed_back(*held[FIRST], first_saved, branch_grad)
+    gains = [
+        jnp.sum(part, axis=0) for part in (grad_gain_attend, grad_gain_convolve, grad_gain_second, grad_final)
+    ]
+    smalls = [*gains, grad_middle, grad_depth.reshape(-1)]
+    sizes = [part.shape[0] for part in smalls]
+    packed = jnp.concatenate(smalls).reshape(-1, 128)
+    if small_plane:
+        packed = jnp.concatenate([packed, got[2]], axis=0)
+    (upstream, branch_grad, grad_gain_first), got = backward_sum(
+        8, branch, start_rows, gain_first, upstream, 1.0, *with_small(spreading(*pair), PlaneSum, packed)
+    )
+    spread(FIRST, got[:2], *pair)
+    grad_gain_first = jnp.sum(grad_gain_first, axis=0)
+    if small_plane:
+        packed = got[2].reshape(-1)
+        (grad_gain_first,) = plane_call(14, (PlaneSum((8, 128)),), (grad_gain_first.reshape(8, 128),))
+        grad_gain_first = grad_gain_first.reshape(-1)
+        table_grad = packed[sum(sizes) : sum(sizes) + table_grad.size].reshape(table_grad.shape)
+    else:
+        table_grad = lax.psum(table_grad, (CLIPS, CONTEXT, TENSOR))
+        packed, grad_gain_first = lax.psum((packed.reshape(-1), grad_gain_first), (CLIPS, CONTEXT))
+    smalls, at = [], 0
+    for size in sizes:
+        smalls.append(packed[at : at + size])
+        at += size
+    grad_depth = smalls[5].reshape(depthwise.shape)
     return (
         final_out[None],
         upstream[None],
+        grad_gain_first,
+        grads[FIRST][0],
+        grads[FIRST][1],
         smalls[0],
-        first_grads[0][0],
-        first_grads[1],
+        grads[ATTEND][0],
+        grads[ATTEND][1],
+        table_grad,
         smalls[1],
-        attend_grads[0],
-        attend_grads[1],
+        grads[CONVOLVE][0],
+        grad_depth,
+        smalls[4],
+        grads[CONVOLVE][1],
         smalls[2],
+        grads[SECOND][0],
+        grads[SECOND][1],
         smalls[3],
-        convolve_grads[0],
-        smalls[4],
-        smalls[5],
-        convolve_grads[1],
-        smalls[6],
-        second_grads[0][0],
-        second_grads[1],
-        smalls[7],
     )
 
 
 def solution(mesh):
     placed = (
-        P("clips", "context", None),
+        P(CLIPS, CONTEXT, None),
         P(),
-        P(("clips", "context"), "tensor"),
-        P("tensor", ("clips", "context")),
+        P((CLIPS, CONTEXT), TENSOR),
+        P(TENSOR, (CLIPS, CONTEXT)),
         P(),
-        P(None, ("clips", "context"), "tensor"),
-        P("tensor", ("clips", "context")),
+        P(None, (CLIPS, CONTEXT), TENSOR),
+        P(TENSOR, (CLIPS, CONTEXT)),
         P(),
         P(),
-        P(None, ("clips", "context"), "tensor"),
-        P(None, "tensor"),
-        P("tensor"),
-        P("tensor", ("clips", "context")),
+        P(None, (CLIPS, CONTEXT), TENSOR),
+        P(None, TENSOR),
+        P(TENSOR),
+        P(TENSOR, (CLIPS, CONTEXT)),
         P(),
-        P(("clips", "context"), "tensor"),
-        P("tensor", ("clips", "context")),
+        P((CLIPS, CONTEXT), TENSOR),
+        P(TENSOR, (CLIPS, CONTEXT)),
         P(),
-        P("clips", "context", None),
+        P(CLIPS, CONTEXT, None),
     )
     return jax.shard_map(
         local,
         mesh=mesh,
         in_specs=placed,
         out_specs=(
-            P("clips", "context", None),
-            P("clips", "context", None),
+            P(CLIPS, CONTEXT, None),
+            P(CLIPS, CONTEXT, None),
             P(),
-            P(("clips", "context"), "tensor"),
-            P("tensor", ("clips", "context")),
+            P((CLIPS, CONTEXT), TENSOR),
+            P(TENSOR, (CLIPS, CONTEXT)),
             P(),
-            P(None, ("clips", "context"), "tensor"),
-            P("tensor", ("clips", "context")),
+            P(None, (CLIPS, CONTEXT), TENSOR),
+            P(TENSOR, (CLIPS, CONTEXT)),
             P(),
             P(),
-            P(None, ("clips", "context"), "tensor"),
-            P(None, "tensor"),
-            P("tensor"),
-            P("tensor", ("clips", "context")),
+            P(None, (CLIPS, CONTEXT), TENSOR),
+            P(None, TENSOR),
+            P(TENSOR),
+            P(TENSOR, (CLIPS, CONTEXT)),
             P(),
-            P(("clips", "context"), "tensor"),
-            P("tensor", ("clips", "context")),
+            P((CLIPS, CONTEXT), TENSOR),
+            P(TENSOR, (CLIPS, CONTEXT)),
             P(),
         ),
         check_vma=False,

time: 911 us -> 544 us (0.60)
  waiting for transfers between devices: 356 us -> 0.23 us
  Pallas kernels: 311 us -> 414 us
  blocking collectives: 62.9 us -> 0 us
  matrix products: 55.5 us -> 30.9 us
  local copies, waits for them, and re-layouts: 64.3 us -> 50.4 us
  between operations: 16.8 us -> 3.5 us
    unnamed x25 -> x0, waiting for transfers between devices: 119 us -> none
    reduce_scatter x4 -> x0, waiting for transfers between devices: 104 us -> none  [the longest x2 77 us: scatter_sum(): lax.psum_scatter(grad.astype(jnp.bfloat16), ('clips', 'context'), scatter...]
    all_gather x8 -> x0, waiting for transfers between devices: 75.6 us -> none  [the longest x4 28.5 us: fetch(): lax.all_gather(weight_in.astype(jnp.bfloat16), ('clips', 'context'), axis...]
    pallas_call x0 -> x6, Pallas kernels: none -> 71.6 us  [the longest x4 41.8 us: context_call(): pl.pallas_call(kernel, out_shape=tuple((jax.ShapeDtypeStruct(shape, kind)...]
    psum x1 -> x0, waiting for transfers between devices: 56.4 us -> none  [local(): lax.psum((grad_gain_first, grad_gain_attend, table_grad, grad_gain_convol...]
    psum x3 -> x0, blocking collectives: 39.7 us -> none  [the longest x1 18.7 us: local(): table_grad = lax.psum(table_grad, 'tensor')]
    pallas_call x8, Pallas kernels: 264 us -> 296 us  [sum_call(): pl.pallas_call(kernel, out_shape=tuple((jax.ShapeDtypeStruct(shape, kind)...]
    all_gather x2 -> x0, blocking collectives: 23.2 us -> none  [fetch(): lax.all_gather(weight_out.astype(jnp.bfloat16), ('clips', 'context'), axi...]
  transfers between devices with their start and end apart: 21 -> 2, of which waited for: 12 -> 1; matrix products, arithmetic and copies ran while one was open for 10% -> 2% of each run, Pallas kernels for 21% -> 0%
where the time goes in v3:
time: 544 us; the launch traced here: 535 us
  Pallas kernels  414 us (76%)
  local copies, waits for them, and re-layouts  50.4 us (9%)
  other arithmetic  33.3 us (6%)
  matrix products  30.9 us (6%)
    pallas_call x8, Pallas kernels, sum_call(): pl.pallas_call(kernel, out_shape=tuple((jax.ShapeDtypeStruct(shape, kind)...  296 us
    pallas_call x4, Pallas kernels, context_call(): pl.pallas_call(kernel, out_shape=tuple((jax.ShapeDtypeStruct(shape, kind)...  41.8 us
    unnamed x340, local copies, waits for them, and re-layouts  38.6 us
    pallas_call x1, Pallas kernels, attention_backward(): pl.pallas_call(backward_kernel, out_shape=(jax.ShapeDtypeStruct((rows, wi...  30.1 us
    pallas_call x2, Pallas kernels, plane_call(): pl.pallas_call(kernel, out_shape=tuple((jax.ShapeDtypeStruct(shape, kind)...  29.8 us
    pallas_call x1, Pallas kernels, attention_forward(): pl.pallas_call(forward_kernel, out_shape=(jax.ShapeDtypeStruct((rows, wid...  16 us
    another operation x2, other arithmetic, conv_backward(): stacked = jnp.stack([unit_grad, gate_grad]).astype(jnp.bfloat16)  10.9 us
  transfers between devices with their start and end apart: 2, of which 1 were waited for; matrix products, arithmetic and copies ran while one was open for 2% of the time, Pallas kernels for 0%

profile of v3, /device:TPU:0, one launch (start us, length us, event | category | flops | bytes accessed | tf_op | source)
XLA Modules:
  0.0 535.1 jit_solution(9107502367406578362)
XLA Ops:
  0.7 1.6 convert_reduce_fusion
  2.3 1.6 fusion.2
  4.3 23.3 %call_9.1 = (bf16[1024,1024]{1,0:T(8,128)(2,1)S(1)}, bf16[1024,1024]{1,0:T(8,128)(2,1)S(1)}) custom-call(bf16[128,1024]{1,0:T(8,128)(2,1)S(1)} %convert_element_type.116.refs_0_, bf16[1024,128]{1,0:T(8,128)(2,1)S(1)} %convert_element_type.117.refs_1_), custom_call_target="tpu_custom_call" | custom-call | flops 30000001024 | bytes 50000000 | tf_op jit(solution)/shard_map/call_9/pallas_call | solution.py:385
  27.7 1.3 fusion.156
  29.6 1.3 convolution_convert_fusion.10.partial_ref
  31.0 35.5 %call_1.1 = (f32[512,1024]{1,0:T(8,128)S(1)}, bf16[512,1024]{1,0:T(8,128)(2,1)S(1)}, bf16[3,1024,256]{2,1,0:T(8,128)(2,1)S(1)}, bf16[256,1024]{1,0:T(8,128)(2,1)S(1)}) custom-call(bf16[512,1024]{1,0:T(8,128)(2,1)S(1)} %convolution_convert_fusion.10.partial_ref, bf16[512,1024]{1,0:T(8,128)(2,1)S(1)} %bitcast.210, f32[1,1024]{1,0:T(1,128)S(1)} %bitcast.226, ...), custom_call_target="tpu_custom_call" | custom-call | flops 60000002048 | bytes 100000000 | tf_op jit(solution)/shard_map/call_1/pallas_call | solution.py:540
  66.5 1.3 copy-done.69
  67.8 1.0 fusion.13
  70.1 15.0 %call_10.1 = (bf16[2048,256]{1,0:T(8,128)(2,1)S(1)}, bf16[2048,256]{1,0:T(8,128)(2,1)S(1)}) custom-call(bf16[512,256]{1,0:T(8,128)(2,1)S(1)} %copy.56.first_ref, bf16[512,256]{1,0:T(8,128)(2,1)S(1)} %copy.57.second_ref), custom_call_target="tpu_custom_call" | custom-call | flops 20000000000 | bytes 30000000 | tf_op jit(solution)/shard_map/call_10/pallas_call | solution.py:635
  85.2 16.0 %attention_forward.1 = (bf16[512,256]{1,0:T(8,128)(2,1)S(1)}, f32[512,256]{1,0:T(8,128)S(1)}) custom-call(s32[1]{0:T(128)} %bitcast.1.pos_ref, bf16[512,256]{1,0:T(8,128)(2,1)S(1)} %copy.59.q_ref, bf16[2048,256]{1,0:T(8,128)(2,1)S(1)} %get-tuple-element.72.k_ref, bf16[2048,256]{1,0:T(8,128)(2,1)S(1)} %get-tuple-element.73.v_ref, ...), custom_call_target="tpu_custom_call" | custom-call | flops 2147483648 | bytes 2621440 | tf_op jit(solution)/shard_map/attention_forward/pallas_call | solution.py:862
  103.1 34.7 %call_2.1 = (f32[512,1024]{1,0:T(8,128)S(1)}, bf16[512,1024]{1,0:T(8,128)(2,1)S(1)}, bf16[2,1024,256]{2,1,0:T(8,128)(2,1)S(1)}, bf16[256,1024]{1,0:T(8,128)(2,1)S(1)}) custom-call(bf16[512,1024]{1,0:T(8,128)(2,1)S(1)} %convolution_convert_fusion.9.partial_ref, f32[512,1024]{1,0:T(8,128)S(1)} %copy-done.70, f32[1,1024]{1,0:T(1,128)S(1)} %bitcast.224, ...), custom_call_target="tpu_custom_call" | custom-call | flops 60000002048 | bytes 100000000 | tf_op jit(solution)/shard_map/call_2/pallas_call | solution.py:540
  139.4 1.6 collective-permute-start
  141.7 6.5 %fusion.158 = (f32[512]{0:T(512)S(1)}, f32[512]{0:T(512)S(1)}, f32[512,256]{0,1:T(8,128)S(1)}) fusion(f32[512,256]{0,1:T(8,128)S(1)} %fusion.144, f32[256]{0:T(256)S(1)} %bitcast.294, f32[30,256]{0,1:T(8,128)S(1)} %collective-permute-done, f32[256]{0:T(256)S(1)} %bitcast.296, f32[256]{0:T(256)S(1)} %bitcast.238, f32[256]{0:T(256)S(1)} %bitcast.240, ...), kind=kLoop, calls=%fused_computation.381 | loop fusion | flops 12319744 | bytes 1115136 | tf_op jit(solution)/shard_map/reduce_sum | solution.py:1056
  148.2 5.5 %call_12.1 = f32[8,128]{1,0:T(8,128)S(1)} custom-call(f32[8,128]{1,0:T(8,128)S(1)} %pad_maximum_fusion.10.value_ref), custom_call_target="tpu_custom_call" | custom-call | flops 5000000000 | bytes 30000000 | tf_op jit(solution)/shard_map/call_12/pallas_call | solution.py:635
  154.8 37.9 %call_3.1 = (f32[512,1024]{1,0:T(8,128)S(1)}, bf16[512,1024]{1,0:T(8,128)(2,1)S(1)}, bf16[1024,1024]{1,0:T(8,128)(2,1)S(1)}, bf16[1024,1024]{1,0:T(8,128)(2,1)S(1)}) custom-call(bf16[512,1024]{1,0:T(8,128)(2,1)S(1)} %convolution_convert_fusion.8.partial_ref, f32[512,1024]{1,0:T(8,128)S(1)} %get-tuple-element.80.refs_0_, f32[1,1024]{1,0:T(1,128)S(1)} %bitcast.222, ...), custom_call_target="tpu_custom_call" | custom-call | flops 60000002048 | bytes 100000000 | tf_op jit(solution)/shard_map/call_3/pallas_call | solution.py:540
  192.7 1.3 fusion.163
  194.0 1.3 convolution_convert_fusion.7.partial_ref
  195.4 30.6 %call_4.1 = (bf16[512,1024]{1,0:T(8,128)(2,1)S(1)}, f32[512,1024]{1,0:T(8,128)S(1)}, bf16[512,1024]{1,0:T(8,128)(2,1)S(1)}, f32[8,1024]{1,0:T(8,128)S(1)}) custom-call(bf16[512,1024]{1,0:T(8,128)(2,1)S(1)} %convolution_convert_fusion.7.partial_ref, f32[512,1024]{1,0:T(8,128)S(1)} %get-tuple-element.84.refs_0_, f32[1,1024]{1,0:T(1,128)S(1)} %bitcast.221, ...), custom_call_target="tpu_custom_call" | custom-call | flops 60000002048 | bytes 100000000 | tf_op jit(solution)/shard_map/call_4/pallas_call | solution.py:540
  226.0 1.7 fusion.7
  227.7 1.3 convolution_convert_fusion.6.partial_ref
  229.0 1.3 convolution_convert_fusion.3.refs_3_
  230.3 1.4 convolution_convert_fusion.2.refs_4_
  231.7 47.3 %call_5.1 = (f32[512,1024]{1,0:T(8,128)S(1)}, bf16[512,1024]{1,0:T(8,128)(2,1)S(1)}, f32[8,1024]{1,0:T(8,128)S(1)}, f32[128,1024]{1,0:T(8,128)S(1)}, f32[1024,128]{1,0:T(8,128)S(1)}) custom-call(bf16[512,1024]{1,0:T(8,128)(2,1)S(1)} %convolution_convert_fusion.6.partial_ref, f32[512,1024]{1,0:T(8,128)S(1)} %get-tuple-element.84.refs_0_, ...), custom_call_target="tpu_custom_call" | custom-call | flops 60000002048 | bytes 100000000 | tf_op jit(solution)/shard_map/call_5/pallas_call | solution.py:540
  279.1 1.5 multiply_reduce_fusion.31
  281.4 5.5 %call_13.1 = f32[8,128]{1,0:T(8,128)S(1)} custom-call(f32[8,128]{1,0:T(8,128)S(1)} %pad_maximum_fusion.11.value_ref), custom_call_target="tpu_custom_call" | custom-call | flops 5000000000 | bytes 30000000 | tf_op jit(solution)/shard_map/call_13/pallas_call | solution.py:635
  286.9 2.8 multiply_reduce_fusion.1
  290.6 1.3 collective-permute-start.1
  291.9 2.8 multiply_reduce_fusion.19
  294.6 2.8 multiply_reduce_fusion.10
  297.4 1.3 multiply_reduce_fusion.28
  299.9 3.0 stack.158
  303.7 10.7 %fusion.145 = (bf16[1,512,256]{1,2,0:T(8,128)(2,1)S(1)}, f32[512,256]{0,1:T(8,128)S(1)}) fusion(f32[2,512,256]{1,2,0:T(8,128)S(1)} %copy-done.79, f32[30,256]{0,1:T(8,128)} %collective-permute-done.1, f32[512,256]{0,1:T(8,128)S(1)} %get-tuple-element.172, f32[256]{0:T(256)S(1)} %bitcast.237, f32[256]{0:T(256)S(1)} %bitcast.275, f32[256]{0:T(256)} %bitcast.293, ...), kind=kLoop, calls=%fused_computation.337 | loop fusion | flops 12582912 | bytes 1897472 | tf_op jit(solution)/shard_map/stack | solution.py:1094
  317.4 37.5 %call_6.1 = (f32[512,1024]{1,0:T(8,128)S(1)}, bf16[512,1024]{1,0:T(8,128)(2,1)S(1)}, f32[8,1024]{1,0:T(8,128)S(1)}, f32[2,128,256]{2,1,0:T(8,128)S(1)}, f32[256,128]{1,0:T(8,128)S(1)}) custom-call(bf16[512,1024]{1,0:T(8,128)(2,1)S(1)} %bitcast_convert_fusion.1.partial_ref, f32[512,1024]{1,0:T(8,128)S(1)} %copy-done.75, f32[1,1024]{1,0:T(1,128)S(1)} %bitcast.225, ...), custom_call_target="tpu_custom_call" | custom-call | flops 60000002048 | bytes 100000000 | tf_op jit(solution)/shard_map/call_6/pallas_call | solution.py:540
  355.5 1.4 copy-done.72
  358.4 1.2 copy-done.55
  359.6 1.0 copy-done.59
  360.6 30.1 %attention_backward.1 = (bf16[512,256]{1,0:T(8,128)(2,1)S(1)}, bf16[256,2048]{1,0:T(8,128)(2,1)S(1)}, bf16[256,2048]{1,0:T(8,128)(2,1)S(1)}, f32[64,512]{1,0:T(8,128)S(1)}, f32[8,128]{1,0:T(8,128)S(1)}) custom-call(s32[1]{0:T(128)} %bitcast.1.pos_ref, bf16[512,256]{1,0:T(8,128)(2,1)S(1)} %copy-done.17, bf16[256,512]{1,0:T(8,128)(2,1)S(1)} %get-tuple-element.177.qt_ref, ...), custom_call_target="tpu_custom_call" | custom-call | flops 5368709120 | bytes 5242880 | tf_op jit(solution)/shard_map/attention_backward/pallas_call | solution.py:974
  390.7 0.9 copy-done.61
  391.7 1.0 copy-done.63
  393.2 1.2 copy-done.62
  394.4 1.2 copy-done.64
  395.6 15.8 %call_11.1 = (bf16[256,512]{1,0:T(8,128)(2,1)S(1)}, bf16[256,512]{1,0:T(8,128)(2,1)S(1)}) custom-call(bf16[256,2048]{1,0:T(8,128)(2,1)S(1)} %copy-done.62, bf16[256,2048]{1,0:T(8,128)(2,1)S(1)} %copy-done.64), custom_call_target="tpu_custom_call" | custom-call | flops 20000000000 | bytes 30000000 | tf_op jit(solution)/shard_map/call_11/pallas_call | solution.py:635
  411.4 1.0 bitcast_convert_fusion.partial_ref
  412.6 2.2 fusion.11.refs_3_
  415.4 1.4 copy-done.41
  416.8 1.6 copy-done.71
  418.4 1.6 copy-done.73
  420.0 36.7 %call_7.1 = (f32[512,1024]{1,0:T(8,128)S(1)}, bf16[512,1024]{1,0:T(8,128)(2,1)S(1)}, f32[8,1024]{1,0:T(8,128)S(1)}, f32[3,128,256]{2,1,0:T(8,128)S(1)}, f32[256,128]{1,0:T(8,128)S(1)}, /*index=5*/f32[40,128]{1,0:T(8,128)S(1)}) custom-call(bf16[512,1024]{1,0:T(8,128)(2,1)S(1)} %bitcast_convert_fusion.partial_ref, f32[512,1024]{1,0:T(8,128)S(1)} %copy-done.71, ...), custom_call_target="tpu_custom_call" | custom-call | flops 60000002048 | bytes 100000000 | tf_op jit(solution)/shard_map/call_7/pallas_call | solution.py:540
  456.7 1.7 fusion.10
  458.4 2.7 convolution_convert_fusion.refs_4_
  461.2 2.3 convolution_convert_fusion.5.partial_ref
  463.5 2.8 convolution_convert_fusion.1.refs_3_
  466.5 1.6 copy-done.50
  468.1 1.2 copy-done.51
  469.3 1.6 copy-done.60
  470.9 1.6 copy-done.68
  472.5 36.2 %call_8.1 = (f32[512,1024]{1,0:T(8,128)S(1)}, bf16[512,1024]{1,0:T(8,128)(2,1)}, f32[8,1024]{1,0:T(8,128)S(1)}, f32[128,1024]{1,0:T(8,128)S(1)}, f32[1024,128]{1,0:T(8,128)S(1)}, /*index=5*/f32[136,128]{1,0:T(8,128)S(1)}) custom-call(bf16[512,1024]{1,0:T(8,128)(2,1)S(1)} %copy-done.51, bf16[512,1024]{1,0:T(8,128)(2,1)S(1)} %bitcast.211, ...), custom_call_target="tpu_custom_call" | custom-call | flops 60000002048 | bytes 100000000 | tf_op jit(solution)/shard_map/call_8/pallas_call | solution.py:540
  512.7 1.6 slice.553
  515.1 6.5 %call_14.1 = f32[8,128]{1,0:T(8,128)S(1)} custom-call(f32[8,128]{1,0:T(8,128)S(1)} %bitcast.218), custom_call_target="tpu_custom_call" | custom-call | flops 30000001024 | bytes 50000000 | tf_op jit(solution)/shard_map/call_14/pallas_call | solution.py:385
  521.6 1.4 reshape.178
  523.0 1.4 slice.692
  524.4 1.5 copy.74
  525.8 1.0 copy.99
  526.8 1.3 copy.100
  (385 shorter events, 27.8 us)
Async XLA Ops:
  2.3 25.4 %copy-start.150 = (f32[512]{0:T(512)}, f32[512]{0:T(512)S(1)}, u32[]{:S(2)}) copy-start(f32[512]{0:T(512)S(1)} %broadcast_multiply_fusion) | copy-start | bytes 6148
  4.0 23.7 %copy-start.154 = (f32[512]{0:T(512)}, f32[512]{0:T(512)S(1)}, u32[]{:S(2)}) copy-start(f32[512]{0:T(512)S(1)} %add_rsqrt_fusion) | copy-start | bytes 6148
  4.3 23.4 %copy-start = (bf16[1,512,1024]{2,1,0:T(8,128)(2,1)S(1)}, bf16[1,512,1024]{2,1,0:T(8,128)(2,1)}, u32[]{:S(2)}) copy-start(bf16[1,512,1024]{2,1,0:T(8,128)(2,1)} %param.18) | copy-start | bytes 3145732
  4.3 23.4 %copy-start.35 = (f32[1024]{0:T(1024)S(1)}, f32[1024]{0:T(1024)}, u32[]{:S(2)}) copy-start(f32[1024]{0:T(1024)} %param.19) | copy-start | bytes 12292
  67.8 34.2 %copy-start.6 = (bf16[256,1024]{1,0:T(8,128)(2,1)}, bf16[256,1024]{1,0:T(8,128)(2,1)S(1)}, u32[]{:S(2)}) copy-start(bf16[256,1024]{1,0:T(8,128)(2,1)S(1)} %get-tuple-element.75) | copy-start | bytes 1572868
  69.6 15.5 %copy-start.16 = (bf16[512,256]{1,0:T(8,128)(2,1)}, bf16[512,256]{1,0:T(8,128)(2,1)S(1)}, u32[]{:S(2)}) copy-start(bf16[512,256]{1,0:T(8,128)(2,1)S(1)} %copy.59.q_ref) | copy-start | bytes 786436
  70.0 15.1 %copy-start.21 = (bf16[512,128]{1,0:T(8,128)(2,1)}, bf16[512,128]{1,0:T(8,128)(2,1)S(1)}, u32[]{:S(2)}) copy-start(bf16[512,128]{1,0:T(8,128)(2,1)S(1)} %maximum_maximum_fusion.span_ref) | copy-start | bytes 393220
  85.1 16.1 %copy-start.52 = (bf16[2048,256]{1,0:T(8,128)(2,1)}, bf16[2048,256]{1,0:T(8,128)(2,1)S(1)}, u32[]{:S(2)}) copy-start(bf16[2048,256]{1,0:T(8,128)(2,1)S(1)} %get-tuple-element.72.k_ref) | copy-start | bytes 3145732
  85.1 16.1 %copy-start.54 = (bf16[2048,256]{1,0:T(8,128)(2,1)}, bf16[2048,256]{1,0:T(8,128)(2,1)S(1)}, u32[]{:S(2)}) copy-start(bf16[2048,256]{1,0:T(8,128)(2,1)S(1)} %get-tuple-element.73.v_ref) | copy-start | bytes 3145732
  85.1 18.0 %copy-start.31 = (f32[1024]{0:T(1024)S(1)}, f32[1024]{0:T(1024)}, u32[]{:S(2)}) copy-start(f32[1024]{0:T(1024)} %param.26) | copy-start | bytes 12292
  85.1 18.0 %copy-start.70 = (f32[512,1024]{1,0:T(8,128)S(1)}, f32[512,1024]{1,0:T(8,128)}, u32[]{:S(2)}) copy-start(f32[512,1024]{1,0:T(8,128)} %copy-done.69) | copy-start | bytes 6291460
  137.9 16.2 %copy-start.48 = (bf16[256,1024]{1,0:T(8,128)(2,1)}, bf16[256,1024]{1,0:T(8,128)(2,1)S(1)}, u32[]{:S(2)}) copy-start(bf16[256,1024]{1,0:T(8,128)(2,1)S(1)} %get-tuple-element.79) | copy-start | bytes 1572868
  137.9 16.9 %copy-start.74 = (f32[512,1024]{1,0:T(8,128)}, f32[512,1024]{1,0:T(8,128)S(1)}, u32[]{:S(2)}) copy-start(f32[512,1024]{1,0:T(8,128)S(1)} %get-tuple-element.80.refs_0_) | copy-start | bytes 6291460
  139.3 14.4 %copy-start.76 = (f32[512,256]{0,1:T(8,128)}, f32[512,256]{0,1:T(8,128)S(1)}, u32[]{:S(2)}) copy-start(f32[512,256]{0,1:T(8,128)S(1)} %fusion.144) | copy-start | bytes 1572868
  139.4 2.3 collective-permute-start
  141.0 12.7 %copy-start.97 = (f32[1,256]{1,0:T(1,128)}, f32[1,256]{1,0:T(1,128)S(1)}, u32[]{:S(2)}) copy-start(f32[1,256]{1,0:T(1,128)S(1)} %get-tuple-element.185) | copy-start | bytes 3076
  141.0 12.7 %copy-start.99 = (f32[1,256]{1,0:T(1,128)}, f32[1,256]{1,0:T(1,128)S(1)}, u32[]{:S(2)}) copy-start(f32[1,256]{1,0:T(1,128)S(1)} %get-tuple-element.186) | copy-start | bytes 3076
  141.0 12.7 %copy-start.101 = (f32[1,256]{1,0:T(1,128)}, f32[1,256]{1,0:T(1,128)S(1)}, u32[]{:S(2)}) copy-start(f32[1,256]{1,0:T(1,128)S(1)} %get-tuple-element.187) | copy-start | bytes 3076
  141.0 12.7 %copy-start.103 = (f32[1,256]{1,0:T(1,128)}, f32[1,256]{1,0:T(1,128)S(1)}, u32[]{:S(2)}) copy-start(f32[1,256]{1,0:T(1,128)S(1)} %get-tuple-element.188) | copy-start | bytes 3076
  141.0 12.7 %copy-start.105 = (f32[1,256]{1,0:T(1,128)}, f32[1,256]{1,0:T(1,128)S(1)}, u32[]{:S(2)}) copy-start(f32[1,256]{1,0:T(1,128)S(1)} %get-tuple-element.189) | copy-start | bytes 3076
  141.0 12.7 %copy-start.107 = (f32[1,256]{1,0:T(1,128)}, f32[1,256]{1,0:T(1,128)S(1)}, u32[]{:S(2)}) copy-start(f32[1,256]{1,0:T(1,128)S(1)} %get-tuple-element.190) | copy-start | bytes 3076
  141.0 12.7 %copy-start.109 = (f32[1,256]{1,0:T(1,128)}, f32[1,256]{1,0:T(1,128)S(1)}, u32[]{:S(2)}) copy-start(f32[1,256]{1,0:T(1,128)S(1)} %get-tuple-element.191) | copy-start | bytes 3076
  141.1 12.7 %copy-start.111 = (f32[1,256]{1,0:T(1,128)}, f32[1,256]{1,0:T(1,128)S(1)}, u32[]{:S(2)}) copy-start(f32[1,256]{1,0:T(1,128)S(1)} %get-tuple-element.192) | copy-start | bytes 3076
  141.1 12.7 %copy-start.113 = (f32[1,256]{1,0:T(1,128)}, f32[1,256]{1,0:T(1,128)S(1)}, u32[]{:S(2)}) copy-start(f32[1,256]{1,0:T(1,128)S(1)} %get-tuple-element.193) | copy-start | bytes 3076
  141.1 12.7 %copy-start.115 = (f32[1,256]{1,0:T(1,128)}, f32[1,256]{1,0:T(1,128)S(1)}, u32[]{:S(2)}) copy-start(f32[1,256]{1,0:T(1,128)S(1)} %get-tuple-element.194) | copy-start | bytes 3076
  141.1 12.7 %copy-start.117 = (f32[1,256]{1,0:T(1,128)}, f32[1,256]{1,0:T(1,128)S(1)}, u32[]{:S(2)}) copy-start(f32[1,256]{1,0:T(1,128)S(1)} %get-tuple-element.195) | copy-start | bytes 3076
  141.1 12.7 %copy-start.119 = (f32[1,256]{1,0:T(1,128)}, f32[1,256]{1,0:T(1,128)S(1)}, u32[]{:S(2)}) copy-start(f32[1,256]{1,0:T(1,128)S(1)} %get-tuple-element.196) | copy-start | bytes 3076
  141.1 12.7 %copy-start.121 = (f32[1,256]{1,0:T(1,128)}, f32[1,256]{1,0:T(1,128)S(1)}, u32[]{:S(2)}) copy-start(f32[1,256]{1,0:T(1,128)S(1)} %get-tuple-element.197) | copy-start | bytes 3076
  141.1 12.7 %copy-start.123 = (f32[1,256]{1,0:T(1,128)}, f32[1,256]{1,0:T(1,128)S(1)}, u32[]{:S(2)}) copy-start(f32[1,256]{1,0:T(1,128)S(1)} %get-tuple-element.198) | copy-start | bytes 3076
  154.1 38.6 %copy-start.148 = (f32[512]{0:T(512)}, f32[512]{0:T(512)S(1)}, u32[]{:S(2)}) copy-start(f32[512]{0:T(512)S(1)} %fusion.150) | copy-start | bytes 6148
  154.1 38.6 %copy-start.152 = (f32[512]{0:T(512)}, f32[512]{0:T(512)S(1)}, u32[]{:S(2)}) copy-start(f32[512]{0:T(512)S(1)} %multiply_bitcast_fusion.2) | copy-start | bytes 6148
  231.7 47.4 %copy-start.49 = (bf16[256,1024]{1,0:T(8,128)(2,1)S(1)}, bf16[256,1024]{1,0:T(8,128)(2,1)}, u32[]{:S(2)}) copy-start(bf16[256,1024]{1,0:T(8,128)(2,1)} %copy-done.48) | copy-start | bytes 1572868
  231.7 47.4 %copy-start.83 = (f32[512,256]{0,1:T(8,128)S(1)}, f32[512,256]{0,1:T(8,128)}, u32[]{:S(2)}) copy-start(f32[512,256]{0,1:T(8,128)} %copy-done.82) | copy-start | bytes 1572868
  231.7 47.4 %copy-start.149 = (f32[512]{0:T(512)S(1)}, f32[512]{0:T(512)}, u32[]{:S(2)}) copy-start(f32[512]{0:T(512)} %copy-done.148) | copy-start | bytes 6148
  231.7 47.4 %copy-start.153 = (f32[512]{0:T(512)S(1)}, f32[512]{0:T(512)}, u32[]{:S(2)}) copy-start(f32[512]{0:T(512)} %copy-done.152) | copy-start | bytes 6148
  231.7 47.4 %copy-start.157 = (f32[256]{0:T(256)S(1)}, f32[256]{0:T(256)}, u32[]{:S(2)}) copy-start(f32[256]{0:T(256)} %param.29) | copy-start | bytes 3076
  289.7 13.8 %copy-start.79 = (f32[2,512,256]{1,2,0:T(8,128)S(1)}, f32[2,512,256]{1,2,0:T(8,128)}, u32[]{:S(2)}) copy-start(f32[2,512,256]{1,2,0:T(8,128)} %copy-done.78) | copy-start | bytes 3145732
  289.7 13.8 %copy-start.98 = (f32[1,256]{1,0:T(1,128)S(1)}, f32[1,256]{1,0:T(1,128)}, u32[]{:S(2)}) copy-start(f32[1,256]{1,0:T(1,128)} %copy-done.97) | copy-start | bytes 3076
  289.7 13.8 %copy-start.100 = (f32[1,256]{1,0:T(1,128)S(1)}, f32[1,256]{1,0:T(1,128)}, u32[]{:S(2)}) copy-start(f32[1,256]{1,0:T(1,128)} %copy-done.99) | copy-start | bytes 3076
  289.7 13.8 %copy-start.102 = (f32[1,256]{1,0:T(1,128)S(1)}, f32[1,256]{1,0:T(1,128)}, u32[]{:S(2)}) copy-start(f32[1,256]{1,0:T(1,128)} %copy-done.101) | copy-start | bytes 3076
  289.7 13.8 %copy-start.104 = (f32[1,256]{1,0:T(1,128)S(1)}, f32[1,256]{1,0:T(1,128)}, u32[]{:S(2)}) copy-start(f32[1,256]{1,0:T(1,128)} %copy-done.103) | copy-start | bytes 3076
  289.7 13.8 %copy-start.106 = (f32[1,256]{1,0:T(1,128)S(1)}, f32[1,256]{1,0:T(1,128)}, u32[]{:S(2)}) copy-start(f32[1,256]{1,0:T(1,128)} %copy-done.105) | copy-start | bytes 3076
  289.7 13.8 %copy-start.108 = (f32[1,256]{1,0:T(1,128)S(1)}, f32[1,256]{1,0:T(1,128)}, u32[]{:S(2)}) copy-start(f32[1,256]{1,0:T(1,128)} %copy-done.107) | copy-start | bytes 3076
  289.8 13.8 %copy-start.110 = (f32[1,256]{1,0:T(1,128)S(1)}, f32[1,256]{1,0:T(1,128)}, u32[]{:S(2)}) copy-start(f32[1,256]{1,0:T(1,128)} %copy-done.109) | copy-start | bytes 3076
  289.8 13.8 %copy-start.112 = (f32[1,256]{1,0:T(1,128)S(1)}, f32[1,256]{1,0:T(1,128)}, u32[]{:S(2)}) copy-start(f32[1,256]{1,0:T(1,128)} %copy-done.111) | copy-start | bytes 3076
  289.8 13.8 %copy-start.114 = (f32[1,256]{1,0:T(1,128)S(1)}, f32[1,256]{1,0:T(1,128)}, u32[]{:S(2)}) copy-start(f32[1,256]{1,0:T(1,128)} %copy-done.113) | copy-start | bytes 3076
  289.8 13.8 %copy-start.116 = (f32[1,256]{1,0:T(1,128)S(1)}, f32[1,256]{1,0:T(1,128)}, u32[]{:S(2)}) copy-start(f32[1,256]{1,0:T(1,128)} %copy-done.115) | copy-start | bytes 3076
  289.8 13.8 %copy-start.118 = (f32[1,256]{1,0:T(1,128)S(1)}, f32[1,256]{1,0:T(1,128)}, u32[]{:S(2)}) copy-start(f32[1,256]{1,0:T(1,128)} %copy-done.117) | copy-start | bytes 3076
  289.8 13.8 %copy-start.120 = (f32[1,256]{1,0:T(1,128)S(1)}, f32[1,256]{1,0:T(1,128)}, u32[]{:S(2)}) copy-start(f32[1,256]{1,0:T(1,128)} %copy-done.119) | copy-start | bytes 3076
  289.8 13.8 %copy-start.122 = (f32[1,256]{1,0:T(1,128)S(1)}, f32[1,256]{1,0:T(1,128)}, u32[]{:S(2)}) copy-start(f32[1,256]{1,0:T(1,128)} %copy-done.121) | copy-start | bytes 3076
  289.8 13.8 %copy-start.124 = (f32[1,256]{1,0:T(1,128)S(1)}, f32[1,256]{1,0:T(1,128)}, u32[]{:S(2)}) copy-start(f32[1,256]{1,0:T(1,128)} %copy-done.123) | copy-start | bytes 3076
  289.8 13.8 %copy-start.126 = (f32[1,256]{1,0:T(1,128)S(1)}, f32[1,256]{1,0:T(1,128)}, u32[]{:S(2)}) copy-start(f32[1,256]{1,0:T(1,128)} %copy-done.125) | copy-start | bytes 3076
  289.8 13.8 %copy-start.128 = (f32[1,256]{1,0:T(1,128)S(1)}, f32[1,256]{1,0:T(1,128)}, u32[]{:S(2)}) copy-start(f32[1,256]{1,0:T(1,128)} %copy-done.127) | copy-start | bytes 3076
  289.9 13.8 %copy-start.130 = (f32[1,256]{1,0:T(1,128)S(1)}, f32[1,256]{1,0:T(1,128)}, u32[]{:S(2)}) copy-start(f32[1,256]{1,0:T(1,128)} %copy-done.129) | copy-start | bytes 3076
  289.9 13.8 %copy-start.132 = (f32[1,256]{1,0:T(1,128)S(1)}, f32[1,256]{1,0:T(1,128)}, u32[]{:S(2)}) copy-start(f32[1,256]{1,0:T(1,128)} %copy-done.131) | copy-start | bytes 3076
  289.9 13.8 %copy-start.134 = (f32[1,256]{1,0:T(1,128)S(1)}, f32[1,256]{1,0:T(1,128)}, u32[]{:S(2)}) copy-start(f32[1,256]{1,0:T(1,128)} %copy-done.133) | copy-start | bytes 3076
  289.9 13.8 %copy-start.136 = (f32[1,256]{1,0:T(1,128)S(1)}, f32[1,256]{1,0:T(1,128)}, u32[]{:S(2)}) copy-start(f32[1,256]{1,0:T(1,128)} %copy-done.135) | copy-start | bytes 3076
  290.6 12.9 %collective-permute-start.1 = (f32[30,256]{0,1:T(8,128)}, f32[30,256]{0,1:T(8,128)}, u32[]{:S(2)}, u32[]{:S(2)}) collective-permute-start(f32[30,256]{0,1:T(8,128)} %slice.630), channel_id=1, source_target_pairs={{4,0},{8,4},{12,8},{5,1},{9,5},{13,9},{6,2},{10,6},{14,10},{7,3},{... | collective-permute-start | bytes 92168 | tf_op jit(solution)/shard_map/ppermute | solution.py:22
  298.7 16.0 %copy-start.40 = (bf16[512,1024]{1,0:T(8,128)(2,1)S(1)}, bf16[512,1024]{1,0:T(8,128)(2,1)}, u32[]{:S(2)}) copy-start(bf16[512,1024]{1,0:T(8,128)(2,1)} %copy-done.39) | copy-start | bytes 3145732
  317.4 39.5 %copy-start.7 = (bf16[256,1024]{1,0:T(8,128)(2,1)S(1)}, bf16[256,1024]{1,0:T(8,128)(2,1)}, u32[]{:S(2)}) copy-start(bf16[256,1024]{1,0:T(8,128)(2,1)} %copy-done.6) | copy-start | bytes 1572868
  317.4 40.2 %copy-start.3 = (bf16[512,256]{1,0:T(8,128)(2,1)S(1)}, bf16[512,256]{1,0:T(8,128)(2,1)}, u32[]{:S(2)}) copy-start(bf16[512,256]{1,0:T(8,128)(2,1)} %copy-done.2) | copy-start | bytes 786436
  395.6 15.8 %copy-start.43 = (bf16[3,1024,256]{2,1,0:T(8,128)(2,1)S(1)}, bf16[3,1024,256]{2,1,0:T(8,128)(2,1)}, u32[]{:S(2)}) copy-start(bf16[3,1024,256]{2,1,0:T(8,128)(2,1)} %copy-done.42) | copy-start | bytes 4718596
  420.0 36.7 %copy-start.57 = (bf16[1024,1024]{1,0:T(8,128)(2,1)S(1)}, bf16[1024,1024]{1,0:T(8,128)(2,1)}, u32[]{:S(2)}) copy-start(bf16[1024,1024]{1,0:T(8,128)(2,1)} %copy-done.56) | copy-start | bytes 6291460
  420.0 36.7 %copy-start.160 = (f32[512,1024]{1,0:T(8,128)S(1)}, f32[512,1024]{1,0:T(8,128)}, u32[]{:S(2)}) copy-start(f32[512,1024]{1,0:T(8,128)} %copy-done.159) | copy-start | bytes 6291460
  (99 other events, 405.8 us)

commit v4 on v3

--- a/solution.py
+++ b/solution.py
@@ -403,7 +403,8 @@
     is_mid = at == mid
     rest = [{axis: (at + step) % 4} for step in range(1, 4)]
     size = partial_ref.shape[0] // CHUNKS
-    gap = (CHUNKS - LAG) // (len(steps) + 1)
+
+    gap = max((CHUNKS - LAG) // (len(steps) + 1), 1)
 
     def rows(chunk):
         return pl.ds(pl.multiple_of(chunk * size, size), size)
@@ -431,7 +432,7 @@
 
     def beside(chunk):
         for index, step in enumerate(steps):
-            pl.when(chunk == LAG + (index + 1) * gap)(step)
+            pl.when(chunk == LAG + gap * (1 + index))(step)
 
     @pl.when(is_mid)
     def _():
@@ -513,6 +514,8 @@
     rows, width = partial.shape
     chunk_shape = pltpu.VMEM((rows, width), jnp.bfloat16)
     vmem = pl.BlockSpec(memory_space=pltpu.VMEM)
+    far = [at for at, operand in enumerate(operands) if operand.shape[0] == rows]
+    kinds = [pl.BlockSpec(memory_space=pltpu.HBM) if at in far else vmem for at in range(len(operands))]
     task_outs = [out for task in tasks for out in task.outs()]
     grant = (30 if any(isinstance(task, Scatter) for task in tasks) else 22) << 20
     pieces = [piece for task in tasks for piece in task.scratch()]
@@ -526,12 +529,25 @@
         ins, task_ins = take(len(operands)), take(len(tasks))
         results, task_results = take(len(outs)), take(len(tasks))
         acc, from_end, from_mid, total, send_sem, recv_sem = take(6)
+        copies, fetch_sem = take(len(far)), take(1)[0]
+        fetches = [
+            pltpu.make_async_copy(ins[at], held, fetch_sem.at[index]) for index, (at, held) in enumerate(zip(far, copies))
+        ]
+        for fetched in fetches:
+            fetched.start()
+        ins = [copies[far.index(at)] if at in far else ref for at, ref in enumerate(ins)]
         begins, steps, lasts, others = [], [], [], []
         if tasks:
             others = list(near()[1])
             begins, steps, lasts = bind_all(tasks, task_ins, task_results, refs)
         start, finish = body(total, ins, results)
         start()
+
+        def arrive():
+            for fetched in fetches:
+                fetched.wait()
+
+        begins.append(arrive)
         line_sum(
             TENSOR, partial_ref, acc, from_end, from_mid, total, send_sem, recv_sem, finish, others,
             any(task.line for task in tasks), begins, steps, lasts,
@@ -540,10 +556,12 @@
     got = pl.pallas_call(
         kernel,
         out_shape=tuple(jax.ShapeDtypeStruct(shape, kind) for shape, kind in list(outs) + task_outs),
-        in_specs=[vmem] * (1 + len(operands) + len(tasks)),
+        in_specs=[vmem] + kinds + [vmem] * len(tasks),
         out_specs=(vmem,) * (len(outs) + len(tasks)),
         scratch_shapes=[chunk_shape] * 4
         + [pltpu.SemaphoreType.DMA((3, CHUNKS)), pltpu.SemaphoreType.DMA((3, CHUNKS))]
+        + [pltpu.VMEM(operands[at].shape, operands[at].dtype) for at in far]
+        + [pltpu.SemaphoreType.DMA((len(far),))]
         + pieces,
         compiler_params=pltpu.CompilerParams(collective_id=cid, has_side_effects=True, vmem_limit_bytes=grant),
         cost_estimate=pl.CostEstimate(flops=60_000_000_000, bytes_accessed=100_000_000, transcendentals=0),
@@ -630,12 +648,12 @@
     return deep, core, {CONTEXT: (1 - deep) * 2 + core}, {CONTEXT: deep * 2 + 1 - core}
 
 
-def context_call(kernel, cid, operands, outs, scratch, ready=20_000_000_000):
+def context_call(kernel, cid, operands, outs, scratch, ready=20_000_000_000, place=pltpu.VMEM):
     vmem = pl.BlockSpec(memory_space=pltpu.VMEM)
     return pl.pallas_call(
         kernel,
         out_shape=tuple(jax.ShapeDtypeStruct(shape, kind) for shape, kind in outs),
-        in_specs=[vmem] * len(operands),
+        in_specs=[pl.BlockSpec(memory_space=place)] * len(operands),
         out_specs=(vmem,) * len(outs),
         scratch_shapes=scratch,
         compiler_params=pltpu.CompilerParams(collective_id=cid, has_side_effects=True, vmem_limit_bytes=12 << 20),
@@ -689,7 +707,7 @@
     rows, width = first.shape
     part = width // 4
 
-    def kernel(first_ref, second_ref, first_out, second_out, from_core, pair, from_y, send, recv):
+    def kernel(first_ref, second_ref, first_out, second_out, from_core, pair, from_y, local, send, recv, local_sem):
         deep, core, to_y, to_core = context_places()
         greet([to_y, to_core])
 
@@ -710,15 +728,23 @@
             for j, at in enumerate((far, close)):
                 inner.append(copy(2 * i + j, block(source, at * 2 + 1 - core), from_core.at[2 * i + j], to_core))
             outer.append(copy(4 + i, pair.at[2 * i], from_y.at[i], to_y))
+        mine = [
+            pltpu.make_async_copy(block(source, at * 2 + core), local.at[2 * i + j], local_sem.at[2 * i + j])
+            for i, source in enumerate(sources)
+            for j, at in enumerate((far, close))
+        ]
         for at in (0, 2, 1, 3):
             inner[at].start()
+            mine[at].start()
         for i, source in enumerate(sources):
             inner[2 * i].wait_recv()
-            pair[2 * i] = (wide(block(source, far * 2 + core)) + wide(from_core.at[2 * i])).astype(jnp.bfloat16)
+            mine[2 * i].wait()
+            pair[2 * i] = (wide(local.at[2 * i]) + wide(from_core.at[2 * i])).astype(jnp.bfloat16)
             outer[i].start()
         for i, source in enumerate(sources):
             inner[2 * i + 1].wait_recv()
-            pair[2 * i + 1] = (wide(block(source, close * 2 + core)) + wide(from_core.at[2 * i + 1])).astype(jnp.bfloat16)
+            mine[2 * i + 1].wait()
+            pair[2 * i + 1] = (wide(local.at[2 * i + 1]) + wide(from_core.at[2 * i + 1])).astype(jnp.bfloat16)
         for i, target in enumerate(targets):
             outer[i].wait_recv()
             target[...] = (wide(pair.at[2 * i + 1]) + wide(from_y.at[i])).astype(target.dtype)
@@ -733,9 +759,12 @@
             pltpu.VMEM((4,) + piece, jnp.bfloat16),
             pltpu.VMEM((4,) + piece, jnp.bfloat16),
             pltpu.VMEM((2,) + piece, jnp.bfloat16),
+            pltpu.VMEM((4,) + piece, jnp.bfloat16),
             pltpu.SemaphoreType.DMA((6,)),
             pltpu.SemaphoreType.DMA((6,)),
+            pltpu.SemaphoreType.DMA((4,)),
         ],
+        place=pltpu.HBM,
     )
 
 
@@ -1038,6 +1067,92 @@
     return (partial_sum.astype(jnp.bfloat16), table_grad, grad_in, grad_out)
 
 
+TILE = 64
+
+
+def sliding(ext_ref, tile, lanes):
+    window = ext_ref[pl.ds(pl.multiple_of(tile * TILE, TILE), TILE + 32), lanes]
+    for low in range(8):
+        moved = window[low : low + TILE + 24]
+        for high in range(0, 31 - low, 8):
+            yield high + low, moved[high : high + TILE]
+
+
+def tile_loop(rows, width, body):
+    def step(tile, carry):
+        for at in range(0, width, 128):
+            body(tile, slice(at, at + 128))
+        return carry
+
+    lax.fori_loop(0, rows // TILE, step, 0)
+
+
+def extended(before, rows, after):
+    pad = -(before.shape[0] + after.shape[0]) % 32
+    return jnp.concatenate([before, rows, after, jnp.zeros((pad, rows.shape[1]), rows.dtype)], axis=0)
+
+
+def depth_forward(ext, depthwise):
+    rows, width = ext.shape[0] - 32, ext.shape[1]
+
+    def kernel(ext_ref, depth_ref, out_ref):
+        def body(tile, lanes):
+            total = None
+            for distance, part in sliding(ext_ref, tile, lanes):
+                term = depth_ref[distance : distance + 1, lanes] * part
+                total = term if total is None else total + term
+            out_ref[pl.ds(pl.multiple_of(tile * TILE, TILE), TILE), lanes] = total
+
+        tile_loop(rows, width, body)
+
+    vmem = pl.BlockSpec(memory_space=pltpu.VMEM)
+    return pl.pallas_call(
+        kernel,
+        out_shape=jax.ShapeDtypeStruct((rows, width), jnp.float32),
+        in_specs=[vmem] * 2,
+        out_specs=vmem,
+        compiler_params=pltpu.CompilerParams(vmem_limit_bytes=6 << 20),
+        cost_estimate=pl.CostEstimate(flops=1_000_000_000, bytes_accessed=2_000_000, transcendentals=0),
+    )(ext, depthwise)
+
+
+def depth_backward(grad_ext, ext, depthwise):
+    rows, width = ext.shape[0] - 32, ext.shape[1]
+    reach = depthwise.shape[0] - 1
+
+    def kernel(grad_ref, ext_ref, depth_ref, out_ref, depth_out, sums):
+        sums[...] = jnp.zeros_like(sums)
+
+        def body(tile, lanes):
+            here = pl.ds(pl.multiple_of(tile * TILE, TILE), TILE)
+            total = None
+            for distance, part in sliding(grad_ref, tile, lanes):
+                term = depth_ref[reach - distance : reach - distance + 1, lanes] * part
+                total = term if total is None else total + term
+            out_ref[here, lanes] = total
+            grad = grad_ref[here, lanes]
+            for distance, part in sliding(ext_ref, tile, lanes):
+                sums[distance, :, lanes] += gather_eight(grad * part)
+
+        tile_loop(rows, width, body)
+        for distance in range(reach + 1):
+            depth_out[distance : distance + 1] = jnp.sum(sums[distance], axis=0, keepdims=True)
+
+    vmem = pl.BlockSpec(memory_space=pltpu.VMEM)
+    return pl.pallas_call(
+        kernel,
+        out_shape=(
+            jax.ShapeDtypeStruct((rows, width), jnp.float32),
+            jax.ShapeDtypeStruct(depthwise.shape, jnp.float32),
+        ),
+        in_specs=[vmem] * 3,
+        out_specs=(vmem, vmem),
+        scratch_shapes=[pltpu.VMEM((reach + 1, 8, width), jnp.float32)],
+        compiler_params=pltpu.CompilerParams(vmem_limit_bytes=8 << 20),
+        cost_estimate=pl.CostEstimate(flops=2_000_000_000, bytes_accessed=4_000_000, transcendentals=0),
+    )(grad_ext, ext, depthwise)
+
+
 def channel_sums(cid, first, second):
     total = line_total(cid, jnp.concatenate([first, second]).reshape(-1, 128)).reshape(2, -1)
     return total[0], total[1]
@@ -1049,10 +1164,8 @@
     rows_here = gated.shape[0]
     reach_rows = depthwise.shape[0] - 1
     edge_rows = shifted_2(gated[rows_here - reach_rows :], CONTEXT, 1)
-    padded = jnp.concatenate([edge_rows, gated], axis=0)
-    mixed = depthwise[0] * padded[0:rows_here]
-    for offset in range(1, reach_rows + 1):
-        mixed = mixed + depthwise[offset] * padded[offset : offset + rows_here]
+    padded = extended(edge_rows, gated, gated[:0])
+    mixed = depth_forward(padded, depthwise)
     row_sums, row_squares = channel_sums(12, jnp.sum(mixed, axis=1), jnp.sum(mixed * mixed, axis=1))
     row_mean = row_sums / D
     inverse = lax.rsqrt(row_squares / D - row_mean * row_mean + epsilon)
@@ -1067,7 +1180,6 @@
 
 def conv_backward(weight_in, weight_out, depthwise, gain_middle, saved, branch_grad):
     normed, projected, padded, scaled, inverse, shaped, active = saved
-    rows_here = scaled.shape[0]
     reach_rows = depthwise.shape[0] - 1
     grad_out = dot_inner(active, branch_grad)
     unused, pullback = jax.vjp(jax.nn.silu, shaped)
@@ -1079,16 +1191,7 @@
         scaled_grad - first_sum[:, None] / D - scaled * (second_sum[:, None] / D)
     )
     next_rows = shifted_2(mixed_grad[:reach_rows], CONTEXT, -1)
-    padded_grad = jnp.concatenate([mixed_grad, next_rows], axis=0)
-    gated_grad = depthwise[reach_rows] * padded_grad[0:rows_here]
-    for offset in range(1, reach_rows + 1):
-        gated_grad = gated_grad + depthwise[reach_rows - offset] * padded_grad[offset : offset + rows_here]
-    depth_grad = jnp.stack(
-        [
-            jnp.sum(padded[offset : offset + rows_here] * mixed_grad, axis=0)
-            for offset in range(reach_rows + 1)
-        ]
-    )
+    gated_grad, depth_grad = depth_backward(extended(mixed_grad[:0], mixed_grad, next_rows), padded, depthwise)
     unused, pullback = jax.vjp(gate_unit, projected[0], projected[1])
     unit_grad, gate_grad = pullback(gated_grad)
     stacked = jnp.stack([unit_grad, gate_grad]).astype(jnp.bfloat16)
@@ -1137,11 +1240,11 @@
     def collect(name, gathered):
         held[name] = gathered if small_plane else fetch(*weights[name])
 
-    def spreading(grad_in, grad_out):
+    def spreading(*sums):
         if not small_plane:
             return (), ()
-        pair = (grad_in.astype(jnp.bfloat16), grad_out.astype(jnp.bfloat16))
-        return tuple(Scatter(wide, grad.shape) for wide, grad in zip((False, True), pair)), pair
+        sums = tuple(grad.astype(jnp.bfloat16) for grad in sums)
+        return tuple(Scatter(at % 2 == 1, grad.shape) for at, grad in enumerate(sums)), sums
 
     def with_small(rest, kind, value):
         if not small_plane:
@@ -1165,24 +1268,24 @@
     collect(SECOND, got)
     branch, second_saved = feed(normed, *held[SECOND])
     final_out, upstream, branch_grad, grad_final = turn_sum(4, branch, after_convolve, gain_final, cotangent[0])
-    branch, *pair = feed_back(*held[SECOND], second_saved, branch_grad)
-    (upstream, branch_grad, grad_gain_second), got = backward_sum(
-        5, branch, after_convolve, gain_second, upstream, 1.0, *spreading(*pair)
-    )
-    spread(SECOND, got, *pair)
-    branch, *pair, grad_middle, grad_depth = conv_backward(
+    branch, *second_pair = feed_back(*held[SECOND], second_saved, branch_grad)
+    (upstream, branch_grad, grad_gain_second), _ = backward_sum(
+        5, branch, after_convolve, gain_second, upstream, 1.0
+    )
+    branch, *convolve_pair, grad_middle, grad_depth = conv_backward(
         *held[CONVOLVE], depthwise, gain_middle, convolve_saved, branch_grad
     )
     (upstream, branch_grad, grad_gain_convolve), got = backward_sum(
-        6, branch, after_attend, gain_convolve, upstream, 1.0, *spreading(*pair)
-    )
-    spread(CONVOLVE, got, *pair)
+        6, branch, after_attend, gain_convolve, upstream, 1.0, *spreading(*second_pair)
+    )
+    spread(SECOND, got, *second_pair)
     branch, table_grad, *pair = attend_backward(*held[ATTEND], position, attend_saved, branch_grad)
     shared = jnp.pad(table_grad.reshape(-1), (0, -table_grad.size % 1024)).reshape(-1, 128)
     (upstream, branch_grad, grad_gain_attend), got = backward_sum(
-        7, branch, after_first, gain_attend, upstream, 0.5, *with_small(spreading(*pair), LineSum, shared)
-    )
-    spread(ATTEND, got[:2], *pair)
+        7, branch, after_first, gain_attend, upstream, 0.5, *with_small(spreading(*convolve_pair, *pair), LineSum, shared)
+    )
+    spread(CONVOLVE, got[:2], *convolve_pair)
+    spread(ATTEND, got[2:4], *pair)
     branch, *pair = feed_back(*held[FIRST], first_saved, branch_grad)
     gains = [
         jnp.sum(part, axis=0) for part in (grad_gain_attend, grad_gain_convolve, grad_gain_second, grad_final)
@@ -1191,7 +1294,7 @@
     sizes = [part.shape[0] for part in smalls]
     packed = jnp.concatenate(smalls).reshape(-1, 128)
     if small_plane:
-        packed = jnp.concatenate([packed, got[2]], axis=0)
+        packed = jnp.concatenate([packed, got[4]], axis=0)
     (upstream, branch_grad, grad_gain_first), got = backward_sum(
         8, branch, start_rows, gain_first, upstream, 1.0, *with_small(spreading(*pair), PlaneSum, packed)
     )

time: 544 us -> 527 us (0.969)
  other arithmetic: 33.3 us -> 7.28 us
  starting transfers between devices: 2.83 us -> 13.7 us
  Pallas kernels: 414 us -> 407 us
    pallas_call x8, Pallas kernels: 296 us -> 282 us  [sum_call(): pl.pallas_call(kernel, out_shape=tuple((jax.ShapeDtypeStruct(shape, kind)...]
    ppermute x2, starting transfers between devices: 2.83 us -> 13.7 us  [shifted_2(): lax.ppermute(value, axis, [(source, source + steps) for source in range(i...]
    another operation x2 -> x1, other arithmetic: 10.9 us -> 0.22 us  [conv_backward(): stacked = jnp.stack([unit_grad, gate_grad]).astype(jnp.bfloat16)]
    reduce_sum x4 -> x0, other arithmetic: 9.64 us -> none  [conv_backward(): jnp.sum(padded[offset:offset + rows_here] * mixed_grad, axis=0)]
    pallas_call x0 -> x2, Pallas kernels: none -> 6.61 us  [the longest x1 4 us: depth_backward(): pl.pallas_call(kernel, out_shape=(jax.ShapeDtypeStruct((rows, width), jnp...]
    reduce_sum x1, other arithmetic: 6.48 us -> 0.22 us  [conv_forward(): jnp.sum(mixed, axis=1)]
    unnamed x340 -> x240, local copies, waits for them, and re-layouts: 38.6 us -> 41.4 us
  transfers between devices with their start and end apart: 2 -> 2, of which waited for: 1 -> 1; matrix products, arithmetic and copies ran while one was open for 2% -> 0% of each run, Pallas kernels for 0% -> 0%
where the time goes in v4:
time: 527 us; the launch traced here: 517 us
  Pallas kernels  407 us (77%)
  local copies, waits for them, and re-layouts  51 us (10%)
  matrix products  35.3 us (7%)
  starting transfers between devices  13.7 us (3%)
  other arithmetic  7.28 us (1%)
    pallas_call x8, Pallas kernels, sum_call(): pl.pallas_call(kernel, out_shape=tuple((jax.ShapeDtypeStruct(shape, kind)...  282 us
    pallas_call x4, Pallas kernels, context_call(): pl.pallas_call(kernel, out_shape=tuple((jax.ShapeDtypeStruct(shape, kind)...  41.9 us
    unnamed x240, local copies, waits for them, and re-layouts  41.4 us
    pallas_call x2, Pallas kernels, plane_call(): pl.pallas_call(kernel, out_shape=tuple((jax.ShapeDtypeStruct(shape, kind)...  30.4 us
    pallas_call x1, Pallas kernels, attention_backward(): pl.pallas_call(backward_kernel, out_shape=(jax.ShapeDtypeStruct((rows, wi...  30.1 us
    pallas_call x1, Pallas kernels, attention_forward(): pl.pallas_call(forward_kernel, out_shape=(jax.ShapeDtypeStruct((rows, wid...  16 us
    ppermute x2, starting transfers between devices, shifted_2(): lax.ppermute(value, axis, [(source, source + steps) for source in range(i...  13.7 us
    dot_general x6, matrix products, dot_inner(): lax.dot_general(former, latter, (((0,), (0,)), ((), ())), preferred_eleme...  11.9 us
  transfers between devices with their start and end apart: 2, of which 1 were waited for; matrix products, arithmetic and copies ran while one was open for 0% of the time, Pallas kernels for 0%

profile of v4, /device:TPU:0, one launch (start us, length us, event | category | flops | bytes accessed | tf_op | source)
XLA Modules:
  0.0 517.3 jit_solution(15286460796622121074)
XLA Ops:
  0.7 1.6 convert_reduce_fusion
  2.3 1.6 fusion.2
  4.3 23.3 %call_9.1 = (bf16[1024,1024]{1,0:T(8,128)(2,1)S(1)}, bf16[1024,1024]{1,0:T(8,128)(2,1)S(1)}) custom-call(bf16[128,1024]{1,0:T(8,128)(2,1)S(1)} %convert_element_type.116.refs_0_, bf16[1024,128]{1,0:T(8,128)(2,1)S(1)} %convert_element_type.117.refs_1_), custom_call_target="tpu_custom_call" | custom-call | flops 30000001024 | bytes 50000000 | tf_op jit(solution)/shard_map/call_9/pallas_call | solution.py:385
  27.7 1.4 fusion.38
  29.6 1.4 convolution_convert_fusion.10.partial_ref
  31.0 35.6 %call_1.1 = (f32[512,1024]{1,0:T(8,128)S(1)}, bf16[512,1024]{1,0:T(8,128)(2,1)S(1)}, bf16[3,1024,256]{2,1,0:T(8,128)(2,1)S(1)}, bf16[256,1024]{1,0:T(8,128)(2,1)S(1)}) custom-call(bf16[512,1024]{1,0:T(8,128)(2,1)S(1)} %convolution_convert_fusion.10.partial_ref, bf16[512,1024]{1,0:T(8,128)(2,1)S(1)} %bitcast.148, f32[1,1024]{1,0:T(1,128)S(1)} %bitcast.164, ...), custom_call_target="tpu_custom_call" | custom-call | flops 60000002048 | bytes 100000000 | tf_op jit(solution)/shard_map/call_1/pallas_call | solution.py:556
  66.6 1.3 copy-done.78
  67.9 1.0 fusion.13
  70.1 14.9 %call_10.1 = (bf16[2048,256]{1,0:T(8,128)(2,1)S(1)}, bf16[2048,256]{1,0:T(8,128)(2,1)S(1)}) custom-call(bf16[512,256]{1,0:T(8,128)(2,1)S(1)} %copy.55.first_ref, bf16[512,256]{1,0:T(8,128)(2,1)S(1)} %copy.56.second_ref), custom_call_target="tpu_custom_call" | custom-call | flops 20000000000 | bytes 30000000 | tf_op jit(solution)/shard_map/call_10/pallas_call | solution.py:653
  85.1 16.0 %attention_forward.1 = (bf16[512,256]{1,0:T(8,128)(2,1)S(1)}, f32[512,256]{1,0:T(8,128)S(1)}) custom-call(s32[1]{0:T(128)} %bitcast.pos_ref, bf16[512,256]{1,0:T(8,128)(2,1)S(1)} %copy.58.q_ref, bf16[2048,256]{1,0:T(8,128)(2,1)S(1)} %get-tuple-element.74.k_ref, bf16[2048,256]{1,0:T(8,128)(2,1)S(1)} %get-tuple-element.75.v_ref, ...), custom_call_target="tpu_custom_call" | custom-call | flops 2147483648 | bytes 2621440 | tf_op jit(solution)/shard_map/attention_forward/pallas_call | solution.py:891
  102.3 35.0 %call_2.1 = (f32[512,1024]{1,0:T(8,128)S(1)}, bf16[512,1024]{1,0:T(8,128)(2,1)S(1)}, bf16[2,1024,256]{2,1,0:T(8,128)(2,1)S(1)}, bf16[256,1024]{1,0:T(8,128)(2,1)S(1)}) custom-call(bf16[512,1024]{1,0:T(8,128)(2,1)S(1)} %convolution_convert_fusion.9.partial_ref, f32[512,1024]{1,0:T(8,128)S(1)} %copy-done.79, f32[1,1024]{1,0:T(1,128)S(1)} %bitcast.162, ...), custom_call_target="tpu_custom_call" | custom-call | flops 60000002048 | bytes 100000000 | tf_op jit(solution)/shard_map/call_2/pallas_call | solution.py:556
  138.7 1.3 collective-permute-start
  141.0 2.6 shard_map.313
  143.9 5.5 %call_12.1 = f32[8,128]{1,0:T(8,128)S(1)} custom-call(f32[8,128]{1,0:T(8,128)S(1)} %pad_maximum_fusion.8.value_ref), custom_call_target="tpu_custom_call" | custom-call | flops 5000000000 | bytes 30000000 | tf_op jit(solution)/shard_map/call_12/pallas_call | solution.py:653
  150.1 37.2 %call_3.1 = (f32[512,1024]{1,0:T(8,128)S(1)}, bf16[512,1024]{1,0:T(8,128)(2,1)S(1)}, bf16[1024,1024]{1,0:T(8,128)(2,1)S(1)}, bf16[1024,1024]{1,0:T(8,128)(2,1)S(1)}) custom-call(bf16[512,1024]{1,0:T(8,128)(2,1)S(1)} %convolution_convert_fusion.8.partial_ref, f32[512,1024]{1,0:T(8,128)S(1)} %get-tuple-element.82.refs_0_, f32[1,1024]{1,0:T(1,128)S(1)} %bitcast.160, ...), custom_call_target="tpu_custom_call" | custom-call | flops 60000002048 | bytes 100000000 | tf_op jit(solution)/shard_map/call_3/pallas_call | solution.py:556
  187.4 1.3 fusion.42
  188.6 1.3 convolution_convert_fusion.7.partial_ref
  190.0 30.9 %call_4.1 = (bf16[512,1024]{1,0:T(8,128)(2,1)S(1)}, f32[512,1024]{1,0:T(8,128)S(1)}, bf16[512,1024]{1,0:T(8,128)(2,1)S(1)}, f32[8,1024]{1,0:T(8,128)S(1)}) custom-call(bf16[512,1024]{1,0:T(8,128)(2,1)S(1)} %convolution_convert_fusion.7.partial_ref, f32[512,1024]{1,0:T(8,128)S(1)} %get-tuple-element.86.refs_0_, f32[1,1024]{1,0:T(1,128)S(1)} %bitcast.159, ...), custom_call_target="tpu_custom_call" | custom-call | flops 60000002048 | bytes 100000000 | tf_op jit(solution)/shard_map/call_4/pallas_call | solution.py:556
  220.9 1.7 fusion.7
  222.7 1.3 convolution_convert_fusion.6.partial_ref
  224.0 2.6 convolution_convert_fusion.3.refs_3_
  226.6 2.8 convolution_convert_fusion.2.refs_4_
  229.3 29.9 %call_5.1 = (f32[512,1024]{1,0:T(8,128)S(1)}, bf16[512,1024]{1,0:T(8,128)(2,1)S(1)}, f32[8,1024]{1,0:T(8,128)S(1)}) custom-call(bf16[512,1024]{1,0:T(8,128)(2,1)S(1)} %convolution_convert_fusion.6.partial_ref, f32[512,1024]{1,0:T(8,128)S(1)} %get-tuple-element.86.refs_0_, f32[1,1024]{1,0:T(1,128)S(1)} %bitcast.161, f32[512,1024]{1,0:T(8,128)S(1)} %get-tuple-element.89.refs_2_), custom_call_target="tpu_custom_call" | custom-call | flops 60000002048 | bytes 100000000 | tf_op jit(solution)/shard_map/call_5/pallas_call | solution.py:556
  259.3 1.2 multiply_reduce_fusion
  260.6 5.5 %call_13.1 = f32[8,128]{1,0:T(8,128)S(1)} custom-call(f32[8,128]{1,0:T(8,128)S(1)} %pad_maximum_fusion.9.value_ref), custom_call_target="tpu_custom_call" | custom-call | flops 5000000000 | bytes 30000000 | tf_op jit(solution)/shard_map/call_13/pallas_call | solution.py:653
  266.5 12.4 %collective-permute-start.1 = (f32[30,256]{1,0:T(8,128)S(1)}, f32[30,256]{1,0:T(8,128)S(1)}, u32[]{:S(2)}, u32[]{:S(2)}) collective-permute-start(f32[30,256]{1,0:T(8,128)S(1)} %slice.147), channel_id=1, source_target_pairs={{4,0},{8,4},{12,8},{5,1},{9,5},{13,9},{6,2},{10,6},{14,10},{7,3},{... | collective-permute-start | bytes 92168 | tf_op jit(solution)/shard_map/ppermute | solution.py:22
  281.0 4.0 shard_map.314
  286.3 1.7 fusion.12.refs_3_
  289.6 39.1 %call_6.1 = (f32[512,1024]{1,0:T(8,128)S(1)}, bf16[512,1024]{1,0:T(8,128)(2,1)S(1)}, f32[8,1024]{1,0:T(8,128)S(1)}, f32[128,1024]{1,0:T(8,128)S(1)}, f32[1024,128]{1,0:T(8,128)S(1)}) custom-call(bf16[512,1024]{1,0:T(8,128)(2,1)S(1)} %bitcast_convert_fusion.1.partial_ref, f32[512,1024]{1,0:T(8,128)S(1)} %copy-done.73, f32[1,1024]{1,0:T(1,128)S(1)} %bitcast.163, ...), custom_call_target="tpu_custom_call" | custom-call | flops 60000002048 | bytes 100000000 | tf_op jit(solution)/shard_map/call_6/pallas_call | solution.py:556
  328.8 1.4 copy-done.74
  331.8 1.2 copy-done.61
  333.0 1.2 copy-done.63
  334.2 30.1 %attention_backward.1 = (bf16[512,256]{1,0:T(8,128)(2,1)S(1)}, bf16[256,2048]{1,0:T(8,128)(2,1)S(1)}, bf16[256,2048]{1,0:T(8,128)(2,1)S(1)}, f32[64,512]{1,0:T(8,128)S(1)}, f32[8,128]{1,0:T(8,128)S(1)}) custom-call(s32[1]{0:T(128)} %bitcast.pos_ref, bf16[512,256]{1,0:T(8,128)(2,1)S(1)} %copy-done.21, bf16[256,512]{1,0:T(8,128)(2,1)S(1)} %get-tuple-element.148.qt_ref, ...), custom_call_target="tpu_custom_call" | custom-call | flops 5368709120 | bytes 5242880 | tf_op jit(solution)/shard_map/attention_backward/pallas_call | solution.py:1003
  364.3 1.0 copy-done.68
  366.8 1.2 copy-done.69
  368.0 1.2 copy-done.71
  369.2 15.9 %call_11.1 = (bf16[256,512]{1,0:T(8,128)(2,1)S(1)}, bf16[256,512]{1,0:T(8,128)(2,1)S(1)}) custom-call(bf16[256,2048]{1,0:T(8,128)(2,1)S(1)} %copy-done.69, bf16[256,2048]{1,0:T(8,128)(2,1)S(1)} %copy-done.71), custom_call_target="tpu_custom_call" | custom-call | flops 20000000000 | bytes 30000000 | tf_op jit(solution)/shard_map/call_11/pallas_call | solution.py:653
  385.2 2.0 bitcast_convert_fusion.partial_ref
  387.2 2.2 fusion.11.refs_5_
  389.9 1.2 copy-done.46
  391.2 1.4 copy-done.47
  392.6 1.2 copy-done.58
  393.8 1.6 copy-done.75
  395.4 1.6 copy-done.80
  397.0 37.6 %call_7.1 = (f32[512,1024]{1,0:T(8,128)S(1)}, bf16[512,1024]{1,0:T(8,128)(2,1)S(1)}, f32[8,1024]{1,0:T(8,128)S(1)}, f32[2,128,256]{2,1,0:T(8,128)S(1)}, f32[256,...) custom-call(bf16[512,1024]{1,0:T(8,128)(2,1)S(1)} %copy-done.58, ...), custom_call_target="tpu_custom_call" | custom-call | flops 60000002048 | bytes 100000000 | tf_op jit(solution)/shard_map/call_7/pallas_call | solution.py:556
  434.6 1.3 copy-done.81
  435.9 1.7 fusion.10
  437.7 2.7 convolution_convert_fusion.refs_4_
  440.4 2.3 convolution_convert_fusion.5.partial_ref
  442.8 2.7 convolution_convert_fusion.1.refs_3_
  445.7 1.6 copy-done.57
  447.3 1.2 copy-done.59
  448.5 1.6 copy-done.67
  450.1 1.6 copy-done.82
  451.7 36.4 %call_8.1 = (f32[512,1024]{1,0:T(8,128)S(1)}, bf16[512,1024]{1,0:T(8,128)(2,1)}, f32[8,1024]{1,0:T(8,128)S(1)}, f32[128,1024]{1,0:T(8,128)S(1)}, f32[1024,128]{1,0:T(8,128)S(1)}, /*index=5*/f32[136,128]{1,0:T(8,128)}) custom-call(bf16[512,1024]{1,0:T(8,128)(2,1)S(1)} %copy-done.59, bf16[512,1024]{1,0:T(8,128)(2,1)S(1)} %bitcast.149, ...), custom_call_target="tpu_custom_call" | custom-call | flops 60000002048 | bytes 100000000 | tf_op jit(solution)/shard_map/call_8/pallas_call | solution.py:556
  490.3 1.2 slice_bitcast_fusion.7
  491.6 1.3 slice_bitcast_fusion.3
  492.9 1.4 slice.132
  494.3 1.6 slice.128
  496.7 7.1 %call_14.1 = f32[8,128]{1,0:T(8,128)S(1)} custom-call(f32[8,128]{1,0:T(8,128)S(1)} %bitcast.156), custom_call_target="tpu_custom_call" | custom-call | flops 30000001024 | bytes 50000000 | tf_op jit(solution)/shard_map/call_14/pallas_call | solution.py:385
  503.8 1.4 reshape.178
  505.2 1.4 slice.151
  506.6 1.5 copy.72
  509.1 1.3 copy.98
  (284 shorter events, 25.7 us)
Async XLA Ops:
  0.7 3.3 copy-start.95
  0.7 3.4 copy-start.91
  0.7 3.5 copy-start.92
  0.7 3.5 copy-start.90
  0.7 3.5 copy-start.89
  0.7 3.5 copy-start.85
  0.7 3.6 copy-start.86
  2.3 25.4 %copy-start.100 = (f32[512]{0:T(512)}, f32[512]{0:T(512)S(1)}, u32[]{:S(2)}) copy-start(f32[512]{0:T(512)S(1)} %broadcast_multiply_fusion) | copy-start | bytes 6148
  4.0 23.7 %copy-start.104 = (f32[512]{0:T(512)}, f32[512]{0:T(512)S(1)}, u32[]{:S(2)}) copy-start(f32[512]{0:T(512)S(1)} %add_rsqrt_fusion) | copy-start | bytes 6148
  4.3 23.4 %copy-start = (bf16[1,512,1024]{2,1,0:T(8,128)(2,1)S(1)}, bf16[1,512,1024]{2,1,0:T(8,128)(2,1)}, u32[]{:S(2)}) copy-start(bf16[1,512,1024]{2,1,0:T(8,128)(2,1)} %param.18) | copy-start | bytes 3145732
  4.3 23.4 %copy-start.40 = (f32[1024]{0:T(1024)S(1)}, f32[1024]{0:T(1024)}, u32[]{:S(2)}) copy-start(f32[1024]{0:T(1024)} %param.19) | copy-start | bytes 12292
  67.9 33.2 %copy-start.10 = (bf16[256,1024]{1,0:T(8,128)(2,1)}, bf16[256,1024]{1,0:T(8,128)(2,1)S(1)}, u32[]{:S(2)}) copy-start(bf16[256,1024]{1,0:T(8,128)(2,1)S(1)} %get-tuple-element.77) | copy-start | bytes 1572868
  69.6 15.4 %copy-start.20 = (bf16[512,256]{1,0:T(8,128)(2,1)}, bf16[512,256]{1,0:T(8,128)(2,1)S(1)}, u32[]{:S(2)}) copy-start(bf16[512,256]{1,0:T(8,128)(2,1)S(1)} %copy.58.q_ref) | copy-start | bytes 786436
  70.1 14.9 %copy-start.24 = (bf16[512,128]{1,0:T(8,128)(2,1)}, bf16[512,128]{1,0:T(8,128)(2,1)S(1)}, u32[]{:S(2)}) copy-start(bf16[512,128]{1,0:T(8,128)(2,1)S(1)} %maximum_maximum_fusion.2.span_ref) | copy-start | bytes 393220
  85.0 16.1 %copy-start.60 = (bf16[2048,256]{1,0:T(8,128)(2,1)}, bf16[2048,256]{1,0:T(8,128)(2,1)S(1)}, u32[]{:S(2)}) copy-start(bf16[2048,256]{1,0:T(8,128)(2,1)S(1)} %get-tuple-element.74.k_ref) | copy-start | bytes 3145732
  85.0 16.1 %copy-start.62 = (bf16[2048,256]{1,0:T(8,128)(2,1)}, bf16[2048,256]{1,0:T(8,128)(2,1)S(1)}, u32[]{:S(2)}) copy-start(bf16[2048,256]{1,0:T(8,128)(2,1)S(1)} %get-tuple-element.75.v_ref) | copy-start | bytes 3145732
  85.0 17.2 %copy-start.36 = (f32[1024]{0:T(1024)S(1)}, f32[1024]{0:T(1024)}, u32[]{:S(2)}) copy-start(f32[1024]{0:T(1024)} %param.26) | copy-start | bytes 12292
  85.0 17.2 %copy-start.79 = (f32[512,1024]{1,0:T(8,128)S(1)}, f32[512,1024]{1,0:T(8,128)}, u32[]{:S(2)}) copy-start(f32[512,1024]{1,0:T(8,128)} %copy-done.78) | copy-start | bytes 6291460
  137.3 12.2 %copy-start.55 = (bf16[256,1024]{1,0:T(8,128)(2,1)}, bf16[256,1024]{1,0:T(8,128)(2,1)S(1)}, u32[]{:S(2)}) copy-start(bf16[256,1024]{1,0:T(8,128)(2,1)S(1)} %get-tuple-element.81) | copy-start | bytes 1572868
  137.3 12.8 %copy-start.72 = (f32[512,1024]{1,0:T(8,128)}, f32[512,1024]{1,0:T(8,128)S(1)}, u32[]{:S(2)}) copy-start(f32[512,1024]{1,0:T(8,128)S(1)} %get-tuple-element.82.refs_0_) | copy-start | bytes 6291460
  137.3 2.7 copy-start.87
  137.3 2.7 copy-start.88
  138.0 2.9 copy-start.83
  138.0 2.9 copy-start.32
  138.7 2.1 collective-permute-start
  140.2 3.4 copy-start.93
  141.0 2.9 copy-start.8
  143.6 5.9 %copy-start.2 = (f32[512,256]{1,0:T(8,128)}, f32[512,256]{1,0:T(8,128)S(1)}, u32[]{:S(2)}) copy-start(f32[512,256]{1,0:T(8,128)S(1)} %shard_map.313) | copy-start | bytes 1572868
  143.9 5.6 %copy-start.107 = (f32[256]{0:T(256)S(1)}, f32[256]{0:T(256)}, u32[]{:S(2)}) copy-start(f32[256]{0:T(256)} %param.29) | copy-start | bytes 3076
  149.4 37.9 %copy-start.98 = (f32[512]{0:T(512)}, f32[512]{0:T(512)S(1)}, u32[]{:S(2)}) copy-start(f32[512]{0:T(512)S(1)} %fusion.32) | copy-start | bytes 6148
  149.5 37.9 %copy-start.102 = (f32[512]{0:T(512)}, f32[512]{0:T(512)S(1)}, u32[]{:S(2)}) copy-start(f32[512]{0:T(512)S(1)} %multiply_bitcast_fusion.2) | copy-start | bytes 6148
  229.3 29.9 %copy-start.3 = (f32[512,256]{1,0:T(8,128)S(1)}, f32[512,256]{1,0:T(8,128)}, u32[]{:S(2)}) copy-start(f32[512,256]{1,0:T(8,128)} %copy-done.2) | copy-start | bytes 1572868
  229.3 30.0 %copy-start.56 = (bf16[256,1024]{1,0:T(8,128)(2,1)S(1)}, bf16[256,1024]{1,0:T(8,128)(2,1)}, u32[]{:S(2)}) copy-start(bf16[256,1024]{1,0:T(8,128)(2,1)} %copy-done.55) | copy-start | bytes 1572868
  229.3 30.0 %copy-start.99 = (f32[512]{0:T(512)S(1)}, f32[512]{0:T(512)}, u32[]{:S(2)}) copy-start(f32[512]{0:T(512)} %copy-done.98) | copy-start | bytes 6148
  229.3 30.0 %copy-start.103 = (f32[512]{0:T(512)S(1)}, f32[512]{0:T(512)}, u32[]{:S(2)}) copy-start(f32[512]{0:T(512)} %copy-done.102) | copy-start | bytes 6148
  229.3 30.0 %copy-start.108 = (f32[256]{0:T(256)S(1)}, f32[256]{0:T(256)}, u32[]{:S(2)}) copy-start(f32[256]{0:T(256)} %param.29) | copy-start | bytes 3076
  266.5 14.4 %copy-start.94 = (f32[544]{0:T(1024)S(1)}, f32[544]{0:T(1024)}, u32[]{:S(2)}) copy-start(f32[544]{0:T(1024)} %copy-done.93) | copy-start | bytes 6532
  266.5 14.5 %copy-start.9 = (f32[544,256]{1,0:T(8,128)S(1)}, f32[544,256]{1,0:T(8,128)}, u32[]{:S(2)}) copy-start(f32[544,256]{1,0:T(8,128)} %copy-done.8) | copy-start | bytes 1671172
  266.5 14.5 %copy-start.33 = (f32[31,256]{1,0:T(8,128)S(1)}, f32[31,256]{1,0:T(8,128)}, u32[]{:S(2)}) copy-start(f32[31,256]{1,0:T(8,128)} %depth_ref.3) | copy-start | bytes 95236
  266.5 14.3 %collective-permute-start.1 = (f32[30,256]{1,0:T(8,128)S(1)}, f32[30,256]{1,0:T(8,128)S(1)}, u32[]{:S(2)}, u32[]{:S(2)}) collective-permute-start(f32[30,256]{1,0:T(8,128)S(1)} %slice.147), channel_id=1, source_target_pairs={{4,0},{8,4},{12,8},{5,1},{9,5},{13,9},{6,2},{10,6},{14,10},{7,3},{... | collective-permute-start | bytes 92168 | tf_op jit(solution)/shard_map/ppermute | solution.py:22
  281.0 4.0 copy-start.84
  281.0 7.7 %copy-start.73 = (f32[512,1024]{1,0:T(8,128)S(1)}, f32[512,1024]{1,0:T(8,128)}, u32[]{:S(2)}) copy-start(f32[512,1024]{1,0:T(8,128)} %copy-done.72) | copy-start | bytes 6291460
  281.0 7.7 %copy-start.77 = (f32[512,1024]{1,0:T(8,128)S(1)}, f32[512,1024]{1,0:T(8,128)}, u32[]{:S(2)}) copy-start(f32[512,1024]{1,0:T(8,128)} %copy-done.76) | copy-start | bytes 6291460
  285.1 2.9 copy-start.43
  286.3 2.5 copy-start.66
  289.6 40.5 %copy-start.11 = (bf16[256,1024]{1,0:T(8,128)(2,1)S(1)}, bf16[256,1024]{1,0:T(8,128)(2,1)}, u32[]{:S(2)}) copy-start(bf16[256,1024]{1,0:T(8,128)(2,1)} %copy-done.10) | copy-start | bytes 1572868
  289.6 41.5 %copy-start.5 = (bf16[512,256]{1,0:T(8,128)(2,1)S(1)}, bf16[512,256]{1,0:T(8,128)(2,1)}, u32[]{:S(2)}) copy-start(bf16[512,256]{1,0:T(8,128)(2,1)} %copy-done.4) | copy-start | bytes 786436
  369.2 15.9 %copy-start.49 = (bf16[3,1024,256]{2,1,0:T(8,128)(2,1)S(1)}, bf16[3,1024,256]{2,1,0:T(8,128)(2,1)}, u32[]{:S(2)}) copy-start(bf16[3,1024,256]{2,1,0:T(8,128)(2,1)} %copy-done.48) | copy-start | bytes 4718596
  387.2 2.7 copy-start.39
  397.0 38.9 %copy-start.65 = (bf16[1024,1024]{1,0:T(8,128)(2,1)S(1)}, bf16[1024,1024]{1,0:T(8,128)(2,1)}, u32[]{:S(2)}) copy-start(bf16[1024,1024]{1,0:T(8,128)(2,1)} %copy-done.64) | copy-start | bytes 6291460
  397.0 38.9 %copy-start.110 = (f32[512,1024]{1,0:T(8,128)S(1)}, f32[512,1024]{1,0:T(8,128)}, u32[]{:S(2)}) copy-start(f32[512,1024]{1,0:T(8,128)} %copy-done.109) | copy-start | bytes 6291460
  437.7 2.7 copy-start.53
  440.4 2.3 copy-start.41
  440.4 2.3 copy-start.101
  442.7 2.9 copy-start.97
  442.7 2.9 copy-start.96
  442.8 2.9 copy-start.106
  496.7 11.4 %copy-start.7 = (bf16[512,1024]{1,0:T(8,128)(2,1)S(1)}, bf16[512,1024]{1,0:T(8,128)(2,1)}, u32[]{:S(2)}) copy-start(bf16[512,1024]{1,0:T(8,128)(2,1)} %copy-done.6) | copy-start | bytes 3145732
  509.1 2.7 copy-start.17
  510.4 2.9 copy-start.29
  510.4 3.6 copy-start.23
  510.4 4.3 copy-start.27
  510.4 5.0 copy-start.15
  511.8 4.4 copy-start.13
  (49 other events, 67.5 us)

commit v5 on v4

--- a/solution.py
+++ b/solution.py
@@ -205,6 +205,8 @@
         return [
             pltpu.VMEM((4,) + self.shape, jnp.bfloat16),
             pltpu.VMEM((4,) + self.shape, jnp.bfloat16),
+            pltpu.VMEM((4,) + self.shape, jnp.bfloat16),
+            pltpu.SemaphoreType.DMA((4,)),
             pltpu.VMEM((2,) + self.shape, jnp.bfloat16),
             pltpu.VMEM((2,) + half, jnp.bfloat16),
             pltpu.SemaphoreType.DMA((self.copies,)),
@@ -213,7 +215,7 @@
 
     def bind(self, ins, outs, scratch):
         (full_ref,), (out_ref,) = ins, outs
-        from_core, pair, whole, halves, send, recv = scratch
+        from_core, pair, local, local_sem, whole, halves, send, recv = scratch
         (x, y, core), (to_x, to_y, to_core) = near()
 
         def copy(index, source, target, device):
@@ -233,14 +235,18 @@
         ]
         wide = lambda ref: ref[...].astype(jnp.float32)
 
+        mine = [pltpu.make_async_copy(place(slot, core), local.at[slot], local_sem.at[slot]) for slot in range(4)]
+
         def begin():
             for slot in range(4):
                 moves[slot].start()
+                mine[slot].start()
 
         def second():
             for slot in range(4):
                 moves[slot].wait_recv()
-                pair[slot] = (wide(place(slot, core)) + wide(from_core.at[slot])).astype(jnp.bfloat16)
+                mine[slot].wait()
+                pair[slot] = (wide(local.at[slot]) + wide(from_core.at[slot])).astype(jnp.bfloat16)
             moves[4].start()
             moves[5].start()
 
@@ -515,9 +521,10 @@
     chunk_shape = pltpu.VMEM((rows, width), jnp.bfloat16)
     vmem = pl.BlockSpec(memory_space=pltpu.VMEM)
     far = [at for at, operand in enumerate(operands) if operand.shape[0] == rows]
-    kinds = [pl.BlockSpec(memory_space=pltpu.HBM) if at in far else vmem for at in range(len(operands))]
+    hbm = pl.BlockSpec(memory_space=pltpu.HBM)
+    kinds = [hbm if at in far else vmem for at in range(len(operands))]
     task_outs = [out for task in tasks for out in task.outs()]
-    grant = (30 if any(isinstance(task, Scatter) for task in tasks) else 22) << 20
+    grant = (56 if any(isinstance(task, Scatter) for task in tasks) else 22) << 20
     pieces = [piece for task in tasks for piece in task.scratch()]
 
     def kernel(partial_ref, *refs):
@@ -556,7 +563,7 @@
     got = pl.pallas_call(
         kernel,
         out_shape=tuple(jax.ShapeDtypeStruct(shape, kind) for shape, kind in list(outs) + task_outs),
-        in_specs=[vmem] + kinds + [vmem] * len(tasks),
+        in_specs=[vmem] + kinds + [hbm if isinstance(task, Scatter) else vmem for task in tasks],
         out_specs=(vmem,) * (len(outs) + len(tasks)),
         scratch_shapes=[chunk_shape] * 4
         + [pltpu.SemaphoreType.DMA((3, CHUNKS)), pltpu.SemaphoreType.DMA((3, CHUNKS))]
@@ -1246,10 +1253,10 @@
         sums = tuple(grad.astype(jnp.bfloat16) for grad in sums)
         return tuple(Scatter(at % 2 == 1, grad.shape) for at, grad in enumerate(sums)), sums
 
-    def with_small(rest, kind, value):
+    def with_small(rest, kind, *values):
         if not small_plane:
             return rest
-        return rest[0] + (kind(value.shape),), rest[1] + (value,)
+        return rest[0] + tuple(kind(value.shape) for value in values), rest[1] + values
 
     def spread(name, scattered, grad_in, grad_out):
         grads[name] = scattered if small_plane else send_grads(grad_in, grad_out)
@@ -1280,9 +1287,8 @@
     )
     spread(SECOND, got, *second_pair)
     branch, table_grad, *pair = attend_backward(*held[ATTEND], position, attend_saved, branch_grad)
-    shared = jnp.pad(table_grad.reshape(-1), (0, -table_grad.size % 1024)).reshape(-1, 128)
     (upstream, branch_grad, grad_gain_attend), got = backward_sum(
-        7, branch, after_first, gain_attend, upstream, 0.5, *with_small(spreading(*convolve_pair, *pair), LineSum, shared)
+        7, branch, after_first, gain_attend, upstream, 0.5, *with_small(spreading(*convolve_pair, *pair), LineSum, table_grad)
     )
     spread(CONVOLVE, got[:2], *convolve_pair)
     spread(ATTEND, got[2:4], *pair)
@@ -1290,29 +1296,23 @@
     gains = [
         jnp.sum(part, axis=0) for part in (grad_gain_attend, grad_gain_convolve, grad_gain_second, grad_final)
     ]
-    smalls = [*gains, grad_middle, grad_depth.reshape(-1)]
-    sizes = [part.shape[0] for part in smalls]
-    packed = jnp.concatenate(smalls).reshape(-1, 128)
     if small_plane:
-        packed = jnp.concatenate([packed, got[4]], axis=0)
+        table_grad = got[4]
+    gains = jnp.concatenate([*gains, grad_middle, jnp.zeros((768,), jnp.float32)]).reshape(-1, 128)
+    smalls = (gains, grad_depth, table_grad)
     (upstream, branch_grad, grad_gain_first), got = backward_sum(
-        8, branch, start_rows, gain_first, upstream, 1.0, *with_small(spreading(*pair), PlaneSum, packed)
+        8, branch, start_rows, gain_first, upstream, 1.0, *with_small(spreading(*pair), PlaneSum, *smalls)
     )
     spread(FIRST, got[:2], *pair)
     grad_gain_first = jnp.sum(grad_gain_first, axis=0)
     if small_plane:
-        packed = got[2].reshape(-1)
+        gains, grad_depth, table_grad = got[2:]
         (grad_gain_first,) = plane_call(14, (PlaneSum((8, 128)),), (grad_gain_first.reshape(8, 128),))
         grad_gain_first = grad_gain_first.reshape(-1)
-        table_grad = packed[sum(sizes) : sum(sizes) + table_grad.size].reshape(table_grad.shape)
     else:
         table_grad = lax.psum(table_grad, (CLIPS, CONTEXT, TENSOR))
-        packed, grad_gain_first = lax.psum((packed.reshape(-1), grad_gain_first), (CLIPS, CONTEXT))
-    smalls, at = [], 0
-    for size in sizes:
-        smalls.append(packed[at : at + size])
-        at += size
-    grad_depth = smalls[5].reshape(depthwise.shape)
+        gains, grad_depth, grad_gain_first = lax.psum((gains, grad_depth, grad_gain_first), (CLIPS, CONTEXT))
+    smalls = [gains[8 * at : 8 * at + 8].reshape(-1) for at in range(4)] + [gains[32:34].reshape(-1)]
     return (
         final_out[None],
         upstream[None],

time: 527 us -> 516 us (0.979)
  local copies, waits for them, and re-layouts: 51 us -> 26.2 us
  Pallas kernels: 407 us -> 415 us
  matrix products: 35.3 us -> 41.6 us
    unnamed x240 -> x205, local copies, waits for them, and re-layouts: 41.4 us -> 22.7 us
    pallas_call x8, Pallas kernels: 282 us -> 290 us  [sum_call(): pl.pallas_call(kernel, out_shape=tuple((jax.ShapeDtypeStruct(shape, kind)...]
    slice x5 -> x0, local copies, waits for them, and re-layouts: 6.96 us -> none  [the longest x3 3.93 us: local(): smalls.append(packed[at:at + size])]
  transfers between devices with their start and end apart: 2 -> 2, of which waited for: 1 -> 1; matrix products, arithmetic and copies ran while one was open for 0% -> 1% of each run, Pallas kernels for 0% -> 0%
where the time goes in v5:
time: 516 us; the launch traced here: 507 us
  Pallas kernels  415 us (80%)
  matrix products  41.6 us (8%)
  local copies, waits for them, and re-layouts  26.2 us (5%)
  starting transfers between devices  13.5 us (3%)
  other arithmetic  7.63 us (1%)
    pallas_call x8, Pallas kernels, sum_call(): pl.pallas_call(kernel, out_shape=tuple((jax.ShapeDtypeStruct(shape, kind)...  290 us
    pallas_call x4, Pallas kernels, context_call(): pl.pallas_call(kernel, out_shape=tuple((jax.ShapeDtypeStruct(shape, kind)...  41.8 us
    pallas_call x2, Pallas kernels, plane_call(): pl.pallas_call(kernel, out_shape=tuple((jax.ShapeDtypeStruct(shape, kind)...  30.3 us
    pallas_call x1, Pallas kernels, attention_backward(): pl.pallas_call(backward_kernel, out_shape=(jax.ShapeDtypeStruct((rows, wi...  30.1 us
    unnamed x205, local copies, waits for them, and re-layouts  22.7 us
    pallas_call x1, Pallas kernels, attention_forward(): pl.pallas_call(forward_kernel, out_shape=(jax.ShapeDtypeStruct((rows, wid...  16 us
    dot_general x6, matrix products, dot_inner(): lax.dot_general(former, latter, (((0,), (0,)), ((), ())), preferred_eleme...  14.8 us
    ppermute x2, starting transfers between devices, shifted_2(): lax.ppermute(value, axis, [(source, source + steps) for source in range(i...  13.5 us
  transfers between devices with their start and end apart: 2, of which 1 were waited for; matrix products, arithmetic and copies ran while one was open for 1% of the time, Pallas kernels for 0%

profile of v5, /device:TPU:0, one launch (start us, length us, event | category | flops | bytes accessed | tf_op | source)
XLA Modules:
  0.0 506.7 jit_solution(9068242959294484610)
XLA Ops:
  0.7 1.6 convert_reduce_fusion
  2.3 1.6 fusion.2
  4.3 23.3 %call_9.1 = (bf16[1024,1024]{1,0:T(8,128)(2,1)S(1)}, bf16[1024,1024]{1,0:T(8,128)(2,1)S(1)}) custom-call(bf16[128,1024]{1,0:T(8,128)(2,1)S(1)} %convert_element_type.114.refs_0_, bf16[1024,128]{1,0:T(8,128)(2,1)S(1)} %convert_element_type.115.refs_1_), custom_call_target="tpu_custom_call" | custom-call | flops 30000001024 | bytes 50000000 | tf_op jit(solution)/shard_map/call_9/pallas_call | solution.py:391
  27.7 1.3 fusion.38
  29.6 1.4 convolution_convert_fusion.10.partial_ref
  31.0 35.6 %call_1.1 = (f32[512,1024]{1,0:T(8,128)S(1)}, bf16[512,1024]{1,0:T(8,128)(2,1)S(1)}, bf16[3,1024,256]{2,1,0:T(8,128)(2,1)S(1)}, bf16[256,1024]{1,0:T(8,128)(2,1)S(1)}) custom-call(bf16[512,1024]{1,0:T(8,128)(2,1)S(1)} %convolution_convert_fusion.10.partial_ref, bf16[512,1024]{1,0:T(8,128)(2,1)S(1)} %bitcast.147, f32[1,1024]{1,0:T(1,128)S(1)} %bitcast.159, ...), custom_call_target="tpu_custom_call" | custom-call | flops 60000002048 | bytes 100000000 | tf_op jit(solution)/shard_map/call_1/pallas_call | solution.py:563
  66.6 1.3 copy-done.46
  68.0 1.0 fusion.13
  70.1 14.9 %call_10.1 = (bf16[2048,256]{1,0:T(8,128)(2,1)S(1)}, bf16[2048,256]{1,0:T(8,128)(2,1)S(1)}) custom-call(bf16[512,256]{1,0:T(8,128)(2,1)S(1)} %copy.37.first_ref, bf16[512,256]{1,0:T(8,128)(2,1)S(1)} %copy.38.second_ref), custom_call_target="tpu_custom_call" | custom-call | flops 20000000000 | bytes 30000000 | tf_op jit(solution)/shard_map/call_10/pallas_call | solution.py:660
  85.1 16.0 %attention_forward.1 = (bf16[512,256]{1,0:T(8,128)(2,1)S(1)}, f32[512,256]{1,0:T(8,128)S(1)}) custom-call(s32[1]{0:T(128)} %bitcast.pos_ref, bf16[512,256]{1,0:T(8,128)(2,1)S(1)} %copy.40.q_ref, bf16[2048,256]{1,0:T(8,128)(2,1)S(1)} %get-tuple-element.76.k_ref, bf16[2048,256]{1,0:T(8,128)(2,1)S(1)} %get-tuple-element.77.v_ref, ...), custom_call_target="tpu_custom_call" | custom-call | flops 2147483648 | bytes 2621440 | tf_op jit(solution)/shard_map/attention_forward/pallas_call | solution.py:898
  102.3 35.0 %call_2.1 = (f32[512,1024]{1,0:T(8,128)S(1)}, bf16[512,1024]{1,0:T(8,128)(2,1)S(1)}, bf16[2,1024,256]{2,1,0:T(8,128)(2,1)S(1)}, bf16[256,1024]{1,0:T(8,128)(2,1)S(1)}) custom-call(bf16[512,1024]{1,0:T(8,128)(2,1)S(1)} %convolution_convert_fusion.9.partial_ref, f32[512,1024]{1,0:T(8,128)S(1)} %copy-done.47, f32[1,1024]{1,0:T(1,128)S(1)} %bitcast.157, ...), custom_call_target="tpu_custom_call" | custom-call | flops 60000002048 | bytes 100000000 | tf_op jit(solution)/shard_map/call_2/pallas_call | solution.py:563
  137.3 0.7 convolution_bitcast_fusion
  138.7 1.3 collective-permute-start
  141.0 2.6 shard_map.313
  143.9 5.5 %call_12.1 = f32[8,128]{1,0:T(8,128)S(1)} custom-call(f32[8,128]{1,0:T(8,128)S(1)} %pad_maximum_fusion.7.value_ref), custom_call_target="tpu_custom_call" | custom-call | flops 5000000000 | bytes 30000000 | tf_op jit(solution)/shard_map/call_12/pallas_call | solution.py:660
  150.1 37.2 %call_3.1 = (f32[512,1024]{1,0:T(8,128)S(1)}, bf16[512,1024]{1,0:T(8,128)(2,1)S(1)}, bf16[1024,1024]{1,0:T(8,128)(2,1)S(1)}, bf16[1024,1024]{1,0:T(8,128)(2,1)S(1)}) custom-call(bf16[512,1024]{1,0:T(8,128)(2,1)S(1)} %convolution_convert_fusion.8.partial_ref, f32[512,1024]{1,0:T(8,128)S(1)} %get-tuple-element.84.refs_0_, f32[1,1024]{1,0:T(1,128)S(1)} %bitcast.154, ...), custom_call_target="tpu_custom_call" | custom-call | flops 60000002048 | bytes 100000000 | tf_op jit(solution)/shard_map/call_3/pallas_call | solution.py:563
  187.3 1.3 fusion.42
  188.6 1.3 convolution_convert_fusion.7.partial_ref
  190.0 30.9 %call_4.1 = (bf16[512,1024]{1,0:T(8,128)(2,1)S(1)}, f32[512,1024]{1,0:T(8,128)S(1)}, bf16[512,1024]{1,0:T(8,128)(2,1)S(1)}, f32[8,1024]{1,0:T(8,128)S(1)}) custom-call(bf16[512,1024]{1,0:T(8,128)(2,1)S(1)} %convolution_convert_fusion.7.partial_ref, f32[512,1024]{1,0:T(8,128)S(1)} %get-tuple-element.88.refs_0_, f32[1,1024]{1,0:T(1,128)S(1)} %bitcast.153, ...), custom_call_target="tpu_custom_call" | custom-call | flops 60000002048 | bytes 100000000 | tf_op jit(solution)/shard_map/call_4/pallas_call | solution.py:563
  220.9 1.7 fusion.7
  222.6 1.3 convolution_convert_fusion.6.partial_ref
  223.9 2.6 convolution_convert_fusion.3.refs_3_
  226.5 2.6 convolution_convert_fusion.2.refs_4_
  229.2 29.9 %call_5.1 = (f32[512,1024]{1,0:T(8,128)S(1)}, bf16[512,1024]{1,0:T(8,128)(2,1)S(1)}, f32[8,1024]{1,0:T(8,128)S(1)}) custom-call(bf16[512,1024]{1,0:T(8,128)(2,1)S(1)} %convolution_convert_fusion.6.partial_ref, f32[512,1024]{1,0:T(8,128)S(1)} %get-tuple-element.88.refs_0_, f32[1,1024]{1,0:T(1,128)S(1)} %bitcast.155, f32[512,1024]{1,0:T(8,128)S(1)} %get-tuple-element.91.refs_2_), custom_call_target="tpu_custom_call" | custom-call | flops 60000002048 | bytes 100000000 | tf_op jit(solution)/shard_map/call_5/pallas_call | solution.py:563
  259.1 1.2 multiply_reduce_fusion
  260.5 5.5 %call_13.1 = f32[8,128]{1,0:T(8,128)S(1)} custom-call(f32[8,128]{1,0:T(8,128)S(1)} %pad_maximum_fusion.8.value_ref), custom_call_target="tpu_custom_call" | custom-call | flops 5000000000 | bytes 30000000 | tf_op jit(solution)/shard_map/call_13/pallas_call | solution.py:660
  266.4 12.2 %collective-permute-start.1 = (f32[30,256]{1,0:T(8,128)S(1)}, f32[30,256]{1,0:T(8,128)S(1)}, u32[]{:S(2)}, u32[]{:S(2)}) collective-permute-start(f32[30,256]{1,0:T(8,128)S(1)} %slice.114), channel_id=1, source_target_pairs={{4,0},{8,4},{12,8},{5,1},{9,5},{13,9},{6,2},{10,6},{14,10},{7,3},{... | collective-permute-start | bytes 92168 | tf_op jit(solution)/shard_map/ppermute | solution.py:22
  278.6 1.5 convolution_convert_fusion.14.refs_4_
  281.5 4.0 shard_map.314
  285.8 1.0 copy-done.24
  286.8 1.7 fusion.12.refs_3_
  288.5 1.7 bitcast_convert_fusion.1.partial_ref
  290.2 42.3 %call_6.1 = (f32[512,1024]{1,0:T(8,128)}, bf16[512,1024]{1,0:T(8,128)(2,1)}, f32[8,1024]{1,0:T(8,128)}, f32[128,1024]{1,0:T(8,128)}, f32[1024,128]{1,0:T(8,128)}) custom-call(bf16[512,1024]{1,0:T(8,128)(2,1)} %bitcast_convert_fusion.1.partial_ref, f32[512,1024]{1,0:T(8,128)} %copy-done.44, f32[1,1024]{1,0:T(1,128)} %bitcast.156, f32[512,1024]{1,0:T(8,128)} %copy-done.45, ...), custom_call_target="tpu_custom_call" | custom-call | flops 60000002048 | bytes 100000000 | tf_op jit(solution)/shard_map/call_6/pallas_call | solution.py:563
  332.6 1.7 convolution_convert_fusion.15
  334.3 2.5 convolution_convert_fusion.13.refs_6_
  337.0 1.2 copy-done.34
  338.2 1.2 copy-done.36
  339.4 30.1 %attention_backward.1 = (bf16[512,256]{1,0:T(8,128)(2,1)S(1)}, bf16[256,2048]{1,0:T(8,128)(2,1)S(1)}, bf16[256,2048]{1,0:T(8,128)(2,1)S(1)}, f32[64,512]{1,0:T(8,128)S(1)}, f32[8,128]{1,0:T(8,128)S(1)}) custom-call(s32[1]{0:T(128)} %bitcast.pos_ref, bf16[512,256]{1,0:T(8,128)(2,1)S(1)} %copy-done.11, bf16[256,512]{1,0:T(8,128)(2,1)S(1)} %get-tuple-element.152.qt_ref, ...), custom_call_target="tpu_custom_call" | custom-call | flops 5368709120 | bytes 5242880 | tf_op jit(solution)/shard_map/attention_backward/pallas_call | solution.py:1010
  369.5 1.0 copy-done.39
  370.5 0.9 copy-done.41
  371.8 1.2 copy-done.40
  373.0 1.2 copy-done.42
  374.3 15.9 %call_11.1 = (bf16[256,512]{1,0:T(8,128)(2,1)S(1)}, bf16[256,512]{1,0:T(8,128)(2,1)S(1)}) custom-call(bf16[256,2048]{1,0:T(8,128)(2,1)S(1)} %copy-done.40, bf16[256,2048]{1,0:T(8,128)(2,1)S(1)} %copy-done.42), custom_call_target="tpu_custom_call" | custom-call | flops 20000000000 | bytes 30000000 | tf_op jit(solution)/shard_map/call_11/pallas_call | solution.py:660
  390.2 2.0 bitcast_convert_fusion.partial_ref
  392.2 2.2 fusion.11.refs_5_
  395.2 41.1 %call_7.1 = (f32[512,1024]{1,0:T(8,128)}, bf16[512,1024]{1,0:T(8,128)(2,1)}, f32[8,1024]{1,0:T(8,128)}, f32[2,128,256]{2,1,0:T(8,128)}, f32[256,128]{1,0:T(8,128...) custom-call(bf16[512,1024]{1,0:T(8,128)(2,1)} %bitcast_convert_fusion.partial_ref, ...), custom_call_target="tpu_custom_call" | custom-call | flops 60000002048 | bytes 100000000 | tf_op jit(solution)/shard_map/call_7/pallas_call | solution.py:563
  436.3 3.0 fusion.10
  439.3 2.7 convolution_convert_fusion.refs_4_
  442.1 2.3 convolution_convert_fusion.5.partial_ref
  444.4 2.9 convolution_convert_fusion.1.refs_3_
  448.0 37.8 %call_8.1 = (f32[512,1024]{1,0:T(8,128)}, bf16[512,1024]{1,0:T(8,128)(2,1)}, f32[8,1024]{1,0:T(8,128)}, f32[128,1024]{1,0:T(8,128)}, f32[1024,128]{1,0:T(8,128)}...) custom-call(bf16[512,1024]{1,0:T(8,128)(2,1)} %convolution_convert_fusion.5.partial_ref, ...), custom_call_target="tpu_custom_call" | custom-call | flops 60000002048 | bytes 100000000 | tf_op jit(solution)/shard_map/call_8/pallas_call | solution.py:563
  485.8 1.2 slice_bitcast_fusion.7
  487.0 1.3 slice_bitcast_fusion.3
  488.3 0.8 reduce_sum.145
  489.1 7.0 %call_14.1 = f32[8,128]{1,0:T(8,128)S(1)} custom-call(f32[8,128]{1,0:T(8,128)S(1)} %bitcast.150), custom_call_target="tpu_custom_call" | custom-call | flops 30000001024 | bytes 50000000 | tf_op jit(solution)/shard_map/call_14/pallas_call | solution.py:391
  496.1 0.7 copy.52
  496.8 1.0 copy.78
  497.8 1.3 copy.79
  499.8 0.8 copy.81
  500.6 0.8 copy.82
  501.3 0.7 copy.83
  502.8 0.7 copy.85
  504.7 0.8 copy.88
  505.5 0.8 copy.89
  (239 shorter events, 12.2 us)
Async XLA Ops:
  0.7 3.3 copy-start.73
  0.7 3.4 copy-start.63
  0.7 3.5 copy-start.64
  0.7 3.5 copy-start.61
  0.7 3.5 copy-start.59
  0.7 3.5 copy-start.51
  0.7 3.6 copy-start.52
  2.3 25.4 %copy-start.78 = (f32[512]{0:T(512)}, f32[512]{0:T(512)S(1)}, u32[]{:S(2)}) copy-start(f32[512]{0:T(512)S(1)} %broadcast_multiply_fusion) | copy-start | bytes 6148
  4.0 23.7 %copy-start.82 = (f32[512]{0:T(512)}, f32[512]{0:T(512)S(1)}, u32[]{:S(2)}) copy-start(f32[512]{0:T(512)S(1)} %add_rsqrt_fusion) | copy-start | bytes 6148
  4.3 23.4 %copy-start = (bf16[1,512,1024]{2,1,0:T(8,128)(2,1)S(1)}, bf16[1,512,1024]{2,1,0:T(8,128)(2,1)}, u32[]{:S(2)}) copy-start(bf16[1,512,1024]{2,1,0:T(8,128)(2,1)} %param.18) | copy-start | bytes 3145732
  4.3 23.4 %copy-start.88 = (f32[1024]{0:T(1024)S(1)}, f32[1024]{0:T(1024)}, u32[]{:S(2)}) copy-start(f32[1024]{0:T(1024)} %param.19) | copy-start | bytes 12292
  67.9 33.2 %copy-start.8 = (bf16[256,1024]{1,0:T(8,128)(2,1)}, bf16[256,1024]{1,0:T(8,128)(2,1)S(1)}, u32[]{:S(2)}) copy-start(bf16[256,1024]{1,0:T(8,128)(2,1)S(1)} %get-tuple-element.79) | copy-start | bytes 1572868
  69.6 15.4 %copy-start.10 = (bf16[512,256]{1,0:T(8,128)(2,1)}, bf16[512,256]{1,0:T(8,128)(2,1)S(1)}, u32[]{:S(2)}) copy-start(bf16[512,256]{1,0:T(8,128)(2,1)S(1)} %copy.40.q_ref) | copy-start | bytes 786436
  70.1 14.9 %copy-start.12 = (bf16[512,128]{1,0:T(8,128)(2,1)}, bf16[512,128]{1,0:T(8,128)(2,1)S(1)}, u32[]{:S(2)}) copy-start(bf16[512,128]{1,0:T(8,128)(2,1)S(1)} %maximum_maximum_fusion.2.span_ref) | copy-start | bytes 393220
  85.0 16.1 %copy-start.33 = (bf16[2048,256]{1,0:T(8,128)(2,1)}, bf16[2048,256]{1,0:T(8,128)(2,1)S(1)}, u32[]{:S(2)}) copy-start(bf16[2048,256]{1,0:T(8,128)(2,1)S(1)} %get-tuple-element.76.k_ref) | copy-start | bytes 3145732
  85.0 16.1 %copy-start.35 = (bf16[2048,256]{1,0:T(8,128)(2,1)}, bf16[2048,256]{1,0:T(8,128)(2,1)S(1)}, u32[]{:S(2)}) copy-start(bf16[2048,256]{1,0:T(8,128)(2,1)S(1)} %get-tuple-element.77.v_ref) | copy-start | bytes 3145732
  85.0 17.2 %copy-start.19 = (f32[1024]{0:T(1024)S(1)}, f32[1024]{0:T(1024)}, u32[]{:S(2)}) copy-start(f32[1024]{0:T(1024)} %param.26) | copy-start | bytes 12292
  85.1 17.2 %copy-start.47 = (f32[512,1024]{1,0:T(8,128)S(1)}, f32[512,1024]{1,0:T(8,128)}, u32[]{:S(2)}) copy-start(f32[512,1024]{1,0:T(8,128)} %copy-done.46) | copy-start | bytes 6291460
  137.3 12.2 %copy-start.31 = (bf16[256,1024]{1,0:T(8,128)(2,1)}, bf16[256,1024]{1,0:T(8,128)(2,1)S(1)}, u32[]{:S(2)}) copy-start(bf16[256,1024]{1,0:T(8,128)(2,1)S(1)} %get-tuple-element.83) | copy-start | bytes 1572868
  137.3 12.7 %copy-start.44 = (f32[512,1024]{1,0:T(8,128)}, f32[512,1024]{1,0:T(8,128)S(1)}, u32[]{:S(2)}) copy-start(f32[512,1024]{1,0:T(8,128)S(1)} %get-tuple-element.84.refs_0_) | copy-start | bytes 6291460
  137.3 2.7 copy-start.54
  138.0 2.9 copy-start.48
  138.0 2.9 copy-start.15
  138.7 2.1 collective-permute-start
  140.2 3.4 copy-start.68
  141.0 2.8 copy-start.6
  143.6 5.9 %copy-start.2 = (f32[512,256]{1,0:T(8,128)}, f32[512,256]{1,0:T(8,128)S(1)}, u32[]{:S(2)}) copy-start(f32[512,256]{1,0:T(8,128)S(1)} %shard_map.313) | copy-start | bytes 1572868
  143.9 5.6 %copy-start.85 = (f32[256]{0:T(256)S(1)}, f32[256]{0:T(256)}, u32[]{:S(2)}) copy-start(f32[256]{0:T(256)} %param.29) | copy-start | bytes 3076
  149.4 37.9 %copy-start.76 = (f32[512]{0:T(512)}, f32[512]{0:T(512)S(1)}, u32[]{:S(2)}) copy-start(f32[512]{0:T(512)S(1)} %fusion.32) | copy-start | bytes 6148
  149.4 37.9 %copy-start.80 = (f32[512]{0:T(512)}, f32[512]{0:T(512)S(1)}, u32[]{:S(2)}) copy-start(f32[512]{0:T(512)S(1)} %multiply_bitcast_fusion.2) | copy-start | bytes 6148
  229.2 29.9 %copy-start.3 = (f32[512,256]{1,0:T(8,128)S(1)}, f32[512,256]{1,0:T(8,128)}, u32[]{:S(2)}) copy-start(f32[512,256]{1,0:T(8,128)} %copy-done.2) | copy-start | bytes 1572868
  229.2 30.0 %copy-start.32 = (bf16[256,1024]{1,0:T(8,128)(2,1)S(1)}, bf16[256,1024]{1,0:T(8,128)(2,1)}, u32[]{:S(2)}) copy-start(bf16[256,1024]{1,0:T(8,128)(2,1)} %copy-done.31) | copy-start | bytes 1572868
  229.2 30.0 %copy-start.77 = (f32[512]{0:T(512)S(1)}, f32[512]{0:T(512)}, u32[]{:S(2)}) copy-start(f32[512]{0:T(512)} %copy-done.76) | copy-start | bytes 6148
  229.2 30.0 %copy-start.81 = (f32[512]{0:T(512)S(1)}, f32[512]{0:T(512)}, u32[]{:S(2)}) copy-start(f32[512]{0:T(512)} %copy-done.80) | copy-start | bytes 6148
  229.2 30.0 %copy-start.86 = (f32[256]{0:T(256)S(1)}, f32[256]{0:T(256)}, u32[]{:S(2)}) copy-start(f32[256]{0:T(256)} %param.29) | copy-start | bytes 3076
  266.4 14.9 %copy-start.69 = (f32[544]{0:T(1024)S(1)}, f32[544]{0:T(1024)}, u32[]{:S(2)}) copy-start(f32[544]{0:T(1024)} %copy-done.68) | copy-start | bytes 6532
  266.4 15.1 %copy-start.7 = (f32[544,256]{1,0:T(8,128)S(1)}, f32[544,256]{1,0:T(8,128)}, u32[]{:S(2)}) copy-start(f32[544,256]{1,0:T(8,128)} %copy-done.6) | copy-start | bytes 1671172
  266.4 15.1 %copy-start.16 = (f32[31,256]{1,0:T(8,128)S(1)}, f32[31,256]{1,0:T(8,128)}, u32[]{:S(2)}) copy-start(f32[31,256]{1,0:T(8,128)} %depth_ref.3) | copy-start | bytes 95236
  266.4 14.9 %collective-permute-start.1 = (f32[30,256]{1,0:T(8,128)S(1)}, f32[30,256]{1,0:T(8,128)S(1)}, u32[]{:S(2)}, u32[]{:S(2)}) collective-permute-start(f32[30,256]{1,0:T(8,128)S(1)} %slice.114), channel_id=1, source_target_pairs={{4,0},{8,4},{12,8},{5,1},{9,5},{13,9},{6,2},{10,6},{14,10},{7,3},{... | collective-permute-start | bytes 92168 | tf_op jit(solution)/shard_map/ppermute | solution.py:22
  281.5 4.0 copy-start.49
  285.5 3.0 copy-start.43
  285.5 3.0 copy-start.22
  290.2 42.3 %copy-start.9 = (bf16[256,1024]{1,0:T(8,128)(2,1)S(1)}, bf16[256,1024]{1,0:T(8,128)(2,1)}, u32[]{:S(2)}) copy-start(bf16[256,1024]{1,0:T(8,128)(2,1)} %copy-done.8) | copy-start | bytes 1572868
  290.2 44.1 %copy-start.5 = (bf16[512,256]{1,0:T(8,128)(2,1)S(1)}, bf16[512,256]{1,0:T(8,128)(2,1)}, u32[]{:S(2)}) copy-start(bf16[512,256]{1,0:T(8,128)(2,1)} %copy-done.4) | copy-start | bytes 786436
  332.5 4.4 copy-start.11
  332.5 4.4 copy-start.13
  374.3 15.9 %copy-start.26 = (bf16[3,1024,256]{2,1,0:T(8,128)(2,1)S(1)}, bf16[3,1024,256]{2,1,0:T(8,128)(2,1)}, u32[]{:S(2)}) copy-start(bf16[3,1024,256]{2,1,0:T(8,128)(2,1)} %copy-done.25) | copy-start | bytes 4718596
  395.2 41.1 %copy-start.38 = (bf16[1024,1024]{1,0:T(8,128)(2,1)S(1)}, bf16[1024,1024]{1,0:T(8,128)(2,1)}, u32[]{:S(2)}) copy-start(bf16[1024,1024]{1,0:T(8,128)(2,1)} %copy-done.37) | copy-start | bytes 6291460
  395.2 41.1 %copy-start.91 = (f32[512,1024]{1,0:T(8,128)S(1)}, f32[512,1024]{1,0:T(8,128)}, u32[]{:S(2)}) copy-start(f32[512,1024]{1,0:T(8,128)} %copy-done.90) | copy-start | bytes 6291460
  436.3 3.0 copy-start.92
  439.3 2.7 copy-start.30
  444.3 2.9 copy-start.70
  444.3 2.9 copy-start.71
  444.4 3.0 copy-start.75
  444.4 3.0 copy-start.74
  444.4 3.0 copy-start.84
  489.1 7.0 %copy-start.67 = (f32[73,64]{1,0:T(8,128)S(1)}, f32[73,64]{1,0:T(8,128)}, u32[]{:S(2)}) copy-start(f32[73,64]{1,0:T(8,128)} %get-tuple-element.134) | copy-start | bytes 56068
  497.8 2.7 copy-start.57
  499.1 3.0 copy-start.66
  499.1 3.6 copy-start.62
  499.1 4.3 copy-start.72
  499.1 4.9 copy-start.65
  499.1 5.6 %copy-start.56 = (f32[128,1024]{1,0:T(8,128)S(1)}, f32[128,1024]{1,0:T(8,128)}, u32[]{:S(2)}) copy-start(f32[128,1024]{1,0:T(8,128)} %get-tuple-element.199) | copy-start | bytes 1572868
  500.6 5.0 copy-start.55
  (31 other events, 46.9 us)
